TPU v7x, 512 devices: a whole 4x8x8 slice. The times are simulated.
512 devices in a mesh: prow: 64 (over z, x, core), pcol: 8 (over y).
Axes of the slice: x: 4, y: 8, z: 8, core: 2. Of those that a mesh axis runs over, the one named last changes fastest.
Arguments:
- rhs: bfloat16 [3, 512, 128, 384], P(None, ('prow', 'pcol')), may hold values from -6 to 6
- inverses: bfloat16 [3, 512, 128, 128], P(None, ('prow', 'pcol')), may hold values from -0.16 to 1.5, as said below
- tiles_first: bfloat16 [64, 64, 8, 128, 128], P('prow', None, 'pcol'), may hold values from -0.0625 to 0.0625
- rows_first: int32 [64, 64, 8], P('prow', None, 'pcol'), may hold values from 0 to 15
- tiles_second: bfloat16 [64, 64, 8, 128, 128], P('prow', None, 'pcol'), may hold values from -0.0625 to 0.0625
- rows_second: int32 [64, 64, 8], P('prow', None, 'pcol'), may hold values from 0 to 7
Outputs:
- solved: bfloat16 [3, 512, 128, 384], P(None, ('prow', 'pcol'))
Inputs may be any that keep to these rules, and one draw needn't show every extreme that they name: `inverses`: each block is lower triangular with its diagonal entries between 0.5 and 1.5.
All inputs are finite; a program needn't handle non-finite values.
Results may differ from a plain program's by a relative error of at most 0.0057.
Values may be sent and summed in bfloat16 or wider, within the bound.
No kernel may reach another device: no remote copies, remote signals or barrier semaphores. Data moves between devices by JAX's collectives and lax.ppermute only.
A program may use at most 128 MiB of HBM per device.

v0:
```python
import jax
import jax.numpy as jnp
from jax import lax
from jax.sharding import PartitionSpec as P


def solve_block(inverse, reduced):
    right = reduced.astype(jnp.bfloat16)
    return jnp.dot(inverse, right, preferred_element_type=jnp.float32).astype(jnp.bfloat16)


def spread_level(level_solved, tiles, rows, slots):
    product = jnp.einsum(
        "nab,nbr->nar",
        tiles,
        lax.all_gather(level_solved[None], "prow", axis=0, tiled=True),
        preferred_element_type=jnp.float32,
    )
    onehot = (rows[:, None] == jnp.arange(slots, dtype=jnp.int32)[None, :]).astype(jnp.float32)
    return jnp.einsum("ns,nar->sar", onehot, product, precision=lax.Precision.HIGHEST)


def reduce_rows(partial_value):
    return lax.psum_scatter(partial_value, "pcol", scatter_dimension=0, tiled=True)[0]


def local(rhs, inverses, tiles_first, rows_first, tiles_second, rows_second):
    columns = lax.axis_size("pcol")
    first_tiles = tiles_first[0, :, 0]
    first_rows = rows_first[0, :, 0]
    second_tiles = tiles_second[0, :, 0]
    second_rows = rows_second[0, :, 0]

    def run_level(level, state):
        right = rhs[level, 0].astype(jnp.float32)
        if level == 0:
            level_zero = solve_block(inverses[0, 0], right)
            update_first = spread_level(level_zero, first_tiles, first_rows, 2 * columns)
            return {
                "outs": [level_zero],
                "later": update_first[columns:],
                "near": update_first[:columns],
            }
        if level == 1:
            level_one = solve_block(inverses[1, 0], right - reduce_rows(state["near"]))
            update_second = spread_level(level_one, second_tiles, second_rows, columns)
            return {"outs": state["outs"] + [level_one], "later": state["later"] + update_second}
        level_two = solve_block(inverses[2, 0], right - reduce_rows(state["later"]))
        return {"outs": state["outs"] + [level_two]}

    state = None
    for level in range(3):
        state = run_level(level, state)
    levels_out = state["outs"]
    return jnp.stack(levels_out)[:, None]


def solution(mesh):
    in_specs = (
        P(None, ("prow", "pcol"), None, None),
        P(None, ("prow", "pcol"), None, None),
        P("prow", None, "pcol", None, None),
        P("prow", None, "pcol"),
        P("prow", None, "pcol", None, None),
        P("prow", None, "pcol"),
    )
    out_specs = P(None, ("prow", "pcol"), None, None)
    return jax.shard_map(local, mesh=mesh, in_specs=in_specs, out_specs=out_specs, check_vma=False)
```

profile of v0, /device:TPU:2, one launch (start us, length us, event | category | flops | bytes accessed | tf_op | source)
XLA Modules:
  0.0 343.0 jit_solution(1718180797089958903)
XLA Ops:
  6.5 0.0 copy-start
  6.5 0.0 all-gather.5.cloned.1.call-start
  6.5 1.9 convolution_convert_fusion.2
  8.4 0.0 all-gather.5.cloned.1.call-update
  8.4 0.0 reduce-scatter.3.cloned.1.call-start
  8.5 92.2 %all-gather.5.cloned.1.call-done = bf16[8192,384]{1,0:T(8,128)(2,1)} async-done(((bf16[128,384]{1,0:T(8,128)(2,1)}), bf16[8192,384]{1,0:T(8,128)(2,1)}) %all-gather.5.cloned.1.call-update) | async-done | bytes 6291472 | tf_op jit(solution)/shard_map/all_gather | solution.py:16
  100.7 0.0 copy-done
  100.7 9.2 %convolution_bitcast_fusion.1 = f32[64,128,384]{1,2,0:T(8,128)} fusion(bf16[64,128,384]{2,1,0:T(8,128)(2,1)} %bitcast.66, bf16[1,64,1,128,128]{4,3,2,1,0:T(8,128)(2,1)S(1)} %copy-done), kind=kOutput, calls=%fused_computation.1 | convolution fusion | flops 805306368 | bytes 20971520 | tf_op jit(solution)/shard_map/nab,nbr->nar/dot_general | solution.py:13
  109.9 12.8 %copy.18 = f32[64,128,384]{2,0,1:T(8,128)} copy(f32[64,128,384]{1,2,0:T(8,128)} %convolution_bitcast_fusion.1) | data formatting | bytes 25165824 | tf_op jit(solution)/shard_map/nab,nbr->nar/dot_general | solution.py:13
  122.7 0.0 copy-done.7
  122.7 7.2 %fusion.22 = f32[16,128,384]{2,0,1:T(8,128)S(1)} fusion(f32[64,128,384]{2,0,1:T(8,128)} %copy.18, s32[64]{0:T(128)S(1)} %bitcast.71), kind=kOutput, calls=%fused_computation.30 | convolution fusion | flops 603980800 | bytes 15728896 | tf_op jit(solution)/shard_map/ns,nar->sar/dot_general | solution.py:20
  129.9 0.0 copy-start.2
  130.0 1.7 copy-done.2
  131.7 0.1 slice.32
  131.8 1.4 copy.19
  133.2 0.0 reduce-scatter.3.cloned.1.call-update
  133.2 0.0 all-gather.7.cloned.1.call-start
  133.3 40.9 %reduce-scatter.3.cloned.1.call-done = f32[1,128,384]{2,1,0:T(8,128)} async-done(((f32[8,128,384]{2,1,0:T(8,128)}), f32[1,128,384]{2,1,0:T(8,128)}) %reduce-scatter.3.cloned.1.call-update) | async-done | bytes 196624 | tf_op jit(solution)/shard_map/reduce_scatter | solution.py:24
  174.2 0.0 copy-done.6
  174.2 1.7 convolution_convert_fusion.1
  175.9 0.0 all-gather.7.cloned.1.call-update
  176.0 0.0 reduce-scatter.5.cloned.1.call-start
  176.0 86.0 %all-gather.7.cloned.1.call-done = bf16[8192,384]{1,0:T(8,128)(2,1)} async-done(((bf16[128,384]{1,0:T(8,128)(2,1)}), bf16[8192,384]{1,0:T(8,128)(2,1)}) %all-gather.7.cloned.1.call-update) | async-done | bytes 6291472 | tf_op jit(solution)/shard_map/all_gather | solution.py:16
  262.0 9.8 %convolution_bitcast_fusion = f32[64,128,384]{1,2,0:T(8,128)} fusion(bf16[64,128,384]{2,1,0:T(8,128)(2,1)} %bitcast.67, bf16[1,64,1,128,128]{4,3,2,1,0:T(8,128)(2,1)} %param.10), kind=kOutput, calls=%fused_computation | convolution fusion | flops 805306368 | bytes 20971520 | tf_op jit(solution)/shard_map/nab,nbr->nar/dot_general | solution.py:13
  271.8 12.8 %copy.22 = f32[64,128,384]{2,0,1:T(8,128)} copy(f32[64,128,384]{1,2,0:T(8,128)} %convolution_bitcast_fusion) | data formatting | bytes 25165824 | tf_op jit(solution)/shard_map/nab,nbr->nar/dot_general | solution.py:13
  284.7 0.0 copy-start.1
  284.7 7.5 %slice_add_fusion = f32[8,128,384]{2,0,1:T(8,128)S(1)} fusion(f32[16,128,384]{2,0,1:T(8,128)} %copy-done.2, f32[64,128,384]{2,0,1:T(8,128)} %copy.22, s32[64]{0:T(128)S(1)} %bitcast.72), kind=kOutput, calls=%fused_computation.4 | convolution fusion | flops 302383616 | bytes 15728896 | tf_op jit(solution)/shard_map/ns,nar->sar/dot_general | solution.py:20
  292.2 1.4 copy.23
  293.6 0.0 reduce-scatter.5.cloned.1.call-update
  293.7 41.0 %reduce-scatter.5.cloned.1.call-done = f32[1,128,384]{2,1,0:T(8,128)} async-done(((f32[8,128,384]{2,1,0:T(8,128)}), f32[1,128,384]{2,1,0:T(8,128)}) %reduce-scatter.5.cloned.1.call-update) | async-done | bytes 196624 | tf_op jit(solution)/shard_map/reduce_scatter | solution.py:24
  334.6 1.1 fusion.2
  335.7 0.8 maximum_bitcast_fusion
  (11 shorter events, 0.0 us)
Async XLA Ops:
  6.5 94.2 %copy-start = (bf16[1,64,1,128,128]{4,3,2,1,0:T(8,128)(2,1)S(1)}, bf16[1,64,1,128,128]{4,3,2,1,0:T(8,128)(2,1)}, u32[]{:S(2)}) copy-start(bf16[1,64,1,128,128]{4,3,2,1,0:T(8,128)(2,1)} %param.8) | copy-start | bytes 6291460
  6.5 94.2 %all-gather.5.cloned.1.call-start = ((), (), s32[]{:S(2)}) async-start(), calls=%async_computation.4 | async-start | bytes 6389760 | tf_op jit(solution)/shard_map/all_gather | solution.py:16
  8.4 165.8 %reduce-scatter.3.cloned.1.call-start = ((), (), s32[]{:S(2)}) async-start(), calls=%async_computation.2 | async-start | bytes 1769472 | tf_op jit(solution)/shard_map/reduce_scatter | solution.py:24
  109.9 12.9 %copy-start.7 = (s32[1,64,1]{1,2,0:T(1,128)S(1)}, s32[1,64,1]{1,2,0:T(1,128)}, u32[]{:S(2)}) copy-start(s32[1,64,1]{1,2,0:T(1,128)} %param.9) | copy-start | bytes 772
  129.9 1.7 copy-start.2
  131.7 42.5 %copy-start.5 = (bf16[3,1,128,384]{3,2,1,0:T(8,128)(2,1)S(1)}, bf16[3,1,128,384]{3,2,1,0:T(8,128)(2,1)}, u32[]{:S(2)}) copy-start(bf16[3,1,128,384]{3,2,1,0:T(8,128)(2,1)} %param.6) | copy-start | bytes 884740
  131.7 42.5 %copy-start.6 = (bf16[3,1,128,128]{3,2,1,0:T(8,128)(2,1)S(1)}, bf16[3,1,128,128]{3,2,1,0:T(8,128)(2,1)}, u32[]{:S(2)}) copy-start(bf16[3,1,128,128]{3,2,1,0:T(8,128)(2,1)} %param.7) | copy-start | bytes 294916
  133.2 128.8 %all-gather.7.cloned.1.call-start = ((), (), s32[]{:S(2)}) async-start(), calls=%async_computation.5 | async-start | bytes 6389760 | tf_op jit(solution)/shard_map/all_gather | solution.py:16
  176.0 158.7 %reduce-scatter.5.cloned.1.call-start = ((), (), s32[]{:S(2)}) async-start(), calls=%async_computation.3 | async-start | bytes 1769472 | tf_op jit(solution)/shard_map/reduce_scatter | solution.py:24
  271.8 12.9 %copy-start.8 = (s32[1,64,1]{1,2,0:T(1,128)S(1)}, s32[1,64,1]{1,2,0:T(1,128)}, u32[]{:S(2)}) copy-start(s32[1,64,1]{1,2,0:T(1,128)} %param.11) | copy-start | bytes 772
  284.6 51.1 %copy-start.3 = (bf16[128,384]{1,0:T(8,128)(2,1)S(1)}, bf16[128,384]{1,0:T(8,128)(2,1)}, u32[]{:S(2)}) copy-start(bf16[128,384]{1,0:T(8,128)(2,1)} %convolution_convert_fusion.2) | copy-start | bytes 294916
  284.6 51.1 %copy-start.4 = (bf16[384,128]{0,1:T(8,128)(2,1)S(1)}, bf16[384,128]{0,1:T(8,128)(2,1)}, u32[]{:S(2)}) copy-start(bf16[384,128]{0,1:T(8,128)(2,1)} %convolution_convert_fusion.1) | copy-start | bytes 294916
  284.7 51.8 %copy-start.1 = (bf16[1,64,1,128,128]{4,3,2,1,0:T(8,128)(2,1)S(1)}, bf16[1,64,1,128,128]{4,3,2,1,0:T(8,128)(2,1)}, u32[]{:S(2)}) copy-start(bf16[1,64,1,128,128]{4,3,2,1,0:T(8,128)(2,1)} %param.8) | copy-start | bytes 6291460
Sparse Core Ops, SparseCore 0:
  10.7 89.9 all-gather.4
  133.4 40.7 reduce-scatter.2
  177.5 84.4 all-gather.6
  293.8 40.7 reduce-scatter.4
where the time goes:
time: 343 us
  waiting for transfers between devices  260 us (76%)
  matrix products  38.4 us (11%)
  local copies, waits for them, and re-layouts  30.4 us (9%)
  between operations  13.2 us (4%)
    all_gather x2, waiting for transfers between devices, spread_level(): lax.all_gather(level_solved[None], 'prow', axis=0, tiled=True)  178 us
    reduce_scatter x2, waiting for transfers between devices, reduce_rows(): lax.psum_scatter(partial_value, 'pcol', scatter_dimension=0, tiled=True)[0]  81.9 us
    dot_general x2, local copies, waits for them, and re-layouts, spread_level(): jnp.einsum('nab,nbr->nar', tiles, lax.all_gather(level_solved[None], 'pro...  25.7 us
    dot_general x2, matrix products, spread_level(): jnp.einsum('nab,nbr->nar', tiles, lax.all_gather(level_solved[None], 'pro...  18.9 us
    dot_general x2, matrix products, spread_level(): jnp.einsum('ns,nar->sar', onehot, product, precision=lax.Precision.HIGHEST)  14.7 us
  transfers between devices with their start and end apart: 4, of which 4 were waited for; matrix products, arithmetic and copies ran while one was open for 0% of the time, Pallas kernels for 0%

commit v1 on v0

v1 whole, which is shorter than its diff:
```python
import functools

import jax
import jax.numpy as jnp
from jax import lax
from jax.experimental import pallas as pl
from jax.experimental.pallas import tpu as pltpu
from jax.sharding import Mesh, PartitionSpec as P


NZ, NX, NC, NY = 8, 4, 2, 8
TILE, COLS = 128, 384
HALF = NZ // 2
CHIPS = NZ * NX
NEAR_SPOTS = ((0, 0), (0, 1), (HALF, 2), (HALF, 1), (0, 2))
FAR_SPOTS = ((0, 3), (HALF, 3))
SOLVE_FLOPS = 2 * TILE * TILE * COLS
PAIR_FLOPS = 2 * SOLVE_FLOPS


MIB = 1 << 20


def vmem():
    return pl.BlockSpec(memory_space=pltpu.VMEM)


def smem():
    return pl.BlockSpec(memory_space=pltpu.SMEM)


def call(body, out_shape, in_specs, out_specs, operands, flops, limit, aliases=None, grid_spec=None):
    specs = {} if grid_spec is not None else {"in_specs": in_specs, "out_specs": out_specs}
    if grid_spec is not None:
        specs = {"grid_spec": grid_spec}
    return pl.pallas_call(
        body,
        out_shape=out_shape,
        input_output_aliases=aliases or {},
        compiler_params=pltpu.CompilerParams(vmem_limit_bytes=limit * MIB),
        cost_estimate=pl.CostEstimate(flops=flops, bytes_accessed=4 * MIB, transcendentals=0),
        **specs,
    )(*operands)


def block_shape(dtype, *lead):
    return jax.ShapeDtypeStruct(lead + (TILE, COLS), dtype)


def level_specs(level):
    return [
        pl.BlockSpec((1, 1, TILE, TILE), lambda i: (level, 0, 0, 0)),
        pl.BlockSpec((1, 1, TILE, COLS), lambda i: (level, 0, 0, 0)),
    ]


def solve_zero_body(inverse, right, out):
    out[...] = jnp.dot(inverse[0, 0], right[0, 0], preferred_element_type=jnp.float32).astype(jnp.bfloat16)


def solve_zero(inverses, rhs):
    grid_spec = pl.GridSpec(grid=(1,), in_specs=level_specs(0), out_specs=pl.BlockSpec((TILE, COLS), lambda i: (0, 0)))
    return call(solve_zero_body, block_shape(jnp.bfloat16), None, None, (inverses, rhs), SOLVE_FLOPS, 8, grid_spec=grid_spec)


def solve_body(inverse, right, parts, out):
    total = parts[0].astype(jnp.float32)
    for q in range(1, NY):
        total = total + parts[q].astype(jnp.float32)
    reduced = (right[0, 0].astype(jnp.float32) - total).astype(jnp.bfloat16)
    out[...] = jnp.dot(inverse[0, 0], reduced, preferred_element_type=jnp.float32).astype(jnp.bfloat16)


def solve_next(level, inverses, rhs, parts):
    grid_spec = pl.GridSpec(
        grid=(1,),
        in_specs=level_specs(level) + [pl.BlockSpec((NY, TILE, COLS), lambda i: (0, 0, 0))],
        out_specs=pl.BlockSpec((TILE, COLS), lambda i: (0, 0)),
    )
    return call(solve_body, block_shape(jnp.bfloat16), None, None, (inverses, rhs, parts), SOLVE_FLOPS, 8, grid_spec=grid_spec)


def accumulate(where, slots, received, level, mine, other, pieces, spots, state):
    core = where[NX]
    for piece, (base, side) in zip(pieces, spots):

        def step(j, carry, piece=piece, base=base, side=side):
            chip = (base + j) * NX + where[side]
            pair = jnp.concatenate([mine[chip, core], other[level, chip]], axis=0)
            product = jnp.dot(pair, piece[j], preferred_element_type=jnp.float32)
            state[0, slots[level, chip * NC + core]] += product[:TILE]
            state[1, received[level, chip * NC + core]] += product[TILE:]
            return carry

        lax.fori_loop(0, piece.shape[0], step, 0, unroll=4)


def early_first_body(where, slots, received, mine, other, *refs):
    pieces, state = refs[:-1], refs[-1]
    state[...] = jnp.zeros_like(state)
    accumulate(where, slots, received, 0, mine, other, pieces, NEAR_SPOTS, state)


def early_second_body(where, slots, received, mine, other, later, *refs):
    pieces, state = refs[:-1], refs[-1]
    state[...] = later[:, NY:]
    accumulate(where, slots, received, 1, mine, other, pieces, NEAR_SPOTS, state)


def early(tables, mine, other, pieces, later=None):
    operands = tables + (mine, other) + (() if later is None else (later,)) + tuple(pieces)
    return call(
        early_first_body if later is None else early_second_body,
        block_shape(jnp.float32, 2, 2 * NY if later is None else NY),
        [smem()] * 3 + [vmem()] * (len(operands) - 3),
        vmem(),
        operands,
        24 * PAIR_FLOPS,
        28,
    )


def late_body(level, where, slots, received, mine, other, state, low, high, out, near_other):
    del state
    accumulate(where, slots, received, level, mine, other, (low, high), FAR_SPOTS, out)
    near_other[...] = out[1, :NY].astype(jnp.bfloat16)


def late(level, tables, mine, other, state, pieces):
    return call(
        functools.partial(late_body, level),
        [jax.ShapeDtypeStruct(state.shape, jnp.float32), block_shape(jnp.bfloat16, NY)],
        [smem()] * 3 + [vmem()] * 5,
        [vmem()] * 2,
        tables + (mine, other, state) + tuple(pieces),
        8 * PAIR_FLOPS,
        28,
        aliases={5: 0},
    )


def join_body(state, received, out):
    out[...] = (state[0] + received[...].astype(jnp.float32)).astype(jnp.bfloat16)


def join(state, received):
    grid_spec = pl.GridSpec(
        grid=(1,),
        in_specs=[
            pl.BlockSpec((1, NY, TILE, COLS), lambda i: (0, 0, 0, 0)),
            pl.BlockSpec((NY, TILE, COLS), lambda i: (0, 0, 0)),
        ],
        out_specs=pl.BlockSpec((NY, TILE, COLS), lambda i: (0, 0, 0)),
    )
    return call(join_body, block_shape(jnp.bfloat16, NY), None, None, (state, received), SOLVE_FLOPS, 12, grid_spec=grid_spec)


def ring(n, d):
    return [(i, (i + d) % n) for i in range(n)]


def gather_rows(block):
    return lax.all_gather(block[None], "z", axis=0, tiled=True)


def gather_columns(own):
    up = functools.partial(lax.ppermute, axis_name="x", perm=ring(NX, 1))
    down = functools.partial(lax.ppermute, axis_name="x", perm=ring(NX, -1))
    low, high = own[:HALF], own[HALF:]
    low_left = up(low)
    high_right = down(high)
    high_left = up(high)
    low_right = down(low)
    low_far = up(low_left)
    high_far = down(high_right)
    return [own, low_left, high_right, high_left, low_right], [low_far, high_far]


def places():
    x = lax.axis_index("x")
    core = lax.axis_index("core")
    return jnp.stack([x, (x + NX - 1) % NX, (x + 1) % NX, (x + 2) % NX, core]).astype(jnp.int32)


def swap(value):
    return lax.ppermute(value, "core", [(0, 1), (1, 0)])


def pick_body(other, first, second, after, out):
    del other, after
    out[0] = first[:, 0]
    out[1] = second[:, 0]


def pick(first, second, after):
    half = (CHIPS, 1, TILE, TILE)
    grid_spec = pltpu.PrefetchScalarGridSpec(
        num_scalar_prefetch=1,
        grid=(1,),
        in_specs=[
            pl.BlockSpec(half, lambda i, other: (0, other[0], 0, 0)),
            pl.BlockSpec(half, lambda i, other: (0, other[0], 0, 0)),
            pl.BlockSpec(memory_space=pl.ANY),
        ],
        out_specs=pl.BlockSpec((2, CHIPS, TILE, TILE), lambda i, other: (0, 0, 0, 0)),
    )
    shape = jax.ShapeDtypeStruct((2, CHIPS, TILE, TILE), jnp.bfloat16)
    other = (1 - lax.axis_index("core")).astype(jnp.int32)[None]
    return call(pick_body, shape, None, None, (other, first, second, after), SOLVE_FLOPS, 12, grid_spec=grid_spec)


def reduce_rows(state, near_other):
    received = swap(near_other)
    return lax.all_to_all(join(state, received), "y", 0, 0, tiled=True)


def local(rhs, inverses, tiles_first, rows_first, tiles_second, rows_second):
    where = places()
    mine_first = tiles_first.reshape(CHIPS, NC, TILE, TILE)
    mine_second = tiles_second.reshape(CHIPS, NC, TILE, TILE)

    level_zero = solve_zero(inverses, rhs)
    own = gather_rows(level_zero)
    near, far = gather_columns(own)
    slots = jnp.concatenate([rows_first.reshape(1, CHIPS * NC), rows_second.reshape(1, CHIPS * NC)])
    received = swap(slots)
    others = swap(pick(mine_first, mine_second, own))
    tables = (where, slots, received)
    state = early(tables, mine_first, others, near)
    state, near_other = late(0, tables, mine_first, others, state, far)
    parts = reduce_rows(state, near_other)

    level_one = solve_next(1, inverses, rhs, parts)
    near, far = gather_columns(gather_rows(level_one))
    state = early(tables, mine_second, others, near, state)
    state, near_other = late(1, tables, mine_second, others, state, far)
    level_two = solve_next(2, inverses, rhs, reduce_rows(state, near_other))
    return jnp.stack([level_zero, level_one, level_two])[:, None]


def solution(mesh):
    grid = Mesh(mesh.devices.reshape(NZ, NX, NC, NY), ("z", "x", "core", "y"))
    blocks = ("z", "x", "core", "y")
    rows = ("z", "x", "core")
    in_specs = (
        P(None, blocks, None, None),
        P(None, blocks, None, None),
        P(rows, None, "y", None, None),
        P(rows, None, "y"),
        P(rows, None, "y", None, None),
        P(rows, None, "y"),
    )
    out_specs = P(None, blocks, None, None)
    return jax.shard_map(local, mesh=grid, in_specs=in_specs, out_specs=out_specs, check_vma=False)
```

time: 343 us -> 203 us (0.59)
  the two profiles are of different devices: /device:TPU:2 before, /device:TPU:1 now
where the time goes in v1:
time: 203 us
  blocking collectives  104 us (51%)
  starting transfers between devices  57 us (28%)
  waiting for transfers between devices  21.2 us (10%)
  Pallas kernels  11.5 us (6%)
  local copies, waits for them, and re-layouts  7.77 us (4%)
    all_to_all x2, blocking collectives, reduce_rows(): return lax.all_to_all(join(state, received), 'y', 0, 0, tiled=True)  55.1 us
    all_gather x2, blocking collectives, gather_rows(): return lax.all_gather(block[None], 'z', axis=0, tiled=True)  48.9 us
    ppermute x4, starting transfers between devices, swap(): return lax.ppermute(value, 'core', [(0, 1), (1, 0)])  20.4 us
    pallas_call x10, Pallas kernels, call(): pl.pallas_call(body, out_shape=out_shape, input_output_aliases=aliases or...  11.5 us
    ppermute x2, starting transfers between devices, gather_columns(): high_far = down(high_right)  9.15 us
    ppermute x2, waiting for transfers between devices, gather_columns(): low_far = up(low_left)  9.09 us
    ppermute x2, starting transfers between devices, gather_columns(): high_right = down(high)  7.95 us
    unnamed x20, local copies, waits for them, and re-layouts  6.65 us
  transfers between devices with their start and end apart: 16, of which 7 were waited for; matrix products, arithmetic and copies ran while one was open for 1% of the time, Pallas kernels for 3%

profile of v1, /device:TPU:1, one launch (start us, length us, event | category | flops | bytes accessed | tf_op | source)
XLA Modules:
  0.0 202.5 jit_solution(2254065080296543959)
XLA Ops:
  2.0 28.1 %all-gather = bf16[1024,384]{1,0:T(8,128)(2,1)S(1)} all-gather(bf16[128,384]{1,0:T(8,128)(2,1)S(1)} %shard_map.64), channel_id=2, replica_groups=mesh['z'=8,'x'=4,'core'=2,'y'=8] {'z'}, dimensions={0}, use_global_device_ids=true | all-gather | bytes 884736 | tf_op jit(solution)/shard_map/all_gather | solution.py:163
  33.3 1.6 shard_map.65
  34.9 7.8 %collective-permute-start.1 = (bf16[2,32,128,128]{3,2,1,0:T(8,128)(2,1)}, bf16[2,32,128,128]{3,2,1,0:T(8,128)(2,1)S(1)}, u32[]{:S(2)}, u32[]{:S(2)}) collective-permute-start(bf16[2,32,128,128]{3,2,1,0:T(8,128)(2,1)} %shard_map.65), channel_id=1, source_target_pairs={{0,8},{8,0},{1,9},{9,1},{2,10},{10,2},{3,11},{11,3},{4,12},{12,4},... | collective-permute-start | bytes 6291464 | tf_op jit(solution)/shard_map/ppermute | solution.py:186
  43.7 3.1 %collective-permute-start.2 = (bf16[4,128,384]{2,1,0:T(8,128)(2,1)}, bf16[4,128,384]{2,1,0:T(8,128)(2,1)S(1)}, u32[]{:S(2)}, u32[]{:S(2)}) collective-permute-start(bf16[4,128,384]{2,1,0:T(8,128)(2,1)} %bitcast.12), channel_id=1, source_target_pairs={{0,16},{16,32},{32,48},{48,0},{1,17},{17,33},{33,49},{49,1},{2,18}... | collective-permute-start | bytes 1179656 | tf_op jit(solution)/shard_map/ppermute | solution.py:170
  46.8 3.4 %collective-permute-start.3 = (bf16[4,128,384]{2,1,0:T(8,128)(2,1)}, bf16[4,128,384]{2,1,0:T(8,128)(2,1)}, u32[]{:S(2)}, u32[]{:S(2)}) collective-permute-start(bf16[4,128,384]{2,1,0:T(8,128)(2,1)} %bitcast.13), channel_id=1, source_target_pairs={{0,48},{16,0},{32,16},{48,32},{1,49},{17,1},{33,17},{49,33},{2,50}... | collective-permute-start | bytes 1179656 | tf_op jit(solution)/shard_map/ppermute | solution.py:171
  50.2 2.5 %collective-permute-start = (s32[2,64]{1,0:T(2,128)S(1)}, s32[2,64]{1,0:T(2,128)S(1)}, u32[]{:S(2)}, u32[]{:S(2)}) collective-permute-start(s32[2,64]{1,0:T(2,128)S(1)} %pad_add_fusion.slots), channel_id=1, source_target_pairs={{0,8},{8,0},{1,9},{9,1},{2,10},{10,2},{3,11},{11,3},{4,12},{12,4},... | collective-permute-start | bytes 1544 | tf_op jit(solution)/shard_map/ppermute | solution.py:186
  52.7 3.2 %collective-permute-start.5 = (bf16[4,128,384]{2,1,0:T(8,128)(2,1)}, bf16[4,128,384]{2,1,0:T(8,128)(2,1)}, u32[]{:S(2)}, u32[]{:S(2)}) collective-permute-start(bf16[4,128,384]{2,1,0:T(8,128)(2,1)} %bitcast.12), channel_id=1, source_target_pairs={{0,48},{16,0},{32,16},{48,32},{1,49},{17,1},{33,17},{49,33},{2,50}... | collective-permute-start | bytes 1179656 | tf_op jit(solution)/shard_map/ppermute | solution.py:173
  55.9 2.1 %collective-permute-start.4 = (bf16[4,128,384]{2,1,0:T(8,128)(2,1)}, bf16[4,128,384]{2,1,0:T(8,128)(2,1)}, u32[]{:S(2)}, u32[]{:S(2)}) collective-permute-start(bf16[4,128,384]{2,1,0:T(8,128)(2,1)} %bitcast.13), channel_id=1, source_target_pairs={{0,16},{16,32},{32,48},{48,0},{1,17},{17,33},{33,49},{49,1},{2,18}... | collective-permute-start | bytes 1179656 | tf_op jit(solution)/shard_map/ppermute | solution.py:172
  58.0 1.9 collective-permute-start.6
  60.0 4.6 %collective-permute-start.7 = (bf16[4,128,384]{2,1,0:T(8,128)(2,1)}, bf16[4,128,384]{2,1,0:T(8,128)(2,1)}, u32[]{:S(2)}, u32[]{:S(2)}) collective-permute-start(bf16[4,128,384]{2,1,0:T(8,128)(2,1)} %collective-permute-done.3.refs_2_), channel_id=1, source_target_pairs={{0,48},{16,0},{32,16},{48,32},{1,49},{17,1},{33,17},{49,33},{2,50}... | collective-permute-start | bytes 1179656 | tf_op jit(solution)/shard_map/ppermute | solution.py:175
  64.7 3.1 %collective-permute-done.5.refs_4_ = bf16[4,128,384]{2,1,0:T(8,128)(2,1)} collective-permute-done((bf16[4,128,384]{2,1,0:T(8,128)(2,1)}, bf16[4,128,384]{2,1,0:T(8,128)(2,1)}, u32[]{:S(2)}, u32[]{:S(2)}) %collective-permute-start.5) | collective-permute-done | bytes 393248 | tf_op jit(solution)/shard_map/ppermute | solution.py:173
  67.8 1.9 collective-permute-done.4.refs_3_
  69.7 1.6 copy-done.3
  71.3 3.4 %shard_map.66.state = f32[2,16,128,384]{3,2,1,0:T(8,128)S(1)} custom-call(s32[5]{0:T(128)S(1)} %stack.36.where, s32[2,64]{1,0:T(2,128)S(1)} %pad_add_fusion.slots, s32[2,64]{1,0:T(2,128)S(1)} %collective-permute-done.received, bf16[32,2,128,128]{3,2,1,0:T(8,128)(2,1)S(1)} %bitcast.27, bf16[2,32,128,128]{3,2,1,0:T(8,128)(2,1)S(1)} %collective-permute-done.1.other, ...), custom_call_target="tpu_custom_call" | custom-call | flops 603979776 | bytes 4194304 | tf_op jit(solution)/shard_map/pallas_call | solution.py:36
  74.7 3.4 %collective-permute-done.6.low = bf16[4,128,384]{2,1,0:T(8,128)(2,1)} collective-permute-done((bf16[4,128,384]{2,1,0:T(8,128)(2,1)S(1)}, bf16[4,128,384]{2,1,0:T(8,128)(2,1)}, u32[]{:S(2)}, u32[]{:S(2)}) %collective-permute-start.6) | collective-permute-done | bytes 393248 | tf_op jit(solution)/shard_map/ppermute | solution.py:174
  78.1 1.8 shard_map.67
  79.9 3.1 %collective-permute-start.8 = (bf16[8,128,384]{2,1,0:T(8,128)(2,1)S(1)}, bf16[8,128,384]{2,1,0:T(8,128)(2,1)S(1)}, u32[]{:S(2)}, u32[]{:S(2)}) collective-permute-start(bf16[8,128,384]{2,1,0:T(8,128)(2,1)S(1)} %get-tuple-element.10), channel_id=1, source_target_pairs={{0,8},{8,0},{1,9},{9,1},{2,10},{10,2},{3,11},{11,3},{4,12},{12,4},... | collective-permute-start | bytes 2359304 | tf_op jit(solution)/shard_map/ppermute | solution.py:186
  83.0 1.9 collective-permute-done.8.received
  85.1 29.1 %all_to_all.10.parts = bf16[8,128,384]{2,1,0:T(8,128)(2,1)S(1)} all-to-all(bf16[8,128,384]{2,1,0:T(8,128)(2,1)S(1)} %shard_map.68), channel_id=1, replica_groups=mesh['z'=8,'x'=4,'core'=2,'y'=8] {'y'}, dimensions={0} | all-to-all | bytes 1572864 | tf_op jit(solution)/shard_map/all_to_all | solution.py:214
  114.4 20.8 %all-gather.1 = bf16[1024,384]{1,0:T(8,128)(2,1)S(1)} all-gather(bf16[128,384]{1,0:T(8,128)(2,1)S(1)} %shard_map.69), channel_id=3, replica_groups=mesh['z'=8,'x'=4,'core'=2,'y'=8] {'z'}, dimensions={0}, use_global_device_ids=true | all-gather | bytes 884736 | tf_op jit(solution)/shard_map/all_gather | solution.py:163
  135.4 1.9 collective-permute-start.9
  137.3 4.6 %collective-permute-start.10 = (bf16[4,128,384]{2,1,0:T(8,128)(2,1)S(1)}, bf16[4,128,384]{2,1,0:T(8,128)(2,1)S(1)}, u32[]{:S(2)}, u32[]{:S(2)}) collective-permute-start(bf16[4,128,384]{2,1,0:T(8,128)(2,1)S(1)} %bitcast.35), channel_id=1, source_target_pairs={{0,48},{16,0},{32,16},{48,32},{1,49},{17,1},{33,17},{49,33},{2,50}... | collective-permute-start | bytes 1179656 | tf_op jit(solution)/shard_map/ppermute | solution.py:171
  141.9 1.9 collective-permute-start.12
  143.8 3.4 %collective-permute-start.11 = (bf16[4,128,384]{2,1,0:T(8,128)(2,1)S(1)}, bf16[4,128,384]{2,1,0:T(8,128)(2,1)S(1)}, u32[]{:S(2)}, u32[]{:S(2)}) collective-permute-start(bf16[4,128,384]{2,1,0:T(8,128)(2,1)S(1)} %bitcast.36), channel_id=1, source_target_pairs={{0,16},{16,32},{32,48},{48,0},{1,17},{17,33},{33,49},{49,1},{2,18}... | collective-permute-start | bytes 1179656 | tf_op jit(solution)/shard_map/ppermute | solution.py:172
  147.2 1.9 collective-permute-start.13
  149.1 4.6 %collective-permute-start.14 = (bf16[4,128,384]{2,1,0:T(8,128)(2,1)S(1)}, bf16[4,128,384]{2,1,0:T(8,128)(2,1)S(1)}, u32[]{:S(2)}, u32[]{:S(2)}) collective-permute-start(bf16[4,128,384]{2,1,0:T(8,128)(2,1)S(1)} %collective-permute-done.10.refs_2_), channel_id=1, source_target_pairs={{0,48},{16,0},{32,16},{48,32},{1,49},{17,1},{33,17},{49,33},{2,50}... | collective-permute-start | bytes 1179656 | tf_op jit(solution)/shard_map/ppermute | solution.py:175
  153.7 3.3 %collective-permute-done.11.refs_3_ = bf16[4,128,384]{2,1,0:T(8,128)(2,1)S(1)} collective-permute-done((bf16[4,128,384]{2,1,0:T(8,128)(2,1)S(1)}, bf16[4,128,384]{2,1,0:T(8,128)(2,1)S(1)}, u32[]{:S(2)}, u32[]{:S(2)}) %collective-permute-start.11) | collective-permute-done | bytes 393248 | tf_op jit(solution)/shard_map/ppermute | solution.py:172
  157.0 2.5 %shard_map.70.state = f32[2,8,128,384]{3,2,1,0:T(8,128)S(1)} custom-call(s32[5]{0:T(128)S(1)} %stack.36.where, s32[2,64]{1,0:T(2,128)S(1)} %pad_add_fusion.slots, s32[2,64]{1,0:T(2,128)S(1)} %collective-permute-done.received, bf16[32,2,128,128]{3,2,1,0:T(8,128)(2,1)S(1)} %bitcast.24, bf16[2,32,128,128]{3,2,1,0:T(8,128)(2,1)S(1)} %collective-permute-done.1.other, ...), custom_call_target="tpu_custom_call" | custom-call | flops 603979776 | bytes 4194304 | tf_op jit(solution)/shard_map/pallas_call | solution.py:36
  159.5 5.6 %collective-permute-done.13.low = bf16[4,128,384]{2,1,0:T(8,128)(2,1)S(1)} collective-permute-done((bf16[4,128,384]{2,1,0:T(8,128)(2,1)S(1)}, bf16[4,128,384]{2,1,0:T(8,128)(2,1)S(1)}, u32[]{:S(2)}, u32[]{:S(2)}) %collective-permute-start.13) | collective-permute-done | bytes 393248 | tf_op jit(solution)/shard_map/ppermute | solution.py:174
  166.4 7.1 %collective-permute-start.15 = (bf16[8,128,384]{2,1,0:T(8,128)(2,1)S(1)}, bf16[8,128,384]{2,1,0:T(8,128)(2,1)S(1)}, u32[]{:S(2)}, u32[]{:S(2)}) collective-permute-start(bf16[8,128,384]{2,1,0:T(8,128)(2,1)S(1)} %get-tuple-element.12), channel_id=1, source_target_pairs={{0,8},{8,0},{1,9},{9,1},{2,10},{10,2},{3,11},{11,3},{4,12},{12,4},... | collective-permute-start | bytes 2359304 | tf_op jit(solution)/shard_map/ppermute | solution.py:186
  173.5 1.9 collective-permute-done.15.received
  175.5 26.0 %all_to_all.11.parts = bf16[8,128,384]{2,1,0:T(8,128)(2,1)S(1)} all-to-all(bf16[8,128,384]{2,1,0:T(8,128)(2,1)S(1)} %shard_map.72), channel_id=1, replica_groups=mesh['z'=8,'x'=4,'core'=2,'y'=8] {'y'}, dimensions={0} | all-to-all | bytes 1572864 | tf_op jit(solution)/shard_map/all_to_all | solution.py:214
  (39 shorter events, 9.2 us)
Async XLA Ops:
  0.0 1.0 copy-start.4
  1.0 0.9 copy-start.6
  30.1 1.6 copy-start
  31.7 1.6 copy-start.2
  33.3 16.9 %copy-start.8 = (s32[1,64,1]{1,2,0:T(1,128)S(1)}, s32[1,64,1]{1,2,0:T(1,128)}, u32[]{:S(2)}) copy-start(s32[1,64,1]{1,2,0:T(1,128)} %param.11) | copy-start | bytes 772
  33.3 16.9 %copy-start.9 = (s32[1,64,1]{1,2,0:T(1,128)S(1)}, s32[1,64,1]{1,2,0:T(1,128)}, u32[]{:S(2)}) copy-start(s32[1,64,1]{1,2,0:T(1,128)} %param.9) | copy-start | bytes 772
  34.9 34.8 %collective-permute-start.1 = (bf16[2,32,128,128]{3,2,1,0:T(8,128)(2,1)}, bf16[2,32,128,128]{3,2,1,0:T(8,128)(2,1)S(1)}, u32[]{:S(2)}, u32[]{:S(2)}) collective-permute-start(bf16[2,32,128,128]{3,2,1,0:T(8,128)(2,1)} %shard_map.65), channel_id=1, source_target_pairs={{0,8},{8,0},{1,9},{9,1},{2,10},{10,2},{3,11},{11,3},{4,12},{12,4},... | collective-permute-start | bytes 6291464 | tf_op jit(solution)/shard_map/ppermute | solution.py:186
  43.7 14.3 %collective-permute-start.2 = (bf16[4,128,384]{2,1,0:T(8,128)(2,1)}, bf16[4,128,384]{2,1,0:T(8,128)(2,1)S(1)}, u32[]{:S(2)}, u32[]{:S(2)}) collective-permute-start(bf16[4,128,384]{2,1,0:T(8,128)(2,1)} %bitcast.12), channel_id=1, source_target_pairs={{0,16},{16,32},{32,48},{48,0},{1,17},{17,33},{33,49},{49,1},{2,18}... | collective-permute-start | bytes 1179656 | tf_op jit(solution)/shard_map/ppermute | solution.py:170
  46.8 13.2 %collective-permute-start.3 = (bf16[4,128,384]{2,1,0:T(8,128)(2,1)}, bf16[4,128,384]{2,1,0:T(8,128)(2,1)}, u32[]{:S(2)}, u32[]{:S(2)}) collective-permute-start(bf16[4,128,384]{2,1,0:T(8,128)(2,1)} %bitcast.13), channel_id=1, source_target_pairs={{0,48},{16,0},{32,16},{48,32},{1,49},{17,1},{33,17},{49,33},{2,50}... | collective-permute-start | bytes 1179656 | tf_op jit(solution)/shard_map/ppermute | solution.py:171
  50.2 5.7 %collective-permute-start = (s32[2,64]{1,0:T(2,128)S(1)}, s32[2,64]{1,0:T(2,128)S(1)}, u32[]{:S(2)}, u32[]{:S(2)}) collective-permute-start(s32[2,64]{1,0:T(2,128)S(1)} %pad_add_fusion.slots), channel_id=1, source_target_pairs={{0,8},{8,0},{1,9},{9,1},{2,10},{10,2},{3,11},{11,3},{4,12},{12,4},... | collective-permute-start | bytes 1544 | tf_op jit(solution)/shard_map/ppermute | solution.py:186
  52.7 15.1 %collective-permute-start.5 = (bf16[4,128,384]{2,1,0:T(8,128)(2,1)}, bf16[4,128,384]{2,1,0:T(8,128)(2,1)}, u32[]{:S(2)}, u32[]{:S(2)}) collective-permute-start(bf16[4,128,384]{2,1,0:T(8,128)(2,1)} %bitcast.12), channel_id=1, source_target_pairs={{0,48},{16,0},{32,16},{48,32},{1,49},{17,1},{33,17},{49,33},{2,50}... | collective-permute-start | bytes 1179656 | tf_op jit(solution)/shard_map/ppermute | solution.py:173
  55.9 13.8 %collective-permute-start.4 = (bf16[4,128,384]{2,1,0:T(8,128)(2,1)}, bf16[4,128,384]{2,1,0:T(8,128)(2,1)}, u32[]{:S(2)}, u32[]{:S(2)}) collective-permute-start(bf16[4,128,384]{2,1,0:T(8,128)(2,1)} %bitcast.13), channel_id=1, source_target_pairs={{0,16},{16,32},{32,48},{48,0},{1,17},{17,33},{33,49},{49,1},{2,18}... | collective-permute-start | bytes 1179656 | tf_op jit(solution)/shard_map/ppermute | solution.py:172
  58.0 20.1 %collective-permute-start.6 = (bf16[4,128,384]{2,1,0:T(8,128)(2,1)S(1)}, bf16[4,128,384]{2,1,0:T(8,128)(2,1)}, u32[]{:S(2)}, u32[]{:S(2)}) collective-permute-start(bf16[4,128,384]{2,1,0:T(8,128)(2,1)S(1)} %collective-permute-done.2.refs_1_), channel_id=1, source_target_pairs={{0,16},{16,32},{32,48},{48,0},{1,17},{17,33},{33,49},{49,1},{2,18}... | collective-permute-start | bytes 1179656 | tf_op jit(solution)/shard_map/ppermute | solution.py:174
  60.0 18.2 %collective-permute-start.7 = (bf16[4,128,384]{2,1,0:T(8,128)(2,1)}, bf16[4,128,384]{2,1,0:T(8,128)(2,1)}, u32[]{:S(2)}, u32[]{:S(2)}) collective-permute-start(bf16[4,128,384]{2,1,0:T(8,128)(2,1)} %collective-permute-done.3.refs_2_), channel_id=1, source_target_pairs={{0,48},{16,0},{32,16},{48,32},{1,49},{17,1},{33,17},{49,33},{2,50}... | collective-permute-start | bytes 1179656 | tf_op jit(solution)/shard_map/ppermute | solution.py:175
  69.7 1.6 copy-start.3
  79.9 5.0 %collective-permute-start.8 = (bf16[8,128,384]{2,1,0:T(8,128)(2,1)S(1)}, bf16[8,128,384]{2,1,0:T(8,128)(2,1)S(1)}, u32[]{:S(2)}, u32[]{:S(2)}) collective-permute-start(bf16[8,128,384]{2,1,0:T(8,128)(2,1)S(1)} %get-tuple-element.10), channel_id=1, source_target_pairs={{0,8},{8,0},{1,9},{9,1},{2,10},{10,2},{3,11},{11,3},{4,12},{12,4},... | collective-permute-start | bytes 2359304 | tf_op jit(solution)/shard_map/ppermute | solution.py:186
  84.9 29.3 %copy-start.5 = (bf16[3,1,128,384]{3,2,1,0:T(8,128)(2,1)S(1)}, bf16[3,1,128,384]{3,2,1,0:T(8,128)(2,1)}, u32[]{:S(2)}) copy-start(bf16[3,1,128,384]{3,2,1,0:T(8,128)(2,1)} %right.5) | copy-start | bytes 884740
  84.9 29.3 %copy-start.7 = (bf16[3,1,128,128]{3,2,1,0:T(8,128)(2,1)S(1)}, bf16[3,1,128,128]{3,2,1,0:T(8,128)(2,1)}, u32[]{:S(2)}) copy-start(bf16[3,1,128,128]{3,2,1,0:T(8,128)(2,1)} %inverse.5) | copy-start | bytes 294916
  85.1 71.9 %copy-start.1 = (bf16[1,64,1,128,128]{4,3,2,1,0:T(8,128)(2,1)S(1)}, bf16[1,64,1,128,128]{4,3,2,1,0:T(8,128)(2,1)}, u32[]{:S(2)}) copy-start(bf16[1,64,1,128,128]{4,3,2,1,0:T(8,128)(2,1)} %param.10) | copy-start | bytes 6291460
  135.4 11.8 %collective-permute-start.9 = (bf16[4,128,384]{2,1,0:T(8,128)(2,1)S(1)}, bf16[4,128,384]{2,1,0:T(8,128)(2,1)S(1)}, u32[]{:S(2)}, u32[]{:S(2)}) collective-permute-start(bf16[4,128,384]{2,1,0:T(8,128)(2,1)S(1)} %bitcast.37), channel_id=1, source_target_pairs={{0,16},{16,32},{32,48},{48,0},{1,17},{17,33},{33,49},{49,1},{2,18}... | collective-permute-start | bytes 1179656 | tf_op jit(solution)/shard_map/ppermute | solution.py:170
  137.3 11.8 %collective-permute-start.10 = (bf16[4,128,384]{2,1,0:T(8,128)(2,1)S(1)}, bf16[4,128,384]{2,1,0:T(8,128)(2,1)S(1)}, u32[]{:S(2)}, u32[]{:S(2)}) collective-permute-start(bf16[4,128,384]{2,1,0:T(8,128)(2,1)S(1)} %bitcast.35), channel_id=1, source_target_pairs={{0,48},{16,0},{32,16},{48,32},{1,49},{17,1},{33,17},{49,33},{2,50}... | collective-permute-start | bytes 1179656 | tf_op jit(solution)/shard_map/ppermute | solution.py:171
  141.9 11.8 %collective-permute-start.12 = (bf16[4,128,384]{2,1,0:T(8,128)(2,1)S(1)}, bf16[4,128,384]{2,1,0:T(8,128)(2,1)S(1)}, u32[]{:S(2)}, u32[]{:S(2)}) collective-permute-start(bf16[4,128,384]{2,1,0:T(8,128)(2,1)S(1)} %bitcast.38), channel_id=1, source_target_pairs={{0,48},{16,0},{32,16},{48,32},{1,49},{17,1},{33,17},{49,33},{2,50}... | collective-permute-start | bytes 1179656 | tf_op jit(solution)/shard_map/ppermute | solution.py:173
  143.8 13.2 %collective-permute-start.11 = (bf16[4,128,384]{2,1,0:T(8,128)(2,1)S(1)}, bf16[4,128,384]{2,1,0:T(8,128)(2,1)S(1)}, u32[]{:S(2)}, u32[]{:S(2)}) collective-permute-start(bf16[4,128,384]{2,1,0:T(8,128)(2,1)S(1)} %bitcast.36), channel_id=1, source_target_pairs={{0,16},{16,32},{32,48},{48,0},{1,17},{17,33},{33,49},{49,1},{2,18}... | collective-permute-start | bytes 1179656 | tf_op jit(solution)/shard_map/ppermute | solution.py:172
  147.2 17.9 %collective-permute-start.13 = (bf16[4,128,384]{2,1,0:T(8,128)(2,1)S(1)}, bf16[4,128,384]{2,1,0:T(8,128)(2,1)S(1)}, u32[]{:S(2)}, u32[]{:S(2)}) collective-permute-start(bf16[4,128,384]{2,1,0:T(8,128)(2,1)S(1)} %collective-permute-done.9.refs_1_), channel_id=1, source_target_pairs={{0,16},{16,32},{32,48},{48,0},{1,17},{17,33},{33,49},{49,1},{2,18}... | collective-permute-start | bytes 1179656 | tf_op jit(solution)/shard_map/ppermute | solution.py:174
  149.1 16.0 %collective-permute-start.14 = (bf16[4,128,384]{2,1,0:T(8,128)(2,1)S(1)}, bf16[4,128,384]{2,1,0:T(8,128)(2,1)S(1)}, u32[]{:S(2)}, u32[]{:S(2)}) collective-permute-start(bf16[4,128,384]{2,1,0:T(8,128)(2,1)S(1)} %collective-permute-done.10.refs_2_), channel_id=1, source_target_pairs={{0,48},{16,0},{32,16},{48,32},{1,49},{17,1},{33,17},{49,33},{2,50}... | collective-permute-start | bytes 1179656 | tf_op jit(solution)/shard_map/ppermute | solution.py:175
  166.4 9.0 %collective-permute-start.15 = (bf16[8,128,384]{2,1,0:T(8,128)(2,1)S(1)}, bf16[8,128,384]{2,1,0:T(8,128)(2,1)S(1)}, u32[]{:S(2)}, u32[]{:S(2)}) collective-permute-start(bf16[8,128,384]{2,1,0:T(8,128)(2,1)S(1)} %get-tuple-element.12), channel_id=1, source_target_pairs={{0,8},{8,0},{1,9},{9,1},{2,10},{10,2},{3,11},{11,3},{4,12},{12,4},... | collective-permute-start | bytes 2359304 | tf_op jit(solution)/shard_map/ppermute | solution.py:186

commit v2 on v1

--- a/solution.py
+++ b/solution.py
@@ -8,12 +8,11 @@
 from jax.sharding import Mesh, PartitionSpec as P
 
 
-NZ, NX, NC, NY = 8, 4, 2, 8
+NQ, NP, NX, NC, NY = 4, 2, 4, 2, 8
 TILE, COLS = 128, 384
-HALF = NZ // 2
-CHIPS = NZ * NX
-NEAR_SPOTS = ((0, 0), (0, 1), (HALF, 2), (HALF, 1), (0, 2))
-FAR_SPOTS = ((0, 3), (HALF, 3))
+CHIPS = NQ * NP * NX
+NEAR_SPOTS = ((0, 0), (1, 0), (0, 1), (1, 2), (1, 1), (0, 2))
+FAR_SPOTS = ((0, 3), (1, 3))
 SOLVE_FLOPS = 2 * TILE * TILE * COLS
 PAIR_FLOPS = 2 * SOLVE_FLOPS
 
@@ -85,8 +84,8 @@
     for piece, (base, side) in zip(pieces, spots):
 
         def step(j, carry, piece=piece, base=base, side=side):
-            chip = (base + j) * NX + where[side]
-            pair = jnp.concatenate([mine[chip, core], other[level, chip]], axis=0)
+            chip = (base + 2 * j) * NX + where[side]
+            pair = jnp.concatenate([mine[chip, core], other[chip, core]], axis=0)
             product = jnp.dot(pair, piece[j], preferred_element_type=jnp.float32)
             state[0, slots[level, chip * NC + core]] += product[:TILE]
             state[1, received[level, chip * NC + core]] += product[TILE:]
@@ -160,20 +159,21 @@
 
 
 def gather_rows(block):
-    return lax.all_gather(block[None], "z", axis=0, tiled=True)
+    even_odd = lax.all_gather(block[None], "zq", axis=0, tiled=True)
+    return lax.all_gather(even_odd[None], "zp", axis=0, tiled=True)
 
 
 def gather_columns(own):
     up = functools.partial(lax.ppermute, axis_name="x", perm=ring(NX, 1))
     down = functools.partial(lax.ppermute, axis_name="x", perm=ring(NX, -1))
-    low, high = own[:HALF], own[HALF:]
+    low, high = own[0], own[1]
     low_left = up(low)
     high_right = down(high)
     high_left = up(high)
     low_right = down(low)
     low_far = up(low_left)
     high_far = down(high_right)
-    return [own, low_left, high_right, high_left, low_right], [low_far, high_far]
+    return [low, high, low_left, high_right, high_left, low_right], [low_far, high_far]
 
 
 def places():
@@ -186,29 +186,6 @@
     return lax.ppermute(value, "core", [(0, 1), (1, 0)])
 
 
-def pick_body(other, first, second, after, out):
-    del other, after
-    out[0] = first[:, 0]
-    out[1] = second[:, 0]
-
-
-def pick(first, second, after):
-    half = (CHIPS, 1, TILE, TILE)
-    grid_spec = pltpu.PrefetchScalarGridSpec(
-        num_scalar_prefetch=1,
-        grid=(1,),
-        in_specs=[
-            pl.BlockSpec(half, lambda i, other: (0, other[0], 0, 0)),
-            pl.BlockSpec(half, lambda i, other: (0, other[0], 0, 0)),
-            pl.BlockSpec(memory_space=pl.ANY),
-        ],
-        out_specs=pl.BlockSpec((2, CHIPS, TILE, TILE), lambda i, other: (0, 0, 0, 0)),
-    )
-    shape = jax.ShapeDtypeStruct((2, CHIPS, TILE, TILE), jnp.bfloat16)
-    other = (1 - lax.axis_index("core")).astype(jnp.int32)[None]
-    return call(pick_body, shape, None, None, (other, first, second, after), SOLVE_FLOPS, 12, grid_spec=grid_spec)
-
-
 def reduce_rows(state, near_other):
     received = swap(near_other)
     return lax.all_to_all(join(state, received), "y", 0, 0, tiled=True)
@@ -219,12 +196,11 @@
     mine_first = tiles_first.reshape(CHIPS, NC, TILE, TILE)
     mine_second = tiles_second.reshape(CHIPS, NC, TILE, TILE)
 
+    others = swap(mine_first)
     level_zero = solve_zero(inverses, rhs)
-    own = gather_rows(level_zero)
-    near, far = gather_columns(own)
+    near, far = gather_columns(gather_rows(level_zero))
     slots = jnp.concatenate([rows_first.reshape(1, CHIPS * NC), rows_second.reshape(1, CHIPS * NC)])
     received = swap(slots)
-    others = swap(pick(mine_first, mine_second, own))
     tables = (where, slots, received)
     state = early(tables, mine_first, others, near)
     state, near_other = late(0, tables, mine_first, others, state, far)
@@ -232,6 +208,7 @@
 
     level_one = solve_next(1, inverses, rhs, parts)
     near, far = gather_columns(gather_rows(level_one))
+    others = swap(mine_second)
     state = early(tables, mine_second, others, near, state)
     state, near_other = late(1, tables, mine_second, others, state, far)
     level_two = solve_next(2, inverses, rhs, reduce_rows(state, near_other))
@@ -239,9 +216,9 @@
 
 
 def solution(mesh):
-    grid = Mesh(mesh.devices.reshape(NZ, NX, NC, NY), ("z", "x", "core", "y"))
-    blocks = ("z", "x", "core", "y")
-    rows = ("z", "x", "core")
+    grid = Mesh(mesh.devices.reshape(NQ, NP, NX, NC, NY), ("zq", "zp", "x", "core", "y"))
+    blocks = ("zq", "zp", "x", "core", "y")
+    rows = ("zq", "zp", "x", "core")
     in_specs = (
         P(None, blocks, None, None),
         P(None, blocks, None, None),

time: 203 us -> 202 us (level)
  the two profiles are of different devices: /device:TPU:1 before, /device:TPU:5 now
where the time goes in v2:
time: 202 us; the launch traced here: 201 us
  blocking collectives  75.7 us (37%)
  starting transfers between devices  60.8 us (30%)
  waiting for transfers between devices  42.3 us (21%)
  Pallas kernels  12.4 us (6%)
  local copies, waits for them, and re-layouts  8.64 us (4%)
    all_gather x2, blocking collectives, gather_rows(): even_odd = lax.all_gather(block[None], 'zq', axis=0, tiled=True)  30.5 us
    all_to_all x1, blocking collectives, reduce_rows(): return lax.all_to_all(join(state, received), 'y', 0, 0, tiled=True)  26 us
    ppermute x5, starting transfers between devices, swap(): return lax.ppermute(value, 'core', [(0, 1), (1, 0)])  21.1 us
    all_to_all x1, waiting for transfers between devices, reduce_rows(): return lax.all_to_all(join(state, received), 'y', 0, 0, tiled=True)  21 us
    all_gather x2, blocking collectives, gather_rows(): return lax.all_gather(even_odd[None], 'zp', axis=0, tiled=True)  19.3 us
    pallas_call x9, Pallas kernels, call(): pl.pallas_call(body, out_shape=out_shape, input_output_aliases=aliases or...  12.4 us
    unnamed x22, local copies, waits for them, and re-layouts  8.39 us
    ppermute x2, starting transfers between devices, gather_columns(): low_left = up(low)  7.35 us
  transfers between devices with their start and end apart: 18, of which 10 were waited for; matrix products, arithmetic and copies ran while one was open for 0% of the time, Pallas kernels for 4%

profile of v2, /device:TPU:5, one launch (start us, length us, event | category | flops | bytes accessed | tf_op | source)
XLA Modules:
  0.0 201.0 jit_solution(15077559527970670397)
XLA Ops:
  0.0 2.7 %collective-permute-start.1 = (bf16[32,2,128,128]{3,2,1,0:T(8,128)(2,1)}, bf16[32,2,128,128]{3,2,1,0:T(8,128)(2,1)}, u32[]{:S(2)}, u32[]{:S(2)}) collective-permute-start(bf16[32,2,128,128]{3,2,1,0:T(8,128)(2,1)} %bitcast.21), channel_id=1, source_target_pairs={{0,8},{8,0},{1,9},{9,1},{2,10},{10,2},{3,11},{11,3},{4,12},{12,4},... | collective-permute-start | bytes 6291464 | tf_op jit(solution)/shard_map/ppermute | solution.py:186
  4.8 18.5 %all-gather = bf16[512,384]{1,0:T(8,128)(2,1)S(1)} all-gather(bf16[128,384]{1,0:T(8,128)(2,1)S(1)} %shard_map.64), channel_id=2, replica_groups=mesh['zq'=4,'zp'=2,'x'=4,'core'=2,'y'=8] {'zq'}, dimensions={0}, use_global_device_ids=true | all-gather | bytes 491520 | tf_op jit(solution)/shard_map/all_gather | solution.py:162
  23.3 10.7 %all-gather.1 = bf16[8,128,384]{2,1,0:T(8,128)(2,1)S(1)} all-gather(bf16[4,128,384]{2,1,0:T(8,128)(2,1)S(1)} %bitcast.27), channel_id=3, replica_groups=mesh['zq'=4,'zp'=2,'x'=4,'core'=2,'y'=8] {'zp'}, dimensions={0}, use_global_device_ids=true | all-gather | bytes 1179648 | tf_op jit(solution)/shard_map/all_gather | solution.py:163
  34.1 2.8 %collective-permute-start.2 = (bf16[4,128,384]{2,1,0:T(8,128)(2,1)S(1)}, bf16[4,128,384]{2,1,0:T(8,128)(2,1)S(1)}, u32[]{:S(2)}, u32[]{:S(2)}) collective-permute-start(bf16[4,128,384]{2,1,0:T(8,128)(2,1)S(1)} %get-tuple-element.16.refs_0_), channel_id=1, source_target_pairs={{0,16},{16,32},{32,48},{48,0},{1,17},{17,33},{33,49},{49,1},{2,18}... | collective-permute-start | bytes 1179656 | tf_op jit(solution)/shard_map/ppermute | solution.py:170
  36.9 2.5 %collective-permute-start.3 = (bf16[4,128,384]{2,1,0:T(8,128)(2,1)S(1)}, bf16[4,128,384]{2,1,0:T(8,128)(2,1)}, u32[]{:S(2)}, u32[]{:S(2)}) collective-permute-start(bf16[4,128,384]{2,1,0:T(8,128)(2,1)S(1)} %get-tuple-element.15.refs_1_), channel_id=1, source_target_pairs={{0,48},{16,0},{32,16},{48,32},{1,49},{17,1},{33,17},{49,33},{2,50}... | collective-permute-start | bytes 1179656 | tf_op jit(solution)/shard_map/ppermute | solution.py:171
  39.4 5.1 %collective-permute-start = (s32[2,64]{1,0:T(2,128)S(1)}, s32[2,64]{1,0:T(2,128)S(1)}, u32[]{:S(2)}, u32[]{:S(2)}) collective-permute-start(s32[2,64]{1,0:T(2,128)S(1)} %pad_add_fusion.slots), channel_id=1, source_target_pairs={{0,8},{8,0},{1,9},{9,1},{2,10},{10,2},{3,11},{11,3},{4,12},{12,4},... | collective-permute-start | bytes 1544 | tf_op jit(solution)/shard_map/ppermute | solution.py:186
  44.5 2.8 %collective-permute-start.4 = (bf16[4,128,384]{2,1,0:T(8,128)(2,1)S(1)}, bf16[4,128,384]{2,1,0:T(8,128)(2,1)}, u32[]{:S(2)}, u32[]{:S(2)}) collective-permute-start(bf16[4,128,384]{2,1,0:T(8,128)(2,1)S(1)} %get-tuple-element.15.refs_1_), channel_id=1, source_target_pairs={{0,16},{16,32},{32,48},{48,0},{1,17},{17,33},{33,49},{49,1},{2,18}... | collective-permute-start | bytes 1179656 | tf_op jit(solution)/shard_map/ppermute | solution.py:172
  47.4 2.5 %collective-permute-start.5 = (bf16[4,128,384]{2,1,0:T(8,128)(2,1)S(1)}, bf16[4,128,384]{2,1,0:T(8,128)(2,1)}, u32[]{:S(2)}, u32[]{:S(2)}) collective-permute-start(bf16[4,128,384]{2,1,0:T(8,128)(2,1)S(1)} %get-tuple-element.16.refs_0_), channel_id=1, source_target_pairs={{0,48},{16,0},{32,16},{48,32},{1,49},{17,1},{33,17},{49,33},{2,50}... | collective-permute-start | bytes 1179656 | tf_op jit(solution)/shard_map/ppermute | solution.py:173
  49.8 2.8 %collective-permute-start.6 = (bf16[4,128,384]{2,1,0:T(8,128)(2,1)S(1)}, bf16[4,128,384]{2,1,0:T(8,128)(2,1)}, u32[]{:S(2)}, u32[]{:S(2)}) collective-permute-start(bf16[4,128,384]{2,1,0:T(8,128)(2,1)S(1)} %collective-permute-done.2.refs_2_), channel_id=1, source_target_pairs={{0,16},{16,32},{32,48},{48,0},{1,17},{17,33},{33,49},{49,1},{2,18}... | collective-permute-start | bytes 1179656 | tf_op jit(solution)/shard_map/ppermute | solution.py:174
  52.7 2.5 %collective-permute-start.7 = (bf16[4,128,384]{2,1,0:T(8,128)(2,1)}, bf16[4,128,384]{2,1,0:T(8,128)(2,1)}, u32[]{:S(2)}, u32[]{:S(2)}) collective-permute-start(bf16[4,128,384]{2,1,0:T(8,128)(2,1)} %collective-permute-done.3.refs_3_), channel_id=1, source_target_pairs={{0,48},{16,0},{32,16},{48,32},{1,49},{17,1},{33,17},{49,33},{2,50}... | collective-permute-start | bytes 1179656 | tf_op jit(solution)/shard_map/ppermute | solution.py:175
  57.2 2.6 %collective-permute-done.5.refs_5_ = bf16[4,128,384]{2,1,0:T(8,128)(2,1)} collective-permute-done((bf16[4,128,384]{2,1,0:T(8,128)(2,1)S(1)}, bf16[4,128,384]{2,1,0:T(8,128)(2,1)}, u32[]{:S(2)}, u32[]{:S(2)}) %collective-permute-start.5) | collective-permute-done | bytes 393248 | tf_op jit(solution)/shard_map/ppermute | solution.py:173
  59.7 3.6 %shard_map.65.state = f32[2,16,128,384]{3,2,1,0:T(8,128)S(1)} custom-call(s32[5]{0:T(128)S(1)} %stack.36.where, s32[2,64]{1,0:T(2,128)S(1)} %pad_add_fusion.slots, s32[2,64]{1,0:T(2,128)S(1)} %collective-permute-done.received, bf16[32,2,128,128]{3,2,1,0:T(8,128)(2,1)S(1)} %bitcast.22, bf16[32,2,128,128]{3,2,1,0:T(8,128)(2,1)} %collective-permute-done.1.other, ...), custom_call_target="tpu_custom_call" | custom-call | flops 603979776 | bytes 4194304 | tf_op jit(solution)/shard_map/pallas_call | solution.py:35
  63.3 2.3 %collective-permute-done.6.low = bf16[4,128,384]{2,1,0:T(8,128)(2,1)} collective-permute-done((bf16[4,128,384]{2,1,0:T(8,128)(2,1)S(1)}, bf16[4,128,384]{2,1,0:T(8,128)(2,1)}, u32[]{:S(2)}, u32[]{:S(2)}) %collective-permute-start.6) | collective-permute-done | bytes 393248 | tf_op jit(solution)/shard_map/ppermute | solution.py:174
  65.6 2.6 %collective-permute-done.7.high = bf16[4,128,384]{2,1,0:T(8,128)(2,1)} collective-permute-done((bf16[4,128,384]{2,1,0:T(8,128)(2,1)}, bf16[4,128,384]{2,1,0:T(8,128)(2,1)}, u32[]{:S(2)}, u32[]{:S(2)}) %collective-permute-start.7) | collective-permute-done | bytes 393248 | tf_op jit(solution)/shard_map/ppermute | solution.py:175
  68.2 2.4 %shard_map.66 = (f32[2,16,128,384]{3,2,1,0:T(8,128)S(1)}, bf16[8,128,384]{2,1,0:T(8,128)(2,1)S(1)}) custom-call(s32[5]{0:T(128)S(1)} %stack.36.where, s32[2,64]{1,0:T(2,128)S(1)} %pad_add_fusion.slots, s32[2,64]{1,0:T(2,128)S(1)} %collective-permute-done.received, bf16[32,2,128,128]{3,2,1,0:T(8,128)(2,1)S(1)} %bitcast.23, ...), custom_call_target="tpu_custom_call", output_to_operand_aliasing={{0}: (5, {})} | custom-call | flops 201326592 | bytes 4194304 | tf_op jit(solution)/shard_map/pallas_call | solution.py:35
  70.6 3.1 %collective-permute-start.8 = (bf16[8,128,384]{2,1,0:T(8,128)(2,1)S(1)}, bf16[8,128,384]{2,1,0:T(8,128)(2,1)S(1)}, u32[]{:S(2)}, u32[]{:S(2)}) collective-permute-start(bf16[8,128,384]{2,1,0:T(8,128)(2,1)S(1)} %get-tuple-element.10), channel_id=1, source_target_pairs={{0,8},{8,0},{1,9},{9,1},{2,10},{10,2},{3,11},{11,3},{4,12},{12,4},... | collective-permute-start | bytes 2359304 | tf_op jit(solution)/shard_map/ppermute | solution.py:186
  75.7 2.8 %copy-done = f32[2,16,128,384]{3,2,1,0:T(8,128)} copy-done((f32[2,16,128,384]{3,2,1,0:T(8,128)}, f32[2,16,128,384]{3,2,1,0:T(8,128)S(1)}, u32[]{:S(2)}) %copy-start) | copy-done | bytes 6291480
  79.4 6.8 %all-to-all-start = ((bf16[8,128,384]{2,1,0:T(8,128)(2,1)}), bf16[8,128,384]{2,1,0:T(8,128)(2,1)S(1)}, u32[]{:S(2)}, u32[]{:S(2)}) async-start(bf16[8,128,384]{2,1,0:T(8,128)(2,1)} %copy-done.4), calls=%async_computation | async-start | bytes 1572864 | tf_op jit(solution)/shard_map/all_to_all | solution.py:191
  86.2 2.6 %collective-permute-start.9 = (bf16[32,2,128,128]{3,2,1,0:T(8,128)(2,1)S(1)}, bf16[32,2,128,128]{3,2,1,0:T(8,128)(2,1)}, u32[]{:S(2)}, u32[]{:S(2)}) collective-permute-start(bf16[32,2,128,128]{3,2,1,0:T(8,128)(2,1)S(1)} %bitcast.18), channel_id=1, source_target_pairs={{0,8},{8,0},{1,9},{9,1},{2,10},{10,2},{3,11},{11,3},{4,12},{12,4},... | collective-permute-start | bytes 6291464 | tf_op jit(solution)/shard_map/ppermute | solution.py:186
  88.8 21.0 %all-to-all-done.parts = bf16[8,128,384]{2,1,0:T(8,128)(2,1)S(1)} async-done(((bf16[8,128,384]{2,1,0:T(8,128)(2,1)}), bf16[8,128,384]{2,1,0:T(8,128)(2,1)S(1)}, u32[]{:S(2)}, u32[]{:S(2)}) %all-to-all-start) | async-done | bytes 786464 | tf_op jit(solution)/shard_map/all_to_all | solution.py:191
  110.1 12.0 %all-gather.2 = bf16[512,384]{1,0:T(8,128)(2,1)S(1)} all-gather(bf16[128,384]{1,0:T(8,128)(2,1)S(1)} %shard_map.68), channel_id=4, replica_groups=mesh['zq'=4,'zp'=2,'x'=4,'core'=2,'y'=8] {'zq'}, dimensions={0}, use_global_device_ids=true | all-gather | bytes 491520 | tf_op jit(solution)/shard_map/all_gather | solution.py:162
  122.1 8.6 %all-gather.3 = bf16[8,128,384]{2,1,0:T(8,128)(2,1)S(1)} all-gather(bf16[4,128,384]{2,1,0:T(8,128)(2,1)S(1)} %bitcast.28), channel_id=5, replica_groups=mesh['zq'=4,'zp'=2,'x'=4,'core'=2,'y'=8] {'zp'}, dimensions={0}, use_global_device_ids=true | all-gather | bytes 1179648 | tf_op jit(solution)/shard_map/all_gather | solution.py:163
  130.7 4.5 %collective-permute-start.10 = (bf16[4,128,384]{2,1,0:T(8,128)(2,1)S(1)}, bf16[4,128,384]{2,1,0:T(8,128)(2,1)S(1)}, u32[]{:S(2)}, u32[]{:S(2)}) collective-permute-start(bf16[4,128,384]{2,1,0:T(8,128)(2,1)S(1)} %get-tuple-element.14.refs_0_), channel_id=1, source_target_pairs={{0,16},{16,32},{32,48},{48,0},{1,17},{17,33},{33,49},{49,1},{2,18}... | collective-permute-start | bytes 1179656 | tf_op jit(solution)/shard_map/ppermute | solution.py:170
  137.2 3.4 %collective-permute-start.12 = (bf16[4,128,384]{2,1,0:T(8,128)(2,1)S(1)}, bf16[4,128,384]{2,1,0:T(8,128)(2,1)S(1)}, u32[]{:S(2)}, u32[]{:S(2)}) collective-permute-start(bf16[4,128,384]{2,1,0:T(8,128)(2,1)S(1)} %get-tuple-element.13.refs_1_), channel_id=1, source_target_pairs={{0,16},{16,32},{32,48},{48,0},{1,17},{17,33},{33,49},{49,1},{2,18}... | collective-permute-start | bytes 1179656 | tf_op jit(solution)/shard_map/ppermute | solution.py:172
  142.5 3.4 %collective-permute-start.14 = (bf16[4,128,384]{2,1,0:T(8,128)(2,1)S(1)}, bf16[4,128,384]{2,1,0:T(8,128)(2,1)S(1)}, u32[]{:S(2)}, u32[]{:S(2)}) collective-permute-start(bf16[4,128,384]{2,1,0:T(8,128)(2,1)S(1)} %collective-permute-done.10.refs_2_), channel_id=1, source_target_pairs={{0,16},{16,32},{32,48},{48,0},{1,17},{17,33},{33,49},{49,1},{2,18}... | collective-permute-start | bytes 1179656 | tf_op jit(solution)/shard_map/ppermute | solution.py:174
  147.8 2.3 %collective-permute-done.12.refs_4_ = bf16[4,128,384]{2,1,0:T(8,128)(2,1)S(1)} collective-permute-done((bf16[4,128,384]{2,1,0:T(8,128)(2,1)S(1)}, bf16[4,128,384]{2,1,0:T(8,128)(2,1)S(1)}, u32[]{:S(2)}, u32[]{:S(2)}) %collective-permute-start.12) | collective-permute-done | bytes 393248 | tf_op jit(solution)/shard_map/ppermute | solution.py:172
  150.1 3.4 %collective-permute-done.13.refs_5_ = bf16[4,128,384]{2,1,0:T(8,128)(2,1)S(1)} collective-permute-done((bf16[4,128,384]{2,1,0:T(8,128)(2,1)S(1)}, bf16[4,128,384]{2,1,0:T(8,128)(2,1)S(1)}, u32[]{:S(2)}, u32[]{:S(2)}) %collective-permute-start.13) | collective-permute-done | bytes 393248 | tf_op jit(solution)/shard_map/ppermute | solution.py:173
  153.6 2.8 %copy-done.1 = f32[2,16,128,384]{3,2,1,0:T(8,128)S(1)} copy-done((f32[2,16,128,384]{3,2,1,0:T(8,128)S(1)}, f32[2,16,128,384]{3,2,1,0:T(8,128)}, u32[]{:S(2)}) %copy-start.1) | copy-done | bytes 6291480
  156.4 3.2 %shard_map.69.state = f32[2,8,128,384]{3,2,1,0:T(8,128)S(1)} custom-call(s32[5]{0:T(128)S(1)} %stack.36.where, s32[2,64]{1,0:T(2,128)S(1)} %pad_add_fusion.slots, s32[2,64]{1,0:T(2,128)S(1)} %collective-permute-done.received, bf16[32,2,128,128]{3,2,1,0:T(8,128)(2,1)S(1)} %bitcast.19, bf16[32,2,128,128]{3,2,1,0:T(8,128)(2,1)} %collective-permute-done.9.other, ...), custom_call_target="tpu_custom_call" | custom-call | flops 603979776 | bytes 4194304 | tf_op jit(solution)/shard_map/pallas_call | solution.py:35
  159.6 2.4 %collective-permute-done.15.high = bf16[4,128,384]{2,1,0:T(8,128)(2,1)S(1)} collective-permute-done((bf16[4,128,384]{2,1,0:T(8,128)(2,1)S(1)}, bf16[4,128,384]{2,1,0:T(8,128)(2,1)S(1)}, u32[]{:S(2)}, u32[]{:S(2)}) %collective-permute-start.15) | collective-permute-done | bytes 393248 | tf_op jit(solution)/shard_map/ppermute | solution.py:175
  164.3 7.7 %collective-permute-start.16 = (bf16[8,128,384]{2,1,0:T(8,128)(2,1)S(1)}, bf16[8,128,384]{2,1,0:T(8,128)(2,1)S(1)}, u32[]{:S(2)}, u32[]{:S(2)}) collective-permute-start(bf16[8,128,384]{2,1,0:T(8,128)(2,1)S(1)} %get-tuple-element.12), channel_id=1, source_target_pairs={{0,8},{8,0},{1,9},{9,1},{2,10},{10,2},{3,11},{11,3},{4,12},{12,4},... | collective-permute-start | bytes 2359304 | tf_op jit(solution)/shard_map/ppermute | solution.py:186
  174.0 26.0 %all_to_all.10.parts = bf16[8,128,384]{2,1,0:T(8,128)(2,1)S(1)} all-to-all(bf16[8,128,384]{2,1,0:T(8,128)(2,1)S(1)} %shard_map.71), channel_id=1, replica_groups=mesh['zq'=4,'zp'=2,'x'=4,'core'=2,'y'=8] {'y'}, dimensions={0} | all-to-all | bytes 1572864 | tf_op jit(solution)/shard_map/all_to_all | solution.py:191
  (45 shorter events, 18.5 us)
Async XLA Ops:
  0.0 59.7 %copy-start.3 = (bf16[1,64,1,128,128]{4,3,2,1,0:T(8,128)(2,1)S(1)}, bf16[1,64,1,128,128]{4,3,2,1,0:T(8,128)(2,1)}, u32[]{:S(2)}) copy-start(bf16[1,64,1,128,128]{4,3,2,1,0:T(8,128)(2,1)} %param.8) | copy-start | bytes 6291460
  0.0 59.7 %collective-permute-start.1 = (bf16[32,2,128,128]{3,2,1,0:T(8,128)(2,1)}, bf16[32,2,128,128]{3,2,1,0:T(8,128)(2,1)}, u32[]{:S(2)}, u32[]{:S(2)}) collective-permute-start(bf16[32,2,128,128]{3,2,1,0:T(8,128)(2,1)} %bitcast.21), channel_id=1, source_target_pairs={{0,8},{8,0},{1,9},{9,1},{2,10},{10,2},{3,11},{11,3},{4,12},{12,4},... | collective-permute-start | bytes 6291464 | tf_op jit(solution)/shard_map/ppermute | solution.py:186
  2.7 1.0 copy-start.5
  3.7 0.9 copy-start.7
  4.6 34.8 %copy-start.9 = (s32[1,64,1]{1,2,0:T(1,128)S(1)}, s32[1,64,1]{1,2,0:T(1,128)}, u32[]{:S(2)}) copy-start(s32[1,64,1]{1,2,0:T(1,128)} %param.11) | copy-start | bytes 772
  4.6 34.8 %copy-start.10 = (s32[1,64,1]{1,2,0:T(1,128)S(1)}, s32[1,64,1]{1,2,0:T(1,128)}, u32[]{:S(2)}) copy-start(s32[1,64,1]{1,2,0:T(1,128)} %param.9) | copy-start | bytes 772
  34.1 15.8 %collective-permute-start.2 = (bf16[4,128,384]{2,1,0:T(8,128)(2,1)S(1)}, bf16[4,128,384]{2,1,0:T(8,128)(2,1)S(1)}, u32[]{:S(2)}, u32[]{:S(2)}) collective-permute-start(bf16[4,128,384]{2,1,0:T(8,128)(2,1)S(1)} %get-tuple-element.16.refs_0_), channel_id=1, source_target_pairs={{0,16},{16,32},{32,48},{48,0},{1,17},{17,33},{33,49},{49,1},{2,18}... | collective-permute-start | bytes 1179656 | tf_op jit(solution)/shard_map/ppermute | solution.py:170
  36.9 15.8 %collective-permute-start.3 = (bf16[4,128,384]{2,1,0:T(8,128)(2,1)S(1)}, bf16[4,128,384]{2,1,0:T(8,128)(2,1)}, u32[]{:S(2)}, u32[]{:S(2)}) collective-permute-start(bf16[4,128,384]{2,1,0:T(8,128)(2,1)S(1)} %get-tuple-element.15.refs_1_), channel_id=1, source_target_pairs={{0,48},{16,0},{32,16},{48,32},{1,49},{17,1},{33,17},{49,33},{2,50}... | collective-permute-start | bytes 1179656 | tf_op jit(solution)/shard_map/ppermute | solution.py:171
  39.4 8.0 %collective-permute-start = (s32[2,64]{1,0:T(2,128)S(1)}, s32[2,64]{1,0:T(2,128)S(1)}, u32[]{:S(2)}, u32[]{:S(2)}) collective-permute-start(s32[2,64]{1,0:T(2,128)S(1)} %pad_add_fusion.slots), channel_id=1, source_target_pairs={{0,8},{8,0},{1,9},{9,1},{2,10},{10,2},{3,11},{11,3},{4,12},{12,4},... | collective-permute-start | bytes 1544 | tf_op jit(solution)/shard_map/ppermute | solution.py:186
  44.5 12.7 %collective-permute-start.4 = (bf16[4,128,384]{2,1,0:T(8,128)(2,1)S(1)}, bf16[4,128,384]{2,1,0:T(8,128)(2,1)}, u32[]{:S(2)}, u32[]{:S(2)}) collective-permute-start(bf16[4,128,384]{2,1,0:T(8,128)(2,1)S(1)} %get-tuple-element.15.refs_1_), channel_id=1, source_target_pairs={{0,16},{16,32},{32,48},{48,0},{1,17},{17,33},{33,49},{49,1},{2,18}... | collective-permute-start | bytes 1179656 | tf_op jit(solution)/shard_map/ppermute | solution.py:172
  47.4 12.4 %collective-permute-start.5 = (bf16[4,128,384]{2,1,0:T(8,128)(2,1)S(1)}, bf16[4,128,384]{2,1,0:T(8,128)(2,1)}, u32[]{:S(2)}, u32[]{:S(2)}) collective-permute-start(bf16[4,128,384]{2,1,0:T(8,128)(2,1)S(1)} %get-tuple-element.16.refs_0_), channel_id=1, source_target_pairs={{0,48},{16,0},{32,16},{48,32},{1,49},{17,1},{33,17},{49,33},{2,50}... | collective-permute-start | bytes 1179656 | tf_op jit(solution)/shard_map/ppermute | solution.py:173
  49.8 15.8 %collective-permute-start.6 = (bf16[4,128,384]{2,1,0:T(8,128)(2,1)S(1)}, bf16[4,128,384]{2,1,0:T(8,128)(2,1)}, u32[]{:S(2)}, u32[]{:S(2)}) collective-permute-start(bf16[4,128,384]{2,1,0:T(8,128)(2,1)S(1)} %collective-permute-done.2.refs_2_), channel_id=1, source_target_pairs={{0,16},{16,32},{32,48},{48,0},{1,17},{17,33},{33,49},{49,1},{2,18}... | collective-permute-start | bytes 1179656 | tf_op jit(solution)/shard_map/ppermute | solution.py:174
  52.7 15.5 %collective-permute-start.7 = (bf16[4,128,384]{2,1,0:T(8,128)(2,1)}, bf16[4,128,384]{2,1,0:T(8,128)(2,1)}, u32[]{:S(2)}, u32[]{:S(2)}) collective-permute-start(bf16[4,128,384]{2,1,0:T(8,128)(2,1)} %collective-permute-done.3.refs_3_), channel_id=1, source_target_pairs={{0,48},{16,0},{32,16},{48,32},{1,49},{17,1},{33,17},{49,33},{2,50}... | collective-permute-start | bytes 1179656 | tf_op jit(solution)/shard_map/ppermute | solution.py:175
  70.6 5.0 %collective-permute-start.8 = (bf16[8,128,384]{2,1,0:T(8,128)(2,1)S(1)}, bf16[8,128,384]{2,1,0:T(8,128)(2,1)S(1)}, u32[]{:S(2)}, u32[]{:S(2)}) collective-permute-start(bf16[8,128,384]{2,1,0:T(8,128)(2,1)S(1)} %get-tuple-element.10), channel_id=1, source_target_pairs={{0,8},{8,0},{1,9},{9,1},{2,10},{10,2},{3,11},{11,3},{4,12},{12,4},... | collective-permute-start | bytes 2359304 | tf_op jit(solution)/shard_map/ppermute | solution.py:186
  75.5 10.7 %copy-start.2 = (bf16[1,64,1,128,128]{4,3,2,1,0:T(8,128)(2,1)S(1)}, bf16[1,64,1,128,128]{4,3,2,1,0:T(8,128)(2,1)}, u32[]{:S(2)}) copy-start(bf16[1,64,1,128,128]{4,3,2,1,0:T(8,128)(2,1)} %param.10) | copy-start | bytes 6291460
  75.5 34.3 %copy-start.6 = (bf16[3,1,128,384]{3,2,1,0:T(8,128)(2,1)S(1)}, bf16[3,1,128,384]{3,2,1,0:T(8,128)(2,1)}, u32[]{:S(2)}) copy-start(bf16[3,1,128,384]{3,2,1,0:T(8,128)(2,1)} %right.5) | copy-start | bytes 884740
  75.5 34.3 %copy-start.8 = (bf16[3,1,128,128]{3,2,1,0:T(8,128)(2,1)S(1)}, bf16[3,1,128,128]{3,2,1,0:T(8,128)(2,1)}, u32[]{:S(2)}) copy-start(bf16[3,1,128,128]{3,2,1,0:T(8,128)(2,1)} %inverse.5) | copy-start | bytes 294916
  75.7 2.8 %copy-start = (f32[2,16,128,384]{3,2,1,0:T(8,128)}, f32[2,16,128,384]{3,2,1,0:T(8,128)S(1)}, u32[]{:S(2)}) copy-start(f32[2,16,128,384]{3,2,1,0:T(8,128)S(1)} %get-tuple-element.9.state.later) | copy-start | bytes 18874372
  78.5 0.9 copy-start.4
  79.4 30.4 %all-to-all-start = ((bf16[8,128,384]{2,1,0:T(8,128)(2,1)}), bf16[8,128,384]{2,1,0:T(8,128)(2,1)S(1)}, u32[]{:S(2)}, u32[]{:S(2)}) async-start(bf16[8,128,384]{2,1,0:T(8,128)(2,1)} %copy-done.4), calls=%async_computation | async-start | bytes 1572864 | tf_op jit(solution)/shard_map/all_to_all | solution.py:191
  86.2 61.6 %collective-permute-start.9 = (bf16[32,2,128,128]{3,2,1,0:T(8,128)(2,1)S(1)}, bf16[32,2,128,128]{3,2,1,0:T(8,128)(2,1)}, u32[]{:S(2)}, u32[]{:S(2)}) collective-permute-start(bf16[32,2,128,128]{3,2,1,0:T(8,128)(2,1)S(1)} %bitcast.18), channel_id=1, source_target_pairs={{0,8},{8,0},{1,9},{9,1},{2,10},{10,2},{3,11},{11,3},{4,12},{12,4},... | collective-permute-start | bytes 6291464 | tf_op jit(solution)/shard_map/ppermute | solution.py:186
  130.7 11.8 %collective-permute-start.10 = (bf16[4,128,384]{2,1,0:T(8,128)(2,1)S(1)}, bf16[4,128,384]{2,1,0:T(8,128)(2,1)S(1)}, u32[]{:S(2)}, u32[]{:S(2)}) collective-permute-start(bf16[4,128,384]{2,1,0:T(8,128)(2,1)S(1)} %get-tuple-element.14.refs_0_), channel_id=1, source_target_pairs={{0,16},{16,32},{32,48},{48,0},{1,17},{17,33},{33,49},{49,1},{2,18}... | collective-permute-start | bytes 1179656 | tf_op jit(solution)/shard_map/ppermute | solution.py:170
  135.2 10.6 %collective-permute-start.11 = (bf16[4,128,384]{2,1,0:T(8,128)(2,1)S(1)}, bf16[4,128,384]{2,1,0:T(8,128)(2,1)S(1)}, u32[]{:S(2)}, u32[]{:S(2)}) collective-permute-start(bf16[4,128,384]{2,1,0:T(8,128)(2,1)S(1)} %get-tuple-element.13.refs_1_), channel_id=1, source_target_pairs={{0,48},{16,0},{32,16},{48,32},{1,49},{17,1},{33,17},{49,33},{2,50}... | collective-permute-start | bytes 1179656 | tf_op jit(solution)/shard_map/ppermute | solution.py:171
  137.2 12.9 %collective-permute-start.12 = (bf16[4,128,384]{2,1,0:T(8,128)(2,1)S(1)}, bf16[4,128,384]{2,1,0:T(8,128)(2,1)S(1)}, u32[]{:S(2)}, u32[]{:S(2)}) collective-permute-start(bf16[4,128,384]{2,1,0:T(8,128)(2,1)S(1)} %get-tuple-element.13.refs_1_), channel_id=1, source_target_pairs={{0,16},{16,32},{32,48},{48,0},{1,17},{17,33},{33,49},{49,1},{2,18}... | collective-permute-start | bytes 1179656 | tf_op jit(solution)/shard_map/ppermute | solution.py:172
  140.5 13.0 %collective-permute-start.13 = (bf16[4,128,384]{2,1,0:T(8,128)(2,1)S(1)}, bf16[4,128,384]{2,1,0:T(8,128)(2,1)S(1)}, u32[]{:S(2)}, u32[]{:S(2)}) collective-permute-start(bf16[4,128,384]{2,1,0:T(8,128)(2,1)S(1)} %get-tuple-element.14.refs_0_), channel_id=1, source_target_pairs={{0,48},{16,0},{32,16},{48,32},{1,49},{17,1},{33,17},{49,33},{2,50}... | collective-permute-start | bytes 1179656 | tf_op jit(solution)/shard_map/ppermute | solution.py:173
  142.5 17.1 %collective-permute-start.14 = (bf16[4,128,384]{2,1,0:T(8,128)(2,1)S(1)}, bf16[4,128,384]{2,1,0:T(8,128)(2,1)S(1)}, u32[]{:S(2)}, u32[]{:S(2)}) collective-permute-start(bf16[4,128,384]{2,1,0:T(8,128)(2,1)S(1)} %collective-permute-done.10.refs_2_), channel_id=1, source_target_pairs={{0,16},{16,32},{32,48},{48,0},{1,17},{17,33},{33,49},{49,1},{2,18}... | collective-permute-start | bytes 1179656 | tf_op jit(solution)/shard_map/ppermute | solution.py:174
  145.9 16.1 %collective-permute-start.15 = (bf16[4,128,384]{2,1,0:T(8,128)(2,1)S(1)}, bf16[4,128,384]{2,1,0:T(8,128)(2,1)S(1)}, u32[]{:S(2)}, u32[]{:S(2)}) collective-permute-start(bf16[4,128,384]{2,1,0:T(8,128)(2,1)S(1)} %collective-permute-done.11.refs_3_), channel_id=1, source_target_pairs={{0,48},{16,0},{32,16},{48,32},{1,49},{17,1},{33,17},{49,33},{2,50}... | collective-permute-start | bytes 1179656 | tf_op jit(solution)/shard_map/ppermute | solution.py:175
  153.6 2.8 %copy-start.1 = (f32[2,16,128,384]{3,2,1,0:T(8,128)S(1)}, f32[2,16,128,384]{3,2,1,0:T(8,128)}, u32[]{:S(2)}) copy-start(f32[2,16,128,384]{3,2,1,0:T(8,128)} %copy-done) | copy-start | bytes 18874372
  164.3 9.6 %collective-permute-start.16 = (bf16[8,128,384]{2,1,0:T(8,128)(2,1)S(1)}, bf16[8,128,384]{2,1,0:T(8,128)(2,1)S(1)}, u32[]{:S(2)}, u32[]{:S(2)}) collective-permute-start(bf16[8,128,384]{2,1,0:T(8,128)(2,1)S(1)} %get-tuple-element.12), channel_id=1, source_target_pairs={{0,8},{8,0},{1,9},{9,1},{2,10},{10,2},{3,11},{11,3},{4,12},{12,4},... | collective-permute-start | bytes 2359304 | tf_op jit(solution)/shard_map/ppermute | solution.py:186

commit v3 on v2

--- a/solution.py
+++ b/solution.py
@@ -59,7 +59,7 @@
 
 def solve_zero(inverses, rhs):
     grid_spec = pl.GridSpec(grid=(1,), in_specs=level_specs(0), out_specs=pl.BlockSpec((TILE, COLS), lambda i: (0, 0)))
-    return call(solve_zero_body, block_shape(jnp.bfloat16), None, None, (inverses, rhs), SOLVE_FLOPS, 8, grid_spec=grid_spec)
+    return call(solve_zero_body, block_shape(jnp.bfloat16), None, None, (inverses, rhs), SOLVE_FLOPS, 60, grid_spec=grid_spec)
 
 
 def solve_body(inverse, right, parts, out):
@@ -121,20 +121,42 @@
 
 def late_body(level, where, slots, received, mine, other, state, low, high, out, near_other):
     del state
-    accumulate(where, slots, received, level, mine, other, (low, high), FAR_SPOTS, out)
+    core = where[NX]
+    for piece, (base, side) in zip((low, high), FAR_SPOTS):
+        for j in range(NQ):
+            row = base + 2 * j
+            entry = (row * NX + where[side]) * NC + core
+            pair = jnp.concatenate([mine[row, 0, 0], other[row, 0, 0]], axis=0)
+            product = jnp.dot(pair, piece[j], preferred_element_type=jnp.float32)
+            out[0, slots[level, entry]] += product[:TILE]
+            out[1, received[level, entry]] += product[TILE:]
     near_other[...] = out[1, :NY].astype(jnp.bfloat16)
 
 
+def whole(shape):
+    return pl.BlockSpec(shape, lambda i, where: (0,) * len(shape))
+
+
 def late(level, tables, mine, other, state, pieces):
+    by_place = (NQ * NP, NX, NC, TILE, TILE)
+    column = pl.BlockSpec((NQ * NP, 1, 1, TILE, TILE), lambda i, where: (0, where[3], where[NX], 0, 0))
+    slab = (NQ, TILE, COLS)
+    grid_spec = pltpu.PrefetchScalarGridSpec(
+        num_scalar_prefetch=1,
+        grid=(1,),
+        in_specs=[smem()] * 2 + [column] * 2 + [whole(state.shape), whole(slab), whole(slab)],
+        out_specs=[whole(state.shape), whole((NY, TILE, COLS))],
+    )
     return call(
         functools.partial(late_body, level),
         [jax.ShapeDtypeStruct(state.shape, jnp.float32), block_shape(jnp.bfloat16, NY)],
-        [smem()] * 3 + [vmem()] * 5,
-        [vmem()] * 2,
-        tables + (mine, other, state) + tuple(pieces),
+        None,
+        None,
+        tables + (mine.reshape(by_place), other.reshape(by_place), state) + tuple(pieces),
         8 * PAIR_FLOPS,
         28,
         aliases={5: 0},
+        grid_spec=grid_spec,
     )
 
 
@@ -196,21 +218,21 @@
     mine_first = tiles_first.reshape(CHIPS, NC, TILE, TILE)
     mine_second = tiles_second.reshape(CHIPS, NC, TILE, TILE)
 
-    others = swap(mine_first)
+    other_first = swap(mine_first)
     level_zero = solve_zero(inverses, rhs)
     near, far = gather_columns(gather_rows(level_zero))
     slots = jnp.concatenate([rows_first.reshape(1, CHIPS * NC), rows_second.reshape(1, CHIPS * NC)])
     received = swap(slots)
     tables = (where, slots, received)
-    state = early(tables, mine_first, others, near)
-    state, near_other = late(0, tables, mine_first, others, state, far)
+    state = early(tables, mine_first, other_first, near)
+    state, near_other = late(0, tables, mine_first, other_first, state, far)
     parts = reduce_rows(state, near_other)
 
     level_one = solve_next(1, inverses, rhs, parts)
     near, far = gather_columns(gather_rows(level_one))
-    others = swap(mine_second)
-    state = early(tables, mine_second, others, near, state)
-    state, near_other = late(1, tables, mine_second, others, state, far)
+    other_second = swap(mine_second)
+    state = early(tables, mine_second, other_second, near, state)
+    state, near_other = late(1, tables, mine_second, other_second, state, far)
     level_two = solve_next(2, inverses, rhs, reduce_rows(state, near_other))
     return jnp.stack([level_zero, level_one, level_two])[:, None]
 

time: 202 us -> 202 us (level)
    unnamed x22 -> x20, local copies, waits for them, and re-layouts: 8.39 us -> 6.56 us
where the time goes in v3:
time: 202 us; the launch traced here: 201 us
  blocking collectives  75.9 us (38%)
  starting transfers between devices  60.8 us (30%)
  waiting for transfers between devices  42.3 us (21%)
  Pallas kernels  13.9 us (7%)
  local copies, waits for them, and re-layouts  6.81 us (3%)
    all_gather x2, blocking collectives, gather_rows(): even_odd = lax.all_gather(block[None], 'zq', axis=0, tiled=True)  30.7 us
    all_to_all x1, blocking collectives, reduce_rows(): return lax.all_to_all(join(state, received), 'y', 0, 0, tiled=True)  26 us
    ppermute x5, starting transfers between devices, swap(): return lax.ppermute(value, 'core', [(0, 1), (1, 0)])  21.2 us
    all_to_all x1, waiting for transfers between devices, reduce_rows(): return lax.all_to_all(join(state, received), 'y', 0, 0, tiled=True)  21 us
    all_gather x2, blocking collectives, gather_rows(): return lax.all_gather(even_odd[None], 'zp', axis=0, tiled=True)  19.3 us
    pallas_call x9, Pallas kernels, call(): pl.pallas_call(body, out_shape=out_shape, input_output_aliases=aliases or...  13.9 us
    ppermute x2, starting transfers between devices, gather_columns(): low_left = up(low)  7.33 us
    all_to_all x1, starting transfers between devices, reduce_rows(): return lax.all_to_all(join(state, received), 'y', 0, 0, tiled=True)  6.82 us
  transfers between devices with their start and end apart: 18, of which 10 were waited for; matrix products, arithmetic and copies ran while one was open for 0% of the time, Pallas kernels for 4%

profile of v3, /device:TPU:5, one launch (start us, length us, event | category | flops | bytes accessed | tf_op | source)
XLA Modules:
  0.0 200.9 jit_solution(14245860801058892481)
XLA Ops:
  0.0 2.7 %collective-permute-start.1 = (bf16[32,2,128,128]{3,2,1,0:T(8,128)(2,1)}, bf16[32,2,128,128]{3,2,1,0:T(8,128)(2,1)}, u32[]{:S(2)}, u32[]{:S(2)}) collective-permute-start(bf16[32,2,128,128]{3,2,1,0:T(8,128)(2,1)} %bitcast.25), channel_id=1, source_target_pairs={{0,8},{8,0},{1,9},{9,1},{2,10},{10,2},{3,11},{11,3},{4,12},{12,4},... | collective-permute-start | bytes 6291464 | tf_op jit(solution)/shard_map/ppermute | solution.py:208
  4.5 18.7 %all-gather = bf16[512,384]{1,0:T(8,128)(2,1)S(1)} all-gather(bf16[128,384]{1,0:T(8,128)(2,1)} %shard_map.64), channel_id=2, replica_groups=mesh['zq'=4,'zp'=2,'x'=4,'core'=2,'y'=8] {'zq'}, dimensions={0}, use_global_device_ids=true | all-gather | bytes 491520 | tf_op jit(solution)/shard_map/all_gather | solution.py:184
  23.2 10.7 %all-gather.1 = bf16[8,128,384]{2,1,0:T(8,128)(2,1)S(1)} all-gather(bf16[4,128,384]{2,1,0:T(8,128)(2,1)S(1)} %bitcast.30), channel_id=3, replica_groups=mesh['zq'=4,'zp'=2,'x'=4,'core'=2,'y'=8] {'zp'}, dimensions={0}, use_global_device_ids=true | all-gather | bytes 1179648 | tf_op jit(solution)/shard_map/all_gather | solution.py:185
  34.0 2.8 %collective-permute-start.2 = (bf16[4,128,384]{2,1,0:T(8,128)(2,1)S(1)}, bf16[4,128,384]{2,1,0:T(8,128)(2,1)S(1)}, u32[]{:S(2)}, u32[]{:S(2)}) collective-permute-start(bf16[4,128,384]{2,1,0:T(8,128)(2,1)S(1)} %get-tuple-element.16.refs_0_), channel_id=1, source_target_pairs={{0,16},{16,32},{32,48},{48,0},{1,17},{17,33},{33,49},{49,1},{2,18}... | collective-permute-start | bytes 1179656 | tf_op jit(solution)/shard_map/ppermute | solution.py:192
  36.8 2.5 %collective-permute-start.3 = (bf16[4,128,384]{2,1,0:T(8,128)(2,1)S(1)}, bf16[4,128,384]{2,1,0:T(8,128)(2,1)}, u32[]{:S(2)}, u32[]{:S(2)}) collective-permute-start(bf16[4,128,384]{2,1,0:T(8,128)(2,1)S(1)} %get-tuple-element.15.refs_1_), channel_id=1, source_target_pairs={{0,48},{16,0},{32,16},{48,32},{1,49},{17,1},{33,17},{49,33},{2,50}... | collective-permute-start | bytes 1179656 | tf_op jit(solution)/shard_map/ppermute | solution.py:193
  39.3 5.1 %collective-permute-start = (s32[2,64]{1,0:T(2,128)S(1)}, s32[2,64]{1,0:T(2,128)S(1)}, u32[]{:S(2)}, u32[]{:S(2)}) collective-permute-start(s32[2,64]{1,0:T(2,128)S(1)} %pad_add_fusion.slots), channel_id=1, source_target_pairs={{0,8},{8,0},{1,9},{9,1},{2,10},{10,2},{3,11},{11,3},{4,12},{12,4},... | collective-permute-start | bytes 1544 | tf_op jit(solution)/shard_map/ppermute | solution.py:208
  44.4 2.8 %collective-permute-start.4 = (bf16[4,128,384]{2,1,0:T(8,128)(2,1)S(1)}, bf16[4,128,384]{2,1,0:T(8,128)(2,1)}, u32[]{:S(2)}, u32[]{:S(2)}) collective-permute-start(bf16[4,128,384]{2,1,0:T(8,128)(2,1)S(1)} %get-tuple-element.15.refs_1_), channel_id=1, source_target_pairs={{0,16},{16,32},{32,48},{48,0},{1,17},{17,33},{33,49},{49,1},{2,18}... | collective-permute-start | bytes 1179656 | tf_op jit(solution)/shard_map/ppermute | solution.py:194
  47.3 2.5 %collective-permute-start.5 = (bf16[4,128,384]{2,1,0:T(8,128)(2,1)S(1)}, bf16[4,128,384]{2,1,0:T(8,128)(2,1)}, u32[]{:S(2)}, u32[]{:S(2)}) collective-permute-start(bf16[4,128,384]{2,1,0:T(8,128)(2,1)S(1)} %get-tuple-element.16.refs_0_), channel_id=1, source_target_pairs={{0,48},{16,0},{32,16},{48,32},{1,49},{17,1},{33,17},{49,33},{2,50}... | collective-permute-start | bytes 1179656 | tf_op jit(solution)/shard_map/ppermute | solution.py:195
  49.7 2.8 %collective-permute-start.6 = (bf16[4,128,384]{2,1,0:T(8,128)(2,1)S(1)}, bf16[4,128,384]{2,1,0:T(8,128)(2,1)}, u32[]{:S(2)}, u32[]{:S(2)}) collective-permute-start(bf16[4,128,384]{2,1,0:T(8,128)(2,1)S(1)} %collective-permute-done.2.refs_2_), channel_id=1, source_target_pairs={{0,16},{16,32},{32,48},{48,0},{1,17},{17,33},{33,49},{49,1},{2,18}... | collective-permute-start | bytes 1179656 | tf_op jit(solution)/shard_map/ppermute | solution.py:196
  52.6 2.5 %collective-permute-start.7 = (bf16[4,128,384]{2,1,0:T(8,128)(2,1)}, bf16[4,128,384]{2,1,0:T(8,128)(2,1)}, u32[]{:S(2)}, u32[]{:S(2)}) collective-permute-start(bf16[4,128,384]{2,1,0:T(8,128)(2,1)} %collective-permute-done.3.refs_3_), channel_id=1, source_target_pairs={{0,48},{16,0},{32,16},{48,32},{1,49},{17,1},{33,17},{49,33},{2,50}... | collective-permute-start | bytes 1179656 | tf_op jit(solution)/shard_map/ppermute | solution.py:197
  57.1 2.6 %collective-permute-done.5.refs_5_ = bf16[4,128,384]{2,1,0:T(8,128)(2,1)} collective-permute-done((bf16[4,128,384]{2,1,0:T(8,128)(2,1)S(1)}, bf16[4,128,384]{2,1,0:T(8,128)(2,1)}, u32[]{:S(2)}, u32[]{:S(2)}) %collective-permute-start.5) | collective-permute-done | bytes 393248 | tf_op jit(solution)/shard_map/ppermute | solution.py:195
  59.7 3.6 %shard_map.65.state = f32[2,16,128,384]{3,2,1,0:T(8,128)S(1)} custom-call(s32[5]{0:T(128)S(1)} %stack.36.where, s32[2,64]{1,0:T(2,128)S(1)} %pad_add_fusion.slots, s32[2,64]{1,0:T(2,128)S(1)} %collective-permute-done.received, bf16[32,2,128,128]{3,2,1,0:T(8,128)(2,1)S(1)} %bitcast.26, bf16[32,2,128,128]{3,2,1,0:T(8,128)(2,1)} %collective-permute-done.1.other, ...), custom_call_target="tpu_custom_call" | custom-call | flops 603979776 | bytes 4194304 | tf_op jit(solution)/shard_map/pallas_call | solution.py:35
  63.2 2.3 %collective-permute-done.6.low = bf16[4,128,384]{2,1,0:T(8,128)(2,1)} collective-permute-done((bf16[4,128,384]{2,1,0:T(8,128)(2,1)S(1)}, bf16[4,128,384]{2,1,0:T(8,128)(2,1)}, u32[]{:S(2)}, u32[]{:S(2)}) %collective-permute-start.6) | collective-permute-done | bytes 393248 | tf_op jit(solution)/shard_map/ppermute | solution.py:196
  65.5 2.6 %collective-permute-done.7.high = bf16[4,128,384]{2,1,0:T(8,128)(2,1)} collective-permute-done((bf16[4,128,384]{2,1,0:T(8,128)(2,1)}, bf16[4,128,384]{2,1,0:T(8,128)(2,1)}, u32[]{:S(2)}, u32[]{:S(2)}) %collective-permute-start.7) | collective-permute-done | bytes 393248 | tf_op jit(solution)/shard_map/ppermute | solution.py:197
  68.1 2.4 %shard_map.66 = (f32[2,16,128,384]{3,2,1,0:T(8,128)S(1)}, bf16[8,128,384]{2,1,0:T(8,128)(2,1)S(1)}) custom-call(s32[5]{0:T(128)S(1)} %stack.36.where, s32[2,64]{1,0:T(2,128)S(1)} %pad_add_fusion.slots, s32[2,64]{1,0:T(2,128)S(1)} %collective-permute-done.received, bf16[8,4,2,128,128]{4,3,2,1,0:T(8,128)(2,1)S(1)} %bitcast.27, ...), custom_call_target="tpu_custom_call", output_to_operand_aliasing={{0}: (5, {})} | custom-call | flops 201326592 | bytes 4194304 | tf_op jit(solution)/shard_map/pallas_call | solution.py:35
  70.5 3.1 %collective-permute-start.8 = (bf16[8,128,384]{2,1,0:T(8,128)(2,1)S(1)}, bf16[8,128,384]{2,1,0:T(8,128)(2,1)S(1)}, u32[]{:S(2)}, u32[]{:S(2)}) collective-permute-start(bf16[8,128,384]{2,1,0:T(8,128)(2,1)S(1)} %get-tuple-element.10), channel_id=1, source_target_pairs={{0,8},{8,0},{1,9},{9,1},{2,10},{10,2},{3,11},{11,3},{4,12},{12,4},... | collective-permute-start | bytes 2359304 | tf_op jit(solution)/shard_map/ppermute | solution.py:208
  75.6 2.8 %copy-done = f32[2,16,128,384]{3,2,1,0:T(8,128)} copy-done((f32[2,16,128,384]{3,2,1,0:T(8,128)}, f32[2,16,128,384]{3,2,1,0:T(8,128)S(1)}, u32[]{:S(2)}) %copy-start) | copy-done | bytes 6291480
  79.4 6.8 %all-to-all-start = ((bf16[8,128,384]{2,1,0:T(8,128)(2,1)}), bf16[8,128,384]{2,1,0:T(8,128)(2,1)S(1)}, u32[]{:S(2)}, u32[]{:S(2)}) async-start(bf16[8,128,384]{2,1,0:T(8,128)(2,1)} %copy-done.4), calls=%async_computation | async-start | bytes 1572864 | tf_op jit(solution)/shard_map/all_to_all | solution.py:213
  86.2 2.6 %collective-permute-start.9 = (bf16[32,2,128,128]{3,2,1,0:T(8,128)(2,1)S(1)}, bf16[32,2,128,128]{3,2,1,0:T(8,128)(2,1)}, u32[]{:S(2)}, u32[]{:S(2)}) collective-permute-start(bf16[32,2,128,128]{3,2,1,0:T(8,128)(2,1)S(1)} %bitcast.22), channel_id=1, source_target_pairs={{0,8},{8,0},{1,9},{9,1},{2,10},{10,2},{3,11},{11,3},{4,12},{12,4},... | collective-permute-start | bytes 6291464 | tf_op jit(solution)/shard_map/ppermute | solution.py:208
  88.8 21.0 %all-to-all-done.parts = bf16[8,128,384]{2,1,0:T(8,128)(2,1)S(1)} async-done(((bf16[8,128,384]{2,1,0:T(8,128)(2,1)}), bf16[8,128,384]{2,1,0:T(8,128)(2,1)S(1)}, u32[]{:S(2)}, u32[]{:S(2)}) %all-to-all-start) | async-done | bytes 786464 | tf_op jit(solution)/shard_map/all_to_all | solution.py:213
  110.0 12.0 %all-gather.2 = bf16[512,384]{1,0:T(8,128)(2,1)S(1)} all-gather(bf16[128,384]{1,0:T(8,128)(2,1)S(1)} %shard_map.68), channel_id=4, replica_groups=mesh['zq'=4,'zp'=2,'x'=4,'core'=2,'y'=8] {'zq'}, dimensions={0}, use_global_device_ids=true | all-gather | bytes 491520 | tf_op jit(solution)/shard_map/all_gather | solution.py:184
  122.0 8.6 %all-gather.3 = bf16[8,128,384]{2,1,0:T(8,128)(2,1)S(1)} all-gather(bf16[4,128,384]{2,1,0:T(8,128)(2,1)S(1)} %bitcast.31), channel_id=5, replica_groups=mesh['zq'=4,'zp'=2,'x'=4,'core'=2,'y'=8] {'zp'}, dimensions={0}, use_global_device_ids=true | all-gather | bytes 1179648 | tf_op jit(solution)/shard_map/all_gather | solution.py:185
  130.7 4.5 %collective-permute-start.10 = (bf16[4,128,384]{2,1,0:T(8,128)(2,1)S(1)}, bf16[4,128,384]{2,1,0:T(8,128)(2,1)S(1)}, u32[]{:S(2)}, u32[]{:S(2)}) collective-permute-start(bf16[4,128,384]{2,1,0:T(8,128)(2,1)S(1)} %get-tuple-element.14.refs_0_), channel_id=1, source_target_pairs={{0,16},{16,32},{32,48},{48,0},{1,17},{17,33},{33,49},{49,1},{2,18}... | collective-permute-start | bytes 1179656 | tf_op jit(solution)/shard_map/ppermute | solution.py:192
  137.1 3.4 %collective-permute-start.12 = (bf16[4,128,384]{2,1,0:T(8,128)(2,1)S(1)}, bf16[4,128,384]{2,1,0:T(8,128)(2,1)S(1)}, u32[]{:S(2)}, u32[]{:S(2)}) collective-permute-start(bf16[4,128,384]{2,1,0:T(8,128)(2,1)S(1)} %get-tuple-element.13.refs_1_), channel_id=1, source_target_pairs={{0,16},{16,32},{32,48},{48,0},{1,17},{17,33},{33,49},{49,1},{2,18}... | collective-permute-start | bytes 1179656 | tf_op jit(solution)/shard_map/ppermute | solution.py:194
  142.4 3.4 %collective-permute-start.14 = (bf16[4,128,384]{2,1,0:T(8,128)(2,1)S(1)}, bf16[4,128,384]{2,1,0:T(8,128)(2,1)S(1)}, u32[]{:S(2)}, u32[]{:S(2)}) collective-permute-start(bf16[4,128,384]{2,1,0:T(8,128)(2,1)S(1)} %collective-permute-done.10.refs_2_), channel_id=1, source_target_pairs={{0,16},{16,32},{32,48},{48,0},{1,17},{17,33},{33,49},{49,1},{2,18}... | collective-permute-start | bytes 1179656 | tf_op jit(solution)/shard_map/ppermute | solution.py:196
  147.7 2.3 %collective-permute-done.12.refs_4_ = bf16[4,128,384]{2,1,0:T(8,128)(2,1)S(1)} collective-permute-done((bf16[4,128,384]{2,1,0:T(8,128)(2,1)S(1)}, bf16[4,128,384]{2,1,0:T(8,128)(2,1)S(1)}, u32[]{:S(2)}, u32[]{:S(2)}) %collective-permute-start.12) | collective-permute-done | bytes 393248 | tf_op jit(solution)/shard_map/ppermute | solution.py:194
  150.1 3.4 %collective-permute-done.13.refs_5_ = bf16[4,128,384]{2,1,0:T(8,128)(2,1)S(1)} collective-permute-done((bf16[4,128,384]{2,1,0:T(8,128)(2,1)S(1)}, bf16[4,128,384]{2,1,0:T(8,128)(2,1)S(1)}, u32[]{:S(2)}, u32[]{:S(2)}) %collective-permute-start.13) | collective-permute-done | bytes 393248 | tf_op jit(solution)/shard_map/ppermute | solution.py:195
  153.5 2.8 %copy-done.1 = f32[2,16,128,384]{3,2,1,0:T(8,128)S(1)} copy-done((f32[2,16,128,384]{3,2,1,0:T(8,128)S(1)}, f32[2,16,128,384]{3,2,1,0:T(8,128)}, u32[]{:S(2)}) %copy-start.1) | copy-done | bytes 6291480
  156.3 3.2 %shard_map.69.state = f32[2,8,128,384]{3,2,1,0:T(8,128)S(1)} custom-call(s32[5]{0:T(128)S(1)} %stack.36.where, s32[2,64]{1,0:T(2,128)S(1)} %pad_add_fusion.slots, s32[2,64]{1,0:T(2,128)S(1)} %collective-permute-done.received, bf16[32,2,128,128]{3,2,1,0:T(8,128)(2,1)S(1)} %bitcast.23, bf16[32,2,128,128]{3,2,1,0:T(8,128)(2,1)} %collective-permute-done.9.other, ...), custom_call_target="tpu_custom_call" | custom-call | flops 603979776 | bytes 4194304 | tf_op jit(solution)/shard_map/pallas_call | solution.py:35
  159.5 2.4 %collective-permute-done.15.high = bf16[4,128,384]{2,1,0:T(8,128)(2,1)S(1)} collective-permute-done((bf16[4,128,384]{2,1,0:T(8,128)(2,1)S(1)}, bf16[4,128,384]{2,1,0:T(8,128)(2,1)S(1)}, u32[]{:S(2)}, u32[]{:S(2)}) %collective-permute-start.15) | collective-permute-done | bytes 393248 | tf_op jit(solution)/shard_map/ppermute | solution.py:197
  164.1 7.7 %collective-permute-start.16 = (bf16[8,128,384]{2,1,0:T(8,128)(2,1)S(1)}, bf16[8,128,384]{2,1,0:T(8,128)(2,1)S(1)}, u32[]{:S(2)}, u32[]{:S(2)}) collective-permute-start(bf16[8,128,384]{2,1,0:T(8,128)(2,1)S(1)} %get-tuple-element.12), channel_id=1, source_target_pairs={{0,8},{8,0},{1,9},{9,1},{2,10},{10,2},{3,11},{11,3},{4,12},{12,4},... | collective-permute-start | bytes 2359304 | tf_op jit(solution)/shard_map/ppermute | solution.py:208
  173.9 26.0 %all_to_all.10.parts = bf16[8,128,384]{2,1,0:T(8,128)(2,1)S(1)} all-to-all(bf16[8,128,384]{2,1,0:T(8,128)(2,1)S(1)} %shard_map.71), channel_id=1, replica_groups=mesh['zq'=4,'zp'=2,'x'=4,'core'=2,'y'=8] {'y'}, dimensions={0} | all-to-all | bytes 1572864 | tf_op jit(solution)/shard_map/all_to_all | solution.py:213
  (43 shorter events, 18.2 us)
Async XLA Ops:
  0.0 59.6 %copy-start.3 = (bf16[1,64,1,128,128]{4,3,2,1,0:T(8,128)(2,1)S(1)}, bf16[1,64,1,128,128]{4,3,2,1,0:T(8,128)(2,1)}, u32[]{:S(2)}) copy-start(bf16[1,64,1,128,128]{4,3,2,1,0:T(8,128)(2,1)} %param.8) | copy-start | bytes 6291460
  0.0 39.3 %copy-start.9 = (s32[1,64,1]{1,2,0:T(1,128)S(1)}, s32[1,64,1]{1,2,0:T(1,128)}, u32[]{:S(2)}) copy-start(s32[1,64,1]{1,2,0:T(1,128)} %param.9) | copy-start | bytes 772
  0.0 39.3 %copy-start.8 = (s32[1,64,1]{1,2,0:T(1,128)S(1)}, s32[1,64,1]{1,2,0:T(1,128)}, u32[]{:S(2)}) copy-start(s32[1,64,1]{1,2,0:T(1,128)} %param.11) | copy-start | bytes 772
  0.0 59.6 %collective-permute-start.1 = (bf16[32,2,128,128]{3,2,1,0:T(8,128)(2,1)}, bf16[32,2,128,128]{3,2,1,0:T(8,128)(2,1)}, u32[]{:S(2)}, u32[]{:S(2)}) collective-permute-start(bf16[32,2,128,128]{3,2,1,0:T(8,128)(2,1)} %bitcast.25), channel_id=1, source_target_pairs={{0,8},{8,0},{1,9},{9,1},{2,10},{10,2},{3,11},{11,3},{4,12},{12,4},... | collective-permute-start | bytes 6291464 | tf_op jit(solution)/shard_map/ppermute | solution.py:208
  34.0 15.8 %collective-permute-start.2 = (bf16[4,128,384]{2,1,0:T(8,128)(2,1)S(1)}, bf16[4,128,384]{2,1,0:T(8,128)(2,1)S(1)}, u32[]{:S(2)}, u32[]{:S(2)}) collective-permute-start(bf16[4,128,384]{2,1,0:T(8,128)(2,1)S(1)} %get-tuple-element.16.refs_0_), channel_id=1, source_target_pairs={{0,16},{16,32},{32,48},{48,0},{1,17},{17,33},{33,49},{49,1},{2,18}... | collective-permute-start | bytes 1179656 | tf_op jit(solution)/shard_map/ppermute | solution.py:192
  36.8 15.8 %collective-permute-start.3 = (bf16[4,128,384]{2,1,0:T(8,128)(2,1)S(1)}, bf16[4,128,384]{2,1,0:T(8,128)(2,1)}, u32[]{:S(2)}, u32[]{:S(2)}) collective-permute-start(bf16[4,128,384]{2,1,0:T(8,128)(2,1)S(1)} %get-tuple-element.15.refs_1_), channel_id=1, source_target_pairs={{0,48},{16,0},{32,16},{48,32},{1,49},{17,1},{33,17},{49,33},{2,50}... | collective-permute-start | bytes 1179656 | tf_op jit(solution)/shard_map/ppermute | solution.py:193
  39.3 8.0 %collective-permute-start = (s32[2,64]{1,0:T(2,128)S(1)}, s32[2,64]{1,0:T(2,128)S(1)}, u32[]{:S(2)}, u32[]{:S(2)}) collective-permute-start(s32[2,64]{1,0:T(2,128)S(1)} %pad_add_fusion.slots), channel_id=1, source_target_pairs={{0,8},{8,0},{1,9},{9,1},{2,10},{10,2},{3,11},{11,3},{4,12},{12,4},... | collective-permute-start | bytes 1544 | tf_op jit(solution)/shard_map/ppermute | solution.py:208
  44.4 12.7 %collective-permute-start.4 = (bf16[4,128,384]{2,1,0:T(8,128)(2,1)S(1)}, bf16[4,128,384]{2,1,0:T(8,128)(2,1)}, u32[]{:S(2)}, u32[]{:S(2)}) collective-permute-start(bf16[4,128,384]{2,1,0:T(8,128)(2,1)S(1)} %get-tuple-element.15.refs_1_), channel_id=1, source_target_pairs={{0,16},{16,32},{32,48},{48,0},{1,17},{17,33},{33,49},{49,1},{2,18}... | collective-permute-start | bytes 1179656 | tf_op jit(solution)/shard_map/ppermute | solution.py:194
  47.3 12.4 %collective-permute-start.5 = (bf16[4,128,384]{2,1,0:T(8,128)(2,1)S(1)}, bf16[4,128,384]{2,1,0:T(8,128)(2,1)}, u32[]{:S(2)}, u32[]{:S(2)}) collective-permute-start(bf16[4,128,384]{2,1,0:T(8,128)(2,1)S(1)} %get-tuple-element.16.refs_0_), channel_id=1, source_target_pairs={{0,48},{16,0},{32,16},{48,32},{1,49},{17,1},{33,17},{49,33},{2,50}... | collective-permute-start | bytes 1179656 | tf_op jit(solution)/shard_map/ppermute | solution.py:195
  49.7 15.8 %collective-permute-start.6 = (bf16[4,128,384]{2,1,0:T(8,128)(2,1)S(1)}, bf16[4,128,384]{2,1,0:T(8,128)(2,1)}, u32[]{:S(2)}, u32[]{:S(2)}) collective-permute-start(bf16[4,128,384]{2,1,0:T(8,128)(2,1)S(1)} %collective-permute-done.2.refs_2_), channel_id=1, source_target_pairs={{0,16},{16,32},{32,48},{48,0},{1,17},{17,33},{33,49},{49,1},{2,18}... | collective-permute-start | bytes 1179656 | tf_op jit(solution)/shard_map/ppermute | solution.py:196
  52.6 15.5 %collective-permute-start.7 = (bf16[4,128,384]{2,1,0:T(8,128)(2,1)}, bf16[4,128,384]{2,1,0:T(8,128)(2,1)}, u32[]{:S(2)}, u32[]{:S(2)}) collective-permute-start(bf16[4,128,384]{2,1,0:T(8,128)(2,1)} %collective-permute-done.3.refs_3_), channel_id=1, source_target_pairs={{0,48},{16,0},{32,16},{48,32},{1,49},{17,1},{33,17},{49,33},{2,50}... | collective-permute-start | bytes 1179656 | tf_op jit(solution)/shard_map/ppermute | solution.py:197
  70.5 5.0 %collective-permute-start.8 = (bf16[8,128,384]{2,1,0:T(8,128)(2,1)S(1)}, bf16[8,128,384]{2,1,0:T(8,128)(2,1)S(1)}, u32[]{:S(2)}, u32[]{:S(2)}) collective-permute-start(bf16[8,128,384]{2,1,0:T(8,128)(2,1)S(1)} %get-tuple-element.10), channel_id=1, source_target_pairs={{0,8},{8,0},{1,9},{9,1},{2,10},{10,2},{3,11},{11,3},{4,12},{12,4},... | collective-permute-start | bytes 2359304 | tf_op jit(solution)/shard_map/ppermute | solution.py:208
  75.5 10.7 %copy-start.2 = (bf16[1,64,1,128,128]{4,3,2,1,0:T(8,128)(2,1)S(1)}, bf16[1,64,1,128,128]{4,3,2,1,0:T(8,128)(2,1)}, u32[]{:S(2)}) copy-start(bf16[1,64,1,128,128]{4,3,2,1,0:T(8,128)(2,1)} %param.10) | copy-start | bytes 6291460
  75.5 34.3 %copy-start.5 = (bf16[3,1,128,384]{3,2,1,0:T(8,128)(2,1)S(1)}, bf16[3,1,128,384]{3,2,1,0:T(8,128)(2,1)}, u32[]{:S(2)}) copy-start(bf16[3,1,128,384]{3,2,1,0:T(8,128)(2,1)} %right.5) | copy-start | bytes 884740
  75.5 34.3 %copy-start.6 = (bf16[3,1,128,128]{3,2,1,0:T(8,128)(2,1)S(1)}, bf16[3,1,128,128]{3,2,1,0:T(8,128)(2,1)}, u32[]{:S(2)}) copy-start(bf16[3,1,128,128]{3,2,1,0:T(8,128)(2,1)} %inverse.5) | copy-start | bytes 294916
  75.6 2.8 %copy-start = (f32[2,16,128,384]{3,2,1,0:T(8,128)}, f32[2,16,128,384]{3,2,1,0:T(8,128)S(1)}, u32[]{:S(2)}) copy-start(f32[2,16,128,384]{3,2,1,0:T(8,128)S(1)} %get-tuple-element.9.state.later) | copy-start | bytes 18874372
  78.4 1.0 copy-start.4
  79.4 30.4 %all-to-all-start = ((bf16[8,128,384]{2,1,0:T(8,128)(2,1)}), bf16[8,128,384]{2,1,0:T(8,128)(2,1)S(1)}, u32[]{:S(2)}, u32[]{:S(2)}) async-start(bf16[8,128,384]{2,1,0:T(8,128)(2,1)} %copy-done.4), calls=%async_computation | async-start | bytes 1572864 | tf_op jit(solution)/shard_map/all_to_all | solution.py:213
  86.2 61.5 %collective-permute-start.9 = (bf16[32,2,128,128]{3,2,1,0:T(8,128)(2,1)S(1)}, bf16[32,2,128,128]{3,2,1,0:T(8,128)(2,1)}, u32[]{:S(2)}, u32[]{:S(2)}) collective-permute-start(bf16[32,2,128,128]{3,2,1,0:T(8,128)(2,1)S(1)} %bitcast.22), channel_id=1, source_target_pairs={{0,8},{8,0},{1,9},{9,1},{2,10},{10,2},{3,11},{11,3},{4,12},{12,4},... | collective-permute-start | bytes 6291464 | tf_op jit(solution)/shard_map/ppermute | solution.py:208
  130.7 11.7 %collective-permute-start.10 = (bf16[4,128,384]{2,1,0:T(8,128)(2,1)S(1)}, bf16[4,128,384]{2,1,0:T(8,128)(2,1)S(1)}, u32[]{:S(2)}, u32[]{:S(2)}) collective-permute-start(bf16[4,128,384]{2,1,0:T(8,128)(2,1)S(1)} %get-tuple-element.14.refs_0_), channel_id=1, source_target_pairs={{0,16},{16,32},{32,48},{48,0},{1,17},{17,33},{33,49},{49,1},{2,18}... | collective-permute-start | bytes 1179656 | tf_op jit(solution)/shard_map/ppermute | solution.py:192
  135.2 10.6 %collective-permute-start.11 = (bf16[4,128,384]{2,1,0:T(8,128)(2,1)S(1)}, bf16[4,128,384]{2,1,0:T(8,128)(2,1)S(1)}, u32[]{:S(2)}, u32[]{:S(2)}) collective-permute-start(bf16[4,128,384]{2,1,0:T(8,128)(2,1)S(1)} %get-tuple-element.13.refs_1_), channel_id=1, source_target_pairs={{0,48},{16,0},{32,16},{48,32},{1,49},{17,1},{33,17},{49,33},{2,50}... | collective-permute-start | bytes 1179656 | tf_op jit(solution)/shard_map/ppermute | solution.py:193
  137.1 13.0 %collective-permute-start.12 = (bf16[4,128,384]{2,1,0:T(8,128)(2,1)S(1)}, bf16[4,128,384]{2,1,0:T(8,128)(2,1)S(1)}, u32[]{:S(2)}, u32[]{:S(2)}) collective-permute-start(bf16[4,128,384]{2,1,0:T(8,128)(2,1)S(1)} %get-tuple-element.13.refs_1_), channel_id=1, source_target_pairs={{0,16},{16,32},{32,48},{48,0},{1,17},{17,33},{33,49},{49,1},{2,18}... | collective-permute-start | bytes 1179656 | tf_op jit(solution)/shard_map/ppermute | solution.py:194
  140.5 13.0 %collective-permute-start.13 = (bf16[4,128,384]{2,1,0:T(8,128)(2,1)S(1)}, bf16[4,128,384]{2,1,0:T(8,128)(2,1)S(1)}, u32[]{:S(2)}, u32[]{:S(2)}) collective-permute-start(bf16[4,128,384]{2,1,0:T(8,128)(2,1)S(1)} %get-tuple-element.14.refs_0_), channel_id=1, source_target_pairs={{0,48},{16,0},{32,16},{48,32},{1,49},{17,1},{33,17},{49,33},{2,50}... | collective-permute-start | bytes 1179656 | tf_op jit(solution)/shard_map/ppermute | solution.py:195
  142.4 17.1 %collective-permute-start.14 = (bf16[4,128,384]{2,1,0:T(8,128)(2,1)S(1)}, bf16[4,128,384]{2,1,0:T(8,128)(2,1)S(1)}, u32[]{:S(2)}, u32[]{:S(2)}) collective-permute-start(bf16[4,128,384]{2,1,0:T(8,128)(2,1)S(1)} %collective-permute-done.10.refs_2_), channel_id=1, source_target_pairs={{0,16},{16,32},{32,48},{48,0},{1,17},{17,33},{33,49},{49,1},{2,18}... | collective-permute-start | bytes 1179656 | tf_op jit(solution)/shard_map/ppermute | solution.py:196
  145.8 16.1 %collective-permute-start.15 = (bf16[4,128,384]{2,1,0:T(8,128)(2,1)S(1)}, bf16[4,128,384]{2,1,0:T(8,128)(2,1)S(1)}, u32[]{:S(2)}, u32[]{:S(2)}) collective-permute-start(bf16[4,128,384]{2,1,0:T(8,128)(2,1)S(1)} %collective-permute-done.11.refs_3_), channel_id=1, source_target_pairs={{0,48},{16,0},{32,16},{48,32},{1,49},{17,1},{33,17},{49,33},{2,50}... | collective-permute-start | bytes 1179656 | tf_op jit(solution)/shard_map/ppermute | solution.py:197
  153.5 2.8 %copy-start.1 = (f32[2,16,128,384]{3,2,1,0:T(8,128)S(1)}, f32[2,16,128,384]{3,2,1,0:T(8,128)}, u32[]{:S(2)}) copy-start(f32[2,16,128,384]{3,2,1,0:T(8,128)} %copy-done) | copy-start | bytes 18874372
  164.1 9.6 %collective-permute-start.16 = (bf16[8,128,384]{2,1,0:T(8,128)(2,1)S(1)}, bf16[8,128,384]{2,1,0:T(8,128)(2,1)S(1)}, u32[]{:S(2)}, u32[]{:S(2)}) collective-permute-start(bf16[8,128,384]{2,1,0:T(8,128)(2,1)S(1)} %get-tuple-element.12), channel_id=1, source_target_pairs={{0,8},{8,0},{1,9},{9,1},{2,10},{10,2},{3,11},{11,3},{4,12},{12,4},... | collective-permute-start | bytes 2359304 | tf_op jit(solution)/shard_map/ppermute | solution.py:208
  173.7 26.4 %copy-start.7 = (bf16[128,384]{1,0:T(8,128)(2,1)S(1)}, bf16[128,384]{1,0:T(8,128)(2,1)}, u32[]{:S(2)}) copy-start(bf16[128,384]{1,0:T(8,128)(2,1)} %shard_map.64) | copy-start | bytes 294916

commit v4 on v3

--- a/solution.py
+++ b/solution.py
@@ -119,43 +119,43 @@
     )
 
 
-def late_body(level, where, slots, received, mine, other, state, low, high, out, near_other):
+def late_body(level, half, where, table, tiles, state, low, high, out, *near):
     del state
     core = where[NX]
     for piece, (base, side) in zip((low, high), FAR_SPOTS):
         for j in range(NQ):
             row = base + 2 * j
             entry = (row * NX + where[side]) * NC + core
-            pair = jnp.concatenate([mine[row, 0, 0], other[row, 0, 0]], axis=0)
-            product = jnp.dot(pair, piece[j], preferred_element_type=jnp.float32)
-            out[0, slots[level, entry]] += product[:TILE]
-            out[1, received[level, entry]] += product[TILE:]
-    near_other[...] = out[1, :NY].astype(jnp.bfloat16)
+            product = jnp.dot(tiles[row, 0, 0], piece[j], preferred_element_type=jnp.float32)
+            out[0, table[level, entry]] += product
+    if half:
+        near[0][...] = out[0, :NY].astype(jnp.bfloat16)
 
 
 def whole(shape):
     return pl.BlockSpec(shape, lambda i, where: (0,) * len(shape))
 
 
-def late(level, tables, mine, other, state, pieces):
+def late(level, half, where, table, tiles, state, pieces):
     by_place = (NQ * NP, NX, NC, TILE, TILE)
     column = pl.BlockSpec((NQ * NP, 1, 1, TILE, TILE), lambda i, where: (0, where[3], where[NX], 0, 0))
+    part = pl.BlockSpec((1,) + state.shape[1:], lambda i, where: (half, 0, 0, 0))
     slab = (NQ, TILE, COLS)
     grid_spec = pltpu.PrefetchScalarGridSpec(
         num_scalar_prefetch=1,
         grid=(1,),
-        in_specs=[smem()] * 2 + [column] * 2 + [whole(state.shape), whole(slab), whole(slab)],
-        out_specs=[whole(state.shape), whole((NY, TILE, COLS))],
+        in_specs=[smem(), column, part, whole(slab), whole(slab)],
+        out_specs=[part] + [whole((NY, TILE, COLS))] * half,
     )
     return call(
-        functools.partial(late_body, level),
-        [jax.ShapeDtypeStruct(state.shape, jnp.float32), block_shape(jnp.bfloat16, NY)],
+        functools.partial(late_body, level, half),
+        [jax.ShapeDtypeStruct(state.shape, jnp.float32)] + [block_shape(jnp.bfloat16, NY)] * half,
         None,
         None,
-        tables + (mine.reshape(by_place), other.reshape(by_place), state) + tuple(pieces),
-        8 * PAIR_FLOPS,
-        28,
-        aliases={5: 0},
+        (where, table, tiles.reshape(by_place), state) + tuple(pieces),
+        4 * PAIR_FLOPS,
+        20,
+        aliases={3: 0},
         grid_spec=grid_spec,
     )
 
@@ -208,9 +208,12 @@
     return lax.ppermute(value, "core", [(0, 1), (1, 0)])
 
 
-def reduce_rows(state, near_other):
-    received = swap(near_other)
-    return lax.all_to_all(join(state, received), "y", 0, 0, tiled=True)
+def reduce_rows(level, tables, mine, other, state, pieces):
+    where, slots, received = tables
+    state, near_other = late(level, 1, where, received, other, state, pieces)
+    near = swap(near_other)
+    (state,) = late(level, 0, where, slots, mine, state, pieces)
+    return state, lax.all_to_all(join(state, near), "y", 0, 0, tiled=True)
 
 
 def local(rhs, inverses, tiles_first, rows_first, tiles_second, rows_second):
@@ -218,22 +221,21 @@
     mine_first = tiles_first.reshape(CHIPS, NC, TILE, TILE)
     mine_second = tiles_second.reshape(CHIPS, NC, TILE, TILE)
 
-    other_first = swap(mine_first)
     level_zero = solve_zero(inverses, rhs)
     near, far = gather_columns(gather_rows(level_zero))
+    other_first = swap(mine_first)
     slots = jnp.concatenate([rows_first.reshape(1, CHIPS * NC), rows_second.reshape(1, CHIPS * NC)])
     received = swap(slots)
     tables = (where, slots, received)
     state = early(tables, mine_first, other_first, near)
-    state, near_other = late(0, tables, mine_first, other_first, state, far)
-    parts = reduce_rows(state, near_other)
+    state, parts = reduce_rows(0, tables, mine_first, other_first, state, far)
 
     level_one = solve_next(1, inverses, rhs, parts)
     near, far = gather_columns(gather_rows(level_one))
     other_second = swap(mine_second)
     state = early(tables, mine_second, other_second, near, state)
-    state, near_other = late(1, tables, mine_second, other_second, state, far)
-    level_two = solve_next(2, inverses, rhs, reduce_rows(state, near_other))
+    state, parts = reduce_rows(1, tables, mine_second, other_second, state, far)
+    level_two = solve_next(2, inverses, rhs, parts)
     return jnp.stack([level_zero, level_one, level_two])[:, None]
 
 

time: 202 us -> 201 us (level)
  waiting for transfers between devices: 42.3 us -> 39 us
  Pallas kernels: 13.9 us -> 16.8 us
    ppermute x5, waiting for transfers between devices: 3.79 us -> 0.42 us  [swap(): return lax.ppermute(value, 'core', [(0, 1), (1, 0)])]
    pallas_call x9 -> x11, Pallas kernels: 13.9 us -> 16.8 us  [call(): pl.pallas_call(body, out_shape=out_shape, input_output_aliases=aliases or...]
  transfers between devices with their start and end apart: 18 -> 18, of which waited for: 10 -> 9; matrix products, arithmetic and copies ran while one was open for 0% -> 0% of each run, Pallas kernels for 4% -> 6%
where the time goes in v4:
time: 201 us; the launch traced here: 200 us
  blocking collectives  76 us (38%)
  starting transfers between devices  60.6 us (30%)
  waiting for transfers between devices  39 us (19%)
  Pallas kernels  16.8 us (8%)
  local copies, waits for them, and re-layouts  6.7 us (3%)
    all_gather x2, blocking collectives, gather_rows(): even_odd = lax.all_gather(block[None], 'zq', axis=0, tiled=True)  30.7 us
    all_to_all x1, blocking collectives, reduce_rows(): return (state, lax.all_to_all(join(state, near), 'y', 0, 0, tiled=True))  26 us
    all_to_all x1, waiting for transfers between devices, reduce_rows(): return (state, lax.all_to_all(join(state, near), 'y', 0, 0, tiled=True))  21.1 us
    ppermute x5, starting transfers between devices, swap(): return lax.ppermute(value, 'core', [(0, 1), (1, 0)])  21 us
    all_gather x2, blocking collectives, gather_rows(): return lax.all_gather(even_odd[None], 'zp', axis=0, tiled=True)  19.3 us
    pallas_call x11, Pallas kernels, call(): pl.pallas_call(body, out_shape=out_shape, input_output_aliases=aliases or...  16.8 us
    ppermute x2, starting transfers between devices, gather_columns(): low_left = up(low)  7.34 us
    all_to_all x1, starting transfers between devices, reduce_rows(): return (state, lax.all_to_all(join(state, near), 'y', 0, 0, tiled=True))  6.82 us
  transfers between devices with their start and end apart: 18, of which 9 were waited for; matrix products, arithmetic and copies ran while one was open for 0% of the time, Pallas kernels for 6%

profile of v4, /device:TPU:5, one launch (start us, length us, event | category | flops | bytes accessed | tf_op | source)
XLA Modules:
  0.0 200.3 jit_solution(7095773550749536730)
XLA Ops:
  0.0 2.7 %collective-permute-start.1 = (bf16[32,2,128,128]{3,2,1,0:T(8,128)(2,1)}, bf16[32,2,128,128]{3,2,1,0:T(8,128)(2,1)}, u32[]{:S(2)}, u32[]{:S(2)}) collective-permute-start(bf16[32,2,128,128]{3,2,1,0:T(8,128)(2,1)} %bitcast.25), channel_id=1, source_target_pairs={{0,8},{8,0},{1,9},{9,1},{2,10},{10,2},{3,11},{11,3},{4,12},{12,4},... | collective-permute-start | bytes 6291464 | tf_op jit(solution)/shard_map/ppermute | solution.py:208
  4.5 18.7 %all-gather = bf16[512,384]{1,0:T(8,128)(2,1)S(1)} all-gather(bf16[128,384]{1,0:T(8,128)(2,1)} %shard_map.64), channel_id=2, replica_groups=mesh['zq'=4,'zp'=2,'x'=4,'core'=2,'y'=8] {'zq'}, dimensions={0}, use_global_device_ids=true | all-gather | bytes 491520 | tf_op jit(solution)/shard_map/all_gather | solution.py:184
  23.2 10.7 %all-gather.1 = bf16[8,128,384]{2,1,0:T(8,128)(2,1)S(1)} all-gather(bf16[4,128,384]{2,1,0:T(8,128)(2,1)S(1)} %bitcast.30), channel_id=3, replica_groups=mesh['zq'=4,'zp'=2,'x'=4,'core'=2,'y'=8] {'zp'}, dimensions={0}, use_global_device_ids=true | all-gather | bytes 1179648 | tf_op jit(solution)/shard_map/all_gather | solution.py:185
  34.0 2.8 %collective-permute-start.2 = (bf16[4,128,384]{2,1,0:T(8,128)(2,1)S(1)}, bf16[4,128,384]{2,1,0:T(8,128)(2,1)}, u32[]{:S(2)}, u32[]{:S(2)}) collective-permute-start(bf16[4,128,384]{2,1,0:T(8,128)(2,1)S(1)} %get-tuple-element.16.refs_0_), channel_id=1, source_target_pairs={{0,16},{16,32},{32,48},{48,0},{1,17},{17,33},{33,49},{49,1},{2,18}... | collective-permute-start | bytes 1179656 | tf_op jit(solution)/shard_map/ppermute | solution.py:192
  36.8 2.5 %collective-permute-start.3 = (bf16[4,128,384]{2,1,0:T(8,128)(2,1)S(1)}, bf16[4,128,384]{2,1,0:T(8,128)(2,1)}, u32[]{:S(2)}, u32[]{:S(2)}) collective-permute-start(bf16[4,128,384]{2,1,0:T(8,128)(2,1)S(1)} %get-tuple-element.15.refs_1_), channel_id=1, source_target_pairs={{0,48},{16,0},{32,16},{48,32},{1,49},{17,1},{33,17},{49,33},{2,50}... | collective-permute-start | bytes 1179656 | tf_op jit(solution)/shard_map/ppermute | solution.py:193
  39.3 5.1 %collective-permute-start = (s32[2,64]{1,0:T(2,128)S(1)}, s32[2,64]{1,0:T(2,128)S(1)}, u32[]{:S(2)}, u32[]{:S(2)}) collective-permute-start(s32[2,64]{1,0:T(2,128)S(1)} %pad_add_fusion.slots.table), channel_id=1, source_target_pairs={{0,8},{8,0},{1,9},{9,1},{2,10},{10,2},{3,11},{11,3},{4,12},{12,4},... | collective-permute-start | bytes 1544 | tf_op jit(solution)/shard_map/ppermute | solution.py:208
  44.4 2.8 %collective-permute-start.4 = (bf16[4,128,384]{2,1,0:T(8,128)(2,1)S(1)}, bf16[4,128,384]{2,1,0:T(8,128)(2,1)}, u32[]{:S(2)}, u32[]{:S(2)}) collective-permute-start(bf16[4,128,384]{2,1,0:T(8,128)(2,1)S(1)} %get-tuple-element.15.refs_1_), channel_id=1, source_target_pairs={{0,16},{16,32},{32,48},{48,0},{1,17},{17,33},{33,49},{49,1},{2,18}... | collective-permute-start | bytes 1179656 | tf_op jit(solution)/shard_map/ppermute | solution.py:194
  47.3 2.5 %collective-permute-start.5 = (bf16[4,128,384]{2,1,0:T(8,128)(2,1)S(1)}, bf16[4,128,384]{2,1,0:T(8,128)(2,1)}, u32[]{:S(2)}, u32[]{:S(2)}) collective-permute-start(bf16[4,128,384]{2,1,0:T(8,128)(2,1)S(1)} %get-tuple-element.16.refs_0_), channel_id=1, source_target_pairs={{0,48},{16,0},{32,16},{48,32},{1,49},{17,1},{33,17},{49,33},{2,50}... | collective-permute-start | bytes 1179656 | tf_op jit(solution)/shard_map/ppermute | solution.py:195
  49.7 2.8 %collective-permute-start.6 = (bf16[4,128,384]{2,1,0:T(8,128)(2,1)}, bf16[4,128,384]{2,1,0:T(8,128)(2,1)S(1)}, u32[]{:S(2)}, u32[]{:S(2)}) collective-permute-start(bf16[4,128,384]{2,1,0:T(8,128)(2,1)} %collective-permute-done.2.refs_2_), channel_id=1, source_target_pairs={{0,16},{16,32},{32,48},{48,0},{1,17},{17,33},{33,49},{49,1},{2,18}... | collective-permute-start | bytes 1179656 | tf_op jit(solution)/shard_map/ppermute | solution.py:196
  52.6 2.5 %collective-permute-start.7 = (bf16[4,128,384]{2,1,0:T(8,128)(2,1)}, bf16[4,128,384]{2,1,0:T(8,128)(2,1)}, u32[]{:S(2)}, u32[]{:S(2)}) collective-permute-start(bf16[4,128,384]{2,1,0:T(8,128)(2,1)} %collective-permute-done.3.refs_3_), channel_id=1, source_target_pairs={{0,48},{16,0},{32,16},{48,32},{1,49},{17,1},{33,17},{49,33},{2,50}... | collective-permute-start | bytes 1179656 | tf_op jit(solution)/shard_map/ppermute | solution.py:197
  57.1 2.6 %collective-permute-done.5.refs_5_ = bf16[4,128,384]{2,1,0:T(8,128)(2,1)} collective-permute-done((bf16[4,128,384]{2,1,0:T(8,128)(2,1)S(1)}, bf16[4,128,384]{2,1,0:T(8,128)(2,1)}, u32[]{:S(2)}, u32[]{:S(2)}) %collective-permute-start.5) | collective-permute-done | bytes 393248 | tf_op jit(solution)/shard_map/ppermute | solution.py:195
  59.7 3.7 %shard_map.65.state = f32[2,16,128,384]{3,2,1,0:T(8,128)S(1)} custom-call(s32[5]{0:T(128)S(1)} %stack.36.where, s32[2,64]{1,0:T(2,128)S(1)} %pad_add_fusion.slots.table, s32[2,64]{1,0:T(2,128)S(1)} %collective-permute-done.received.table, bf16[32,2,128,128]{3,2,1,0:T(8,128)(2,1)S(1)} %bitcast.26, bf16[32,2,128,128]{3,2,1,0:T(8,128)(2,1)} %collective-permute-done.1.other, ...), custom_call_target="tpu_custom_call" | custom-call | flops 603979776 | bytes 4194304 | tf_op jit(solution)/shard_map/pallas_call | solution.py:35
  63.3 2.2 %collective-permute-done.6.low = bf16[4,128,384]{2,1,0:T(8,128)(2,1)S(1)} collective-permute-done((bf16[4,128,384]{2,1,0:T(8,128)(2,1)}, bf16[4,128,384]{2,1,0:T(8,128)(2,1)S(1)}, u32[]{:S(2)}, u32[]{:S(2)}) %collective-permute-start.6) | collective-permute-done | bytes 393248 | tf_op jit(solution)/shard_map/ppermute | solution.py:196
  65.5 2.6 %collective-permute-done.7.high = bf16[4,128,384]{2,1,0:T(8,128)(2,1)} collective-permute-done((bf16[4,128,384]{2,1,0:T(8,128)(2,1)}, bf16[4,128,384]{2,1,0:T(8,128)(2,1)}, u32[]{:S(2)}, u32[]{:S(2)}) %collective-permute-start.7) | collective-permute-done | bytes 393248 | tf_op jit(solution)/shard_map/ppermute | solution.py:197
  68.1 2.1 %shard_map.66 = (f32[2,16,128,384]{3,2,1,0:T(8,128)S(1)}, bf16[8,128,384]{2,1,0:T(8,128)(2,1)S(1)}) custom-call(s32[5]{0:T(128)S(1)} %stack.36.where, s32[2,64]{1,0:T(2,128)S(1)} %collective-permute-done.received.table, bf16[8,4,2,128,128]{4,3,2,1,0:T(8,128)(2,1)} %bitcast.10.tiles, ...), custom_call_target="tpu_custom_call", output_to_operand_aliasing={{0}: (3, {})} | custom-call | flops 100663296 | bytes 4194304 | tf_op jit(solution)/shard_map/pallas_call | solution.py:35
  70.2 3.1 %collective-permute-start.8 = (bf16[8,128,384]{2,1,0:T(8,128)(2,1)S(1)}, bf16[8,128,384]{2,1,0:T(8,128)(2,1)S(1)}, u32[]{:S(2)}, u32[]{:S(2)}) collective-permute-start(bf16[8,128,384]{2,1,0:T(8,128)(2,1)S(1)} %get-tuple-element.10), channel_id=1, source_target_pairs={{0,8},{8,0},{1,9},{9,1},{2,10},{10,2},{3,11},{11,3},{4,12},{12,4},... | collective-permute-start | bytes 2359304 | tf_op jit(solution)/shard_map/ppermute | solution.py:208
  75.4 2.7 %copy-done = f32[2,16,128,384]{3,2,1,0:T(8,128)} copy-done((f32[2,16,128,384]{3,2,1,0:T(8,128)}, f32[2,16,128,384]{3,2,1,0:T(8,128)S(1)}, u32[]{:S(2)}) %copy-start) | copy-done | bytes 6291480
  79.0 6.8 %all-to-all-start = ((bf16[8,128,384]{2,1,0:T(8,128)(2,1)}), bf16[8,128,384]{2,1,0:T(8,128)(2,1)S(1)}, u32[]{:S(2)}, u32[]{:S(2)}) async-start(bf16[8,128,384]{2,1,0:T(8,128)(2,1)} %copy-done.4), calls=%async_computation | async-start | bytes 1572864 | tf_op jit(solution)/shard_map/all_to_all | solution.py:216
  85.9 2.4 %collective-permute-start.9 = (bf16[32,2,128,128]{3,2,1,0:T(8,128)(2,1)S(1)}, bf16[32,2,128,128]{3,2,1,0:T(8,128)(2,1)}, u32[]{:S(2)}, u32[]{:S(2)}) collective-permute-start(bf16[32,2,128,128]{3,2,1,0:T(8,128)(2,1)S(1)} %bitcast.22), channel_id=1, source_target_pairs={{0,8},{8,0},{1,9},{9,1},{2,10},{10,2},{3,11},{11,3},{4,12},{12,4},... | collective-permute-start | bytes 6291464 | tf_op jit(solution)/shard_map/ppermute | solution.py:208
  88.3 21.1 %all-to-all-done.parts = bf16[8,128,384]{2,1,0:T(8,128)(2,1)S(1)} async-done(((bf16[8,128,384]{2,1,0:T(8,128)(2,1)}), bf16[8,128,384]{2,1,0:T(8,128)(2,1)S(1)}, u32[]{:S(2)}, u32[]{:S(2)}) %all-to-all-start) | async-done | bytes 786464 | tf_op jit(solution)/shard_map/all_to_all | solution.py:216
  109.7 12.0 %all-gather.2 = bf16[512,384]{1,0:T(8,128)(2,1)S(1)} all-gather(bf16[128,384]{1,0:T(8,128)(2,1)S(1)} %shard_map.69), channel_id=4, replica_groups=mesh['zq'=4,'zp'=2,'x'=4,'core'=2,'y'=8] {'zq'}, dimensions={0}, use_global_device_ids=true | all-gather | bytes 491520 | tf_op jit(solution)/shard_map/all_gather | solution.py:184
  121.7 8.6 %all-gather.3 = bf16[8,128,384]{2,1,0:T(8,128)(2,1)S(1)} all-gather(bf16[4,128,384]{2,1,0:T(8,128)(2,1)S(1)} %bitcast.31), channel_id=5, replica_groups=mesh['zq'=4,'zp'=2,'x'=4,'core'=2,'y'=8] {'zp'}, dimensions={0}, use_global_device_ids=true | all-gather | bytes 1179648 | tf_op jit(solution)/shard_map/all_gather | solution.py:185
  130.4 4.5 %collective-permute-start.10 = (bf16[4,128,384]{2,1,0:T(8,128)(2,1)S(1)}, bf16[4,128,384]{2,1,0:T(8,128)(2,1)S(1)}, u32[]{:S(2)}, u32[]{:S(2)}) collective-permute-start(bf16[4,128,384]{2,1,0:T(8,128)(2,1)S(1)} %get-tuple-element.14.refs_0_), channel_id=1, source_target_pairs={{0,16},{16,32},{32,48},{48,0},{1,17},{17,33},{33,49},{49,1},{2,18}... | collective-permute-start | bytes 1179656 | tf_op jit(solution)/shard_map/ppermute | solution.py:192
  136.8 3.4 %collective-permute-start.12 = (bf16[4,128,384]{2,1,0:T(8,128)(2,1)S(1)}, bf16[4,128,384]{2,1,0:T(8,128)(2,1)S(1)}, u32[]{:S(2)}, u32[]{:S(2)}) collective-permute-start(bf16[4,128,384]{2,1,0:T(8,128)(2,1)S(1)} %get-tuple-element.13.refs_1_), channel_id=1, source_target_pairs={{0,16},{16,32},{32,48},{48,0},{1,17},{17,33},{33,49},{49,1},{2,18}... | collective-permute-start | bytes 1179656 | tf_op jit(solution)/shard_map/ppermute | solution.py:194
  142.1 3.4 %collective-permute-start.14 = (bf16[4,128,384]{2,1,0:T(8,128)(2,1)S(1)}, bf16[4,128,384]{2,1,0:T(8,128)(2,1)S(1)}, u32[]{:S(2)}, u32[]{:S(2)}) collective-permute-start(bf16[4,128,384]{2,1,0:T(8,128)(2,1)S(1)} %collective-permute-done.10.refs_2_), channel_id=1, source_target_pairs={{0,16},{16,32},{32,48},{48,0},{1,17},{17,33},{33,49},{49,1},{2,18}... | collective-permute-start | bytes 1179656 | tf_op jit(solution)/shard_map/ppermute | solution.py:196
  147.5 2.3 %collective-permute-done.12.refs_4_ = bf16[4,128,384]{2,1,0:T(8,128)(2,1)S(1)} collective-permute-done((bf16[4,128,384]{2,1,0:T(8,128)(2,1)S(1)}, bf16[4,128,384]{2,1,0:T(8,128)(2,1)S(1)}, u32[]{:S(2)}, u32[]{:S(2)}) %collective-permute-start.12) | collective-permute-done | bytes 393248 | tf_op jit(solution)/shard_map/ppermute | solution.py:194
  149.7 3.5 %collective-permute-done.13.refs_5_ = bf16[4,128,384]{2,1,0:T(8,128)(2,1)S(1)} collective-permute-done((bf16[4,128,384]{2,1,0:T(8,128)(2,1)S(1)}, bf16[4,128,384]{2,1,0:T(8,128)(2,1)S(1)}, u32[]{:S(2)}, u32[]{:S(2)}) %collective-permute-start.13) | collective-permute-done | bytes 393248 | tf_op jit(solution)/shard_map/ppermute | solution.py:195
  153.2 2.8 %copy-done.1 = f32[2,16,128,384]{3,2,1,0:T(8,128)S(1)} copy-done((f32[2,16,128,384]{3,2,1,0:T(8,128)S(1)}, f32[2,16,128,384]{3,2,1,0:T(8,128)}, u32[]{:S(2)}) %copy-start.1) | copy-done | bytes 6291480
  156.0 3.2 %shard_map.70.state = f32[2,8,128,384]{3,2,1,0:T(8,128)S(1)} custom-call(s32[5]{0:T(128)S(1)} %stack.36.where, s32[2,64]{1,0:T(2,128)S(1)} %pad_add_fusion.slots.table, s32[2,64]{1,0:T(2,128)S(1)} %collective-permute-done.received.table, bf16[32,2,128,128]{3,2,1,0:T(8,128)(2,1)S(1)} %bitcast.23, bf16[32,2,128,128]{3,2,1,0:T(8,128)(2,1)} %collective-permute-done.9.other, ...), custom_call_target="tpu_custom_call" | custom-call | flops 603979776 | bytes 4194304 | tf_op jit(solution)/shard_map/pallas_call | solution.py:35
  159.2 2.4 %collective-permute-done.15.high = bf16[4,128,384]{2,1,0:T(8,128)(2,1)S(1)} collective-permute-done((bf16[4,128,384]{2,1,0:T(8,128)(2,1)S(1)}, bf16[4,128,384]{2,1,0:T(8,128)(2,1)S(1)}, u32[]{:S(2)}, u32[]{:S(2)}) %collective-permute-start.15) | collective-permute-done | bytes 393248 | tf_op jit(solution)/shard_map/ppermute | solution.py:197
  163.6 7.6 %collective-permute-start.16 = (bf16[8,128,384]{2,1,0:T(8,128)(2,1)S(1)}, bf16[8,128,384]{2,1,0:T(8,128)(2,1)S(1)}, u32[]{:S(2)}, u32[]{:S(2)}) collective-permute-start(bf16[8,128,384]{2,1,0:T(8,128)(2,1)S(1)} %get-tuple-element.12), channel_id=1, source_target_pairs={{0,8},{8,0},{1,9},{9,1},{2,10},{10,2},{3,11},{11,3},{4,12},{12,4},... | collective-permute-start | bytes 2359304 | tf_op jit(solution)/shard_map/ppermute | solution.py:208
  173.3 26.0 %all_to_all.10.parts = bf16[8,128,384]{2,1,0:T(8,128)(2,1)S(1)} all-to-all(bf16[8,128,384]{2,1,0:T(8,128)(2,1)S(1)} %shard_map.73), channel_id=1, replica_groups=mesh['zq'=4,'zp'=2,'x'=4,'core'=2,'y'=8] {'y'}, dimensions={0} | all-to-all | bytes 1572864 | tf_op jit(solution)/shard_map/all_to_all | solution.py:216
  (45 shorter events, 18.0 us)
Async XLA Ops:
  0.0 59.7 %copy-start.3 = (bf16[1,64,1,128,128]{4,3,2,1,0:T(8,128)(2,1)S(1)}, bf16[1,64,1,128,128]{4,3,2,1,0:T(8,128)(2,1)}, u32[]{:S(2)}) copy-start(bf16[1,64,1,128,128]{4,3,2,1,0:T(8,128)(2,1)} %param.8) | copy-start | bytes 6291460
  0.0 39.3 %copy-start.9 = (s32[1,64,1]{1,2,0:T(1,128)S(1)}, s32[1,64,1]{1,2,0:T(1,128)}, u32[]{:S(2)}) copy-start(s32[1,64,1]{1,2,0:T(1,128)} %param.9) | copy-start | bytes 772
  0.0 39.3 %copy-start.8 = (s32[1,64,1]{1,2,0:T(1,128)S(1)}, s32[1,64,1]{1,2,0:T(1,128)}, u32[]{:S(2)}) copy-start(s32[1,64,1]{1,2,0:T(1,128)} %param.11) | copy-start | bytes 772
  0.0 59.6 %collective-permute-start.1 = (bf16[32,2,128,128]{3,2,1,0:T(8,128)(2,1)}, bf16[32,2,128,128]{3,2,1,0:T(8,128)(2,1)}, u32[]{:S(2)}, u32[]{:S(2)}) collective-permute-start(bf16[32,2,128,128]{3,2,1,0:T(8,128)(2,1)} %bitcast.25), channel_id=1, source_target_pairs={{0,8},{8,0},{1,9},{9,1},{2,10},{10,2},{3,11},{11,3},{4,12},{12,4},... | collective-permute-start | bytes 6291464 | tf_op jit(solution)/shard_map/ppermute | solution.py:208
  34.0 15.8 %collective-permute-start.2 = (bf16[4,128,384]{2,1,0:T(8,128)(2,1)S(1)}, bf16[4,128,384]{2,1,0:T(8,128)(2,1)}, u32[]{:S(2)}, u32[]{:S(2)}) collective-permute-start(bf16[4,128,384]{2,1,0:T(8,128)(2,1)S(1)} %get-tuple-element.16.refs_0_), channel_id=1, source_target_pairs={{0,16},{16,32},{32,48},{48,0},{1,17},{17,33},{33,49},{49,1},{2,18}... | collective-permute-start | bytes 1179656 | tf_op jit(solution)/shard_map/ppermute | solution.py:192
  36.8 15.8 %collective-permute-start.3 = (bf16[4,128,384]{2,1,0:T(8,128)(2,1)S(1)}, bf16[4,128,384]{2,1,0:T(8,128)(2,1)}, u32[]{:S(2)}, u32[]{:S(2)}) collective-permute-start(bf16[4,128,384]{2,1,0:T(8,128)(2,1)S(1)} %get-tuple-element.15.refs_1_), channel_id=1, source_target_pairs={{0,48},{16,0},{32,16},{48,32},{1,49},{17,1},{33,17},{49,33},{2,50}... | collective-permute-start | bytes 1179656 | tf_op jit(solution)/shard_map/ppermute | solution.py:193
  39.3 8.0 %collective-permute-start = (s32[2,64]{1,0:T(2,128)S(1)}, s32[2,64]{1,0:T(2,128)S(1)}, u32[]{:S(2)}, u32[]{:S(2)}) collective-permute-start(s32[2,64]{1,0:T(2,128)S(1)} %pad_add_fusion.slots.table), channel_id=1, source_target_pairs={{0,8},{8,0},{1,9},{9,1},{2,10},{10,2},{3,11},{11,3},{4,12},{12,4},... | collective-permute-start | bytes 1544 | tf_op jit(solution)/shard_map/ppermute | solution.py:208
  44.4 12.7 %collective-permute-start.4 = (bf16[4,128,384]{2,1,0:T(8,128)(2,1)S(1)}, bf16[4,128,384]{2,1,0:T(8,128)(2,1)}, u32[]{:S(2)}, u32[]{:S(2)}) collective-permute-start(bf16[4,128,384]{2,1,0:T(8,128)(2,1)S(1)} %get-tuple-element.15.refs_1_), channel_id=1, source_target_pairs={{0,16},{16,32},{32,48},{48,0},{1,17},{17,33},{33,49},{49,1},{2,18}... | collective-permute-start | bytes 1179656 | tf_op jit(solution)/shard_map/ppermute | solution.py:194
  47.3 12.4 %collective-permute-start.5 = (bf16[4,128,384]{2,1,0:T(8,128)(2,1)S(1)}, bf16[4,128,384]{2,1,0:T(8,128)(2,1)}, u32[]{:S(2)}, u32[]{:S(2)}) collective-permute-start(bf16[4,128,384]{2,1,0:T(8,128)(2,1)S(1)} %get-tuple-element.16.refs_0_), channel_id=1, source_target_pairs={{0,48},{16,0},{32,16},{48,32},{1,49},{17,1},{33,17},{49,33},{2,50}... | collective-permute-start | bytes 1179656 | tf_op jit(solution)/shard_map/ppermute | solution.py:195
  49.7 15.8 %collective-permute-start.6 = (bf16[4,128,384]{2,1,0:T(8,128)(2,1)}, bf16[4,128,384]{2,1,0:T(8,128)(2,1)S(1)}, u32[]{:S(2)}, u32[]{:S(2)}) collective-permute-start(bf16[4,128,384]{2,1,0:T(8,128)(2,1)} %collective-permute-done.2.refs_2_), channel_id=1, source_target_pairs={{0,16},{16,32},{32,48},{48,0},{1,17},{17,33},{33,49},{49,1},{2,18}... | collective-permute-start | bytes 1179656 | tf_op jit(solution)/shard_map/ppermute | solution.py:196
  52.6 15.5 %collective-permute-start.7 = (bf16[4,128,384]{2,1,0:T(8,128)(2,1)}, bf16[4,128,384]{2,1,0:T(8,128)(2,1)}, u32[]{:S(2)}, u32[]{:S(2)}) collective-permute-start(bf16[4,128,384]{2,1,0:T(8,128)(2,1)} %collective-permute-done.3.refs_3_), channel_id=1, source_target_pairs={{0,48},{16,0},{32,16},{48,32},{1,49},{17,1},{33,17},{49,33},{2,50}... | collective-permute-start | bytes 1179656 | tf_op jit(solution)/shard_map/ppermute | solution.py:197
  70.2 5.0 %collective-permute-start.8 = (bf16[8,128,384]{2,1,0:T(8,128)(2,1)S(1)}, bf16[8,128,384]{2,1,0:T(8,128)(2,1)S(1)}, u32[]{:S(2)}, u32[]{:S(2)}) collective-permute-start(bf16[8,128,384]{2,1,0:T(8,128)(2,1)S(1)} %get-tuple-element.10), channel_id=1, source_target_pairs={{0,8},{8,0},{1,9},{9,1},{2,10},{10,2},{3,11},{11,3},{4,12},{12,4},... | collective-permute-start | bytes 2359304 | tf_op jit(solution)/shard_map/ppermute | solution.py:208
  75.1 10.7 %copy-start.2 = (bf16[1,64,1,128,128]{4,3,2,1,0:T(8,128)(2,1)S(1)}, bf16[1,64,1,128,128]{4,3,2,1,0:T(8,128)(2,1)}, u32[]{:S(2)}) copy-start(bf16[1,64,1,128,128]{4,3,2,1,0:T(8,128)(2,1)} %param.10) | copy-start | bytes 6291460
  75.2 34.3 %copy-start.5 = (bf16[3,1,128,384]{3,2,1,0:T(8,128)(2,1)S(1)}, bf16[3,1,128,384]{3,2,1,0:T(8,128)(2,1)}, u32[]{:S(2)}) copy-start(bf16[3,1,128,384]{3,2,1,0:T(8,128)(2,1)} %right.5) | copy-start | bytes 884740
  75.2 34.3 %copy-start.6 = (bf16[3,1,128,128]{3,2,1,0:T(8,128)(2,1)S(1)}, bf16[3,1,128,128]{3,2,1,0:T(8,128)(2,1)}, u32[]{:S(2)}) copy-start(bf16[3,1,128,128]{3,2,1,0:T(8,128)(2,1)} %inverse.5) | copy-start | bytes 294916
  75.4 2.7 %copy-start = (f32[2,16,128,384]{3,2,1,0:T(8,128)}, f32[2,16,128,384]{3,2,1,0:T(8,128)S(1)}, u32[]{:S(2)}) copy-start(f32[2,16,128,384]{3,2,1,0:T(8,128)S(1)} %shard_map.67.state.later) | copy-start | bytes 18874372
  78.1 1.0 copy-start.4
  79.0 30.4 %all-to-all-start = ((bf16[8,128,384]{2,1,0:T(8,128)(2,1)}), bf16[8,128,384]{2,1,0:T(8,128)(2,1)S(1)}, u32[]{:S(2)}, u32[]{:S(2)}) async-start(bf16[8,128,384]{2,1,0:T(8,128)(2,1)} %copy-done.4), calls=%async_computation | async-start | bytes 1572864 | tf_op jit(solution)/shard_map/all_to_all | solution.py:216
  85.9 61.6 %collective-permute-start.9 = (bf16[32,2,128,128]{3,2,1,0:T(8,128)(2,1)S(1)}, bf16[32,2,128,128]{3,2,1,0:T(8,128)(2,1)}, u32[]{:S(2)}, u32[]{:S(2)}) collective-permute-start(bf16[32,2,128,128]{3,2,1,0:T(8,128)(2,1)S(1)} %bitcast.22), channel_id=1, source_target_pairs={{0,8},{8,0},{1,9},{9,1},{2,10},{10,2},{3,11},{11,3},{4,12},{12,4},... | collective-permute-start | bytes 6291464 | tf_op jit(solution)/shard_map/ppermute | solution.py:208
  130.4 11.8 %collective-permute-start.10 = (bf16[4,128,384]{2,1,0:T(8,128)(2,1)S(1)}, bf16[4,128,384]{2,1,0:T(8,128)(2,1)S(1)}, u32[]{:S(2)}, u32[]{:S(2)}) collective-permute-start(bf16[4,128,384]{2,1,0:T(8,128)(2,1)S(1)} %get-tuple-element.14.refs_0_), channel_id=1, source_target_pairs={{0,16},{16,32},{32,48},{48,0},{1,17},{17,33},{33,49},{49,1},{2,18}... | collective-permute-start | bytes 1179656 | tf_op jit(solution)/shard_map/ppermute | solution.py:192
  134.9 10.6 %collective-permute-start.11 = (bf16[4,128,384]{2,1,0:T(8,128)(2,1)S(1)}, bf16[4,128,384]{2,1,0:T(8,128)(2,1)S(1)}, u32[]{:S(2)}, u32[]{:S(2)}) collective-permute-start(bf16[4,128,384]{2,1,0:T(8,128)(2,1)S(1)} %get-tuple-element.13.refs_1_), channel_id=1, source_target_pairs={{0,48},{16,0},{32,16},{48,32},{1,49},{17,1},{33,17},{49,33},{2,50}... | collective-permute-start | bytes 1179656 | tf_op jit(solution)/shard_map/ppermute | solution.py:193
  136.8 12.9 %collective-permute-start.12 = (bf16[4,128,384]{2,1,0:T(8,128)(2,1)S(1)}, bf16[4,128,384]{2,1,0:T(8,128)(2,1)S(1)}, u32[]{:S(2)}, u32[]{:S(2)}) collective-permute-start(bf16[4,128,384]{2,1,0:T(8,128)(2,1)S(1)} %get-tuple-element.13.refs_1_), channel_id=1, source_target_pairs={{0,16},{16,32},{32,48},{48,0},{1,17},{17,33},{33,49},{49,1},{2,18}... | collective-permute-start | bytes 1179656 | tf_op jit(solution)/shard_map/ppermute | solution.py:194
  140.2 13.0 %collective-permute-start.13 = (bf16[4,128,384]{2,1,0:T(8,128)(2,1)S(1)}, bf16[4,128,384]{2,1,0:T(8,128)(2,1)S(1)}, u32[]{:S(2)}, u32[]{:S(2)}) collective-permute-start(bf16[4,128,384]{2,1,0:T(8,128)(2,1)S(1)} %get-tuple-element.14.refs_0_), channel_id=1, source_target_pairs={{0,48},{16,0},{32,16},{48,32},{1,49},{17,1},{33,17},{49,33},{2,50}... | collective-permute-start | bytes 1179656 | tf_op jit(solution)/shard_map/ppermute | solution.py:195
  142.1 17.1 %collective-permute-start.14 = (bf16[4,128,384]{2,1,0:T(8,128)(2,1)S(1)}, bf16[4,128,384]{2,1,0:T(8,128)(2,1)S(1)}, u32[]{:S(2)}, u32[]{:S(2)}) collective-permute-start(bf16[4,128,384]{2,1,0:T(8,128)(2,1)S(1)} %collective-permute-done.10.refs_2_), channel_id=1, source_target_pairs={{0,16},{16,32},{32,48},{48,0},{1,17},{17,33},{33,49},{49,1},{2,18}... | collective-permute-start | bytes 1179656 | tf_op jit(solution)/shard_map/ppermute | solution.py:196
  145.5 16.1 %collective-permute-start.15 = (bf16[4,128,384]{2,1,0:T(8,128)(2,1)S(1)}, bf16[4,128,384]{2,1,0:T(8,128)(2,1)S(1)}, u32[]{:S(2)}, u32[]{:S(2)}) collective-permute-start(bf16[4,128,384]{2,1,0:T(8,128)(2,1)S(1)} %collective-permute-done.11.refs_3_), channel_id=1, source_target_pairs={{0,48},{16,0},{32,16},{48,32},{1,49},{17,1},{33,17},{49,33},{2,50}... | collective-permute-start | bytes 1179656 | tf_op jit(solution)/shard_map/ppermute | solution.py:197
  153.2 2.8 %copy-start.1 = (f32[2,16,128,384]{3,2,1,0:T(8,128)S(1)}, f32[2,16,128,384]{3,2,1,0:T(8,128)}, u32[]{:S(2)}) copy-start(f32[2,16,128,384]{3,2,1,0:T(8,128)} %copy-done) | copy-start | bytes 18874372
  163.6 9.5 %collective-permute-start.16 = (bf16[8,128,384]{2,1,0:T(8,128)(2,1)S(1)}, bf16[8,128,384]{2,1,0:T(8,128)(2,1)S(1)}, u32[]{:S(2)}, u32[]{:S(2)}) collective-permute-start(bf16[8,128,384]{2,1,0:T(8,128)(2,1)S(1)} %get-tuple-element.12), channel_id=1, source_target_pairs={{0,8},{8,0},{1,9},{9,1},{2,10},{10,2},{3,11},{11,3},{4,12},{12,4},... | collective-permute-start | bytes 2359304 | tf_op jit(solution)/shard_map/ppermute | solution.py:208
  172.7 26.8 %copy-start.7 = (bf16[128,384]{1,0:T(8,128)(2,1)S(1)}, bf16[128,384]{1,0:T(8,128)(2,1)}, u32[]{:S(2)}) copy-start(bf16[128,384]{1,0:T(8,128)(2,1)} %shard_map.64) | copy-start | bytes 294916

commit v5 on v4

--- a/solution.py
+++ b/solution.py
@@ -11,8 +11,10 @@
 NQ, NP, NX, NC, NY = 4, 2, 4, 2, 8
 TILE, COLS = 128, 384
 CHIPS = NQ * NP * NX
-NEAR_SPOTS = ((0, 0), (1, 0), (0, 1), (1, 2), (1, 1), (0, 2))
-FAR_SPOTS = ((0, 3), (1, 3))
+LOW = 5
+ROWS = NQ * NP
+NEAR_SPOTS = ((0, 0), (LOW, 0), (0, 1), (LOW, 2), (LOW, 1), (0, 2))
+FAR_SPOTS = ((0, 3), (LOW, 3))
 SOLVE_FLOPS = 2 * TILE * TILE * COLS
 PAIR_FLOPS = 2 * SOLVE_FLOPS
 
@@ -84,14 +86,15 @@
     for piece, (base, side) in zip(pieces, spots):
 
         def step(j, carry, piece=piece, base=base, side=side):
-            chip = (base + 2 * j) * NX + where[side]
+            k = base + j
+            chip = (2 * lax.rem(k, NQ) + lax.div(k, NQ)) * NX + where[side]
             pair = jnp.concatenate([mine[chip, core], other[chip, core]], axis=0)
             product = jnp.dot(pair, piece[j], preferred_element_type=jnp.float32)
             state[0, slots[level, chip * NC + core]] += product[:TILE]
             state[1, received[level, chip * NC + core]] += product[TILE:]
             return carry
 
-        lax.fori_loop(0, piece.shape[0], step, 0, unroll=4)
+        lax.fori_loop(0, piece.shape[0], step, 0, unroll=True)
 
 
 def early_first_body(where, slots, received, mine, other, *refs):
@@ -123,8 +126,8 @@
     del state
     core = where[NX]
     for piece, (base, side) in zip((low, high), FAR_SPOTS):
-        for j in range(NQ):
-            row = base + 2 * j
+        for j in range(piece.shape[0]):
+            row = 2 * ((base + j) % NQ) + (base + j) // NQ
             entry = (row * NX + where[side]) * NC + core
             product = jnp.dot(tiles[row, 0, 0], piece[j], preferred_element_type=jnp.float32)
             out[0, table[level, entry]] += product
@@ -137,14 +140,13 @@
 
 
 def late(level, half, where, table, tiles, state, pieces):
-    by_place = (NQ * NP, NX, NC, TILE, TILE)
-    column = pl.BlockSpec((NQ * NP, 1, 1, TILE, TILE), lambda i, where: (0, where[3], where[NX], 0, 0))
+    by_place = (ROWS, NX, NC, TILE, TILE)
+    column = pl.BlockSpec((ROWS, 1, 1, TILE, TILE), lambda i, where: (0, where[3], where[NX], 0, 0))
     part = pl.BlockSpec((1,) + state.shape[1:], lambda i, where: (half, 0, 0, 0))
-    slab = (NQ, TILE, COLS)
     grid_spec = pltpu.PrefetchScalarGridSpec(
         num_scalar_prefetch=1,
         grid=(1,),
-        in_specs=[smem(), column, part, whole(slab), whole(slab)],
+        in_specs=[smem(), column, part] + [whole(piece.shape) for piece in pieces],
         out_specs=[part] + [whole((NY, TILE, COLS))] * half,
     )
     return call(
@@ -182,13 +184,13 @@
 
 def gather_rows(block):
     even_odd = lax.all_gather(block[None], "zq", axis=0, tiled=True)
-    return lax.all_gather(even_odd[None], "zp", axis=0, tiled=True)
+    return lax.all_gather(even_odd, "zp", axis=0, tiled=True)
 
 
 def gather_columns(own):
     up = functools.partial(lax.ppermute, axis_name="x", perm=ring(NX, 1))
     down = functools.partial(lax.ppermute, axis_name="x", perm=ring(NX, -1))
-    low, high = own[0], own[1]
+    low, high = own[:LOW], own[LOW:]
     low_left = up(low)
     high_right = down(high)
     high_left = up(high)

time: 201 us -> 213 us (1.060)
  the two profiles are of different devices: /device:TPU:5 before, /device:TPU:1 now
where the time goes in v5:
time: 213 us; the launch traced here: 212 us
  blocking collectives  72 us (34%)
  starting transfers between devices  70.3 us (33%)
  waiting for transfers between devices  45.2 us (21%)
  Pallas kernels  16.8 us (8%)
  local copies, waits for them, and re-layouts  6.72 us (3%)
    ppermute x5, starting transfers between devices, swap(): return lax.ppermute(value, 'core', [(0, 1), (1, 0)])  28.6 us
    all_gather x2, blocking collectives, gather_rows(): even_odd = lax.all_gather(block[None], 'zq', axis=0, tiled=True)  26.2 us
    all_to_all x1, blocking collectives, reduce_rows(): return (state, lax.all_to_all(join(state, near), 'y', 0, 0, tiled=True))  26 us
    all_to_all x1, waiting for transfers between devices, reduce_rows(): return (state, lax.all_to_all(join(state, near), 'y', 0, 0, tiled=True))  21.1 us
    all_gather x2, blocking collectives, gather_rows(): return lax.all_gather(even_odd, 'zp', axis=0, tiled=True)  19.9 us
    pallas_call x11, Pallas kernels, call(): pl.pallas_call(body, out_shape=out_shape, input_output_aliases=aliases or...  16.8 us
    ppermute x2, waiting for transfers between devices, gather_columns(): high_left = up(high)  15.2 us
    ppermute x2, starting transfers between devices, gather_columns(): high_far = down(high_right)  7.96 us
  transfers between devices with their start and end apart: 18, of which 7 were waited for; matrix products, arithmetic and copies ran while one was open for 0% of the time, Pallas kernels for 6%

profile of v5, /device:TPU:1, one launch (start us, length us, event | category | flops | bytes accessed | tf_op | source)
XLA Modules:
  0.0 212.2 jit_solution(5305837350611591699)
XLA Ops:
  0.0 8.9 %collective-permute-start.1 = (bf16[32,2,128,128]{3,2,1,0:T(8,128)(2,1)}, bf16[32,2,128,128]{3,2,1,0:T(8,128)(2,1)}, u32[]{:S(2)}, u32[]{:S(2)}) collective-permute-start(bf16[32,2,128,128]{3,2,1,0:T(8,128)(2,1)} %bitcast.25), channel_id=1, source_target_pairs={{0,8},{8,0},{1,9},{9,1},{2,10},{10,2},{3,11},{11,3},{4,12},{12,4},... | collective-permute-start | bytes 6291464 | tf_op jit(solution)/shard_map/ppermute | solution.py:210
  10.6 13.4 %all-gather = bf16[512,384]{1,0:T(8,128)(2,1)S(1)} all-gather(bf16[128,384]{1,0:T(8,128)(2,1)} %shard_map.64), channel_id=2, replica_groups=mesh['zq'=4,'zp'=2,'x'=4,'core'=2,'y'=8] {'zq'}, dimensions={0}, use_global_device_ids=true | all-gather | bytes 491520 | tf_op jit(solution)/shard_map/all_gather | solution.py:186
  24.0 10.7 %all_gather.13 = bf16[8,128,384]{2,1,0:T(8,128)(2,1)S(1)} all-gather(bf16[4,128,384]{2,1,0:T(8,128)(2,1)S(1)} %bitcast.30), channel_id=1, replica_groups=mesh['zq'=4,'zp'=2,'x'=4,'core'=2,'y'=8] {'zp'}, dimensions={0}, use_global_device_ids=true | all-gather | bytes 1179648 | tf_op jit(solution)/shard_map/all_gather | solution.py:187
  34.7 3.1 %collective-permute-start.2 = (bf16[5,128,384]{2,1,0:T(8,128)(2,1)S(1)}, bf16[5,128,384]{2,1,0:T(8,128)(2,1)}, u32[]{:S(2)}, u32[]{:S(2)}) collective-permute-start(bf16[5,128,384]{2,1,0:T(8,128)(2,1)S(1)} %slice.16.refs_0_), channel_id=1, source_target_pairs={{0,16},{16,32},{32,48},{48,0},{1,17},{17,33},{33,49},{49,1},{2,18}... | collective-permute-start | bytes 1474568 | tf_op jit(solution)/shard_map/ppermute | solution.py:194
  37.9 3.4 %collective-permute-start.3 = (bf16[3,128,384]{2,1,0:T(8,128)(2,1)S(1)}, bf16[3,128,384]{2,1,0:T(8,128)(2,1)}, u32[]{:S(2)}, u32[]{:S(2)}) collective-permute-start(bf16[3,128,384]{2,1,0:T(8,128)(2,1)S(1)} %slice.17.refs_1_), channel_id=1, source_target_pairs={{0,48},{16,0},{32,16},{48,32},{1,49},{17,1},{33,17},{49,33},{2,50}... | collective-permute-start | bytes 884744 | tf_op jit(solution)/shard_map/ppermute | solution.py:195
  41.3 3.2 %collective-permute-start.5 = (bf16[5,128,384]{2,1,0:T(8,128)(2,1)S(1)}, bf16[5,128,384]{2,1,0:T(8,128)(2,1)}, u32[]{:S(2)}, u32[]{:S(2)}) collective-permute-start(bf16[5,128,384]{2,1,0:T(8,128)(2,1)S(1)} %slice.16.refs_0_), channel_id=1, source_target_pairs={{0,48},{16,0},{32,16},{48,32},{1,49},{17,1},{33,17},{49,33},{2,50}... | collective-permute-start | bytes 1474568 | tf_op jit(solution)/shard_map/ppermute | solution.py:197
  44.5 3.6 %collective-permute-done.2.refs_2_ = bf16[5,128,384]{2,1,0:T(8,128)(2,1)} collective-permute-done((bf16[5,128,384]{2,1,0:T(8,128)(2,1)S(1)}, bf16[5,128,384]{2,1,0:T(8,128)(2,1)}, u32[]{:S(2)}, u32[]{:S(2)}) %collective-permute-start.2) | collective-permute-done | bytes 491552 | tf_op jit(solution)/shard_map/ppermute | solution.py:194
  50.0 5.7 %collective-permute-start = (s32[2,64]{1,0:T(2,128)S(1)}, s32[2,64]{1,0:T(2,128)S(1)}, u32[]{:S(2)}, u32[]{:S(2)}) collective-permute-start(s32[2,64]{1,0:T(2,128)S(1)} %pad_add_fusion.slots.table), channel_id=1, source_target_pairs={{0,8},{8,0},{1,9},{9,1},{2,10},{10,2},{3,11},{11,3},{4,12},{12,4},... | collective-permute-start | bytes 1544 | tf_op jit(solution)/shard_map/ppermute | solution.py:210
  56.5 3.1 %collective-permute-start.4 = (bf16[3,128,384]{2,1,0:T(8,128)(2,1)S(1)}, bf16[3,128,384]{2,1,0:T(8,128)(2,1)}, u32[]{:S(2)}, u32[]{:S(2)}) collective-permute-start(bf16[3,128,384]{2,1,0:T(8,128)(2,1)S(1)} %slice.17.refs_1_), channel_id=1, source_target_pairs={{0,16},{16,32},{32,48},{48,0},{1,17},{17,33},{33,49},{49,1},{2,18}... | collective-permute-start | bytes 884744 | tf_op jit(solution)/shard_map/ppermute | solution.py:196
  59.6 3.4 %collective-permute-start.7 = (bf16[3,128,384]{2,1,0:T(8,128)(2,1)}, bf16[3,128,384]{2,1,0:T(8,128)(2,1)}, u32[]{:S(2)}, u32[]{:S(2)}) collective-permute-start(bf16[3,128,384]{2,1,0:T(8,128)(2,1)} %collective-permute-done.3.refs_3_), channel_id=1, source_target_pairs={{0,48},{16,0},{32,16},{48,32},{1,49},{17,1},{33,17},{49,33},{2,50}... | collective-permute-start | bytes 884744 | tf_op jit(solution)/shard_map/ppermute | solution.py:199
  63.2 5.6 %collective-permute-done.4.refs_4_ = bf16[3,128,384]{2,1,0:T(8,128)(2,1)} collective-permute-done((bf16[3,128,384]{2,1,0:T(8,128)(2,1)S(1)}, bf16[3,128,384]{2,1,0:T(8,128)(2,1)}, u32[]{:S(2)}, u32[]{:S(2)}) %collective-permute-start.4) | collective-permute-done | bytes 294944 | tf_op jit(solution)/shard_map/ppermute | solution.py:196
  68.8 3.7 %shard_map.65.state = f32[2,16,128,384]{3,2,1,0:T(8,128)S(1)} custom-call(s32[5]{0:T(128)S(1)} %stack.36.where, s32[2,64]{1,0:T(2,128)S(1)} %pad_add_fusion.slots.table, s32[2,64]{1,0:T(2,128)S(1)} %collective-permute-done.received.table, bf16[32,2,128,128]{3,2,1,0:T(8,128)(2,1)S(1)} %bitcast.26, bf16[32,2,128,128]{3,2,1,0:T(8,128)(2,1)} %collective-permute-done.1.other, ...), custom_call_target="tpu_custom_call" | custom-call | flops 603979776 | bytes 4194304 | tf_op jit(solution)/shard_map/pallas_call | solution.py:37
  72.5 2.0 shard_map.66
  74.5 4.6 %collective-permute-start.8 = (bf16[8,128,384]{2,1,0:T(8,128)(2,1)S(1)}, bf16[8,128,384]{2,1,0:T(8,128)(2,1)S(1)}, u32[]{:S(2)}, u32[]{:S(2)}) collective-permute-start(bf16[8,128,384]{2,1,0:T(8,128)(2,1)S(1)} %get-tuple-element.10), channel_id=1, source_target_pairs={{0,8},{8,0},{1,9},{9,1},{2,10},{10,2},{3,11},{11,3},{4,12},{12,4},... | collective-permute-start | bytes 2359304 | tf_op jit(solution)/shard_map/ppermute | solution.py:210
  81.3 2.7 %copy-done = f32[2,16,128,384]{3,2,1,0:T(8,128)} copy-done((f32[2,16,128,384]{3,2,1,0:T(8,128)}, f32[2,16,128,384]{3,2,1,0:T(8,128)S(1)}, u32[]{:S(2)}) %copy-start) | copy-done | bytes 6291480
  84.9 6.8 %all-to-all-start = ((bf16[8,128,384]{2,1,0:T(8,128)(2,1)}), bf16[8,128,384]{2,1,0:T(8,128)(2,1)S(1)}, u32[]{:S(2)}, u32[]{:S(2)}) async-start(bf16[8,128,384]{2,1,0:T(8,128)(2,1)} %copy-done.4), calls=%async_computation | async-start | bytes 1572864 | tf_op jit(solution)/shard_map/all_to_all | solution.py:218
  91.8 2.5 %collective-permute-start.9 = (bf16[32,2,128,128]{3,2,1,0:T(8,128)(2,1)S(1)}, bf16[32,2,128,128]{3,2,1,0:T(8,128)(2,1)}, u32[]{:S(2)}, u32[]{:S(2)}) collective-permute-start(bf16[32,2,128,128]{3,2,1,0:T(8,128)(2,1)S(1)} %bitcast.22), channel_id=1, source_target_pairs={{0,8},{8,0},{1,9},{9,1},{2,10},{10,2},{3,11},{11,3},{4,12},{12,4},... | collective-permute-start | bytes 6291464 | tf_op jit(solution)/shard_map/ppermute | solution.py:210
  94.3 21.1 %all-to-all-done.parts = bf16[8,128,384]{2,1,0:T(8,128)(2,1)S(1)} async-done(((bf16[8,128,384]{2,1,0:T(8,128)(2,1)}), bf16[8,128,384]{2,1,0:T(8,128)(2,1)S(1)}, u32[]{:S(2)}, u32[]{:S(2)}) %all-to-all-start) | async-done | bytes 786464 | tf_op jit(solution)/shard_map/all_to_all | solution.py:218
  115.6 12.8 %all-gather.1 = bf16[512,384]{1,0:T(8,128)(2,1)S(1)} all-gather(bf16[128,384]{1,0:T(8,128)(2,1)S(1)} %shard_map.69), channel_id=3, replica_groups=mesh['zq'=4,'zp'=2,'x'=4,'core'=2,'y'=8] {'zq'}, dimensions={0}, use_global_device_ids=true | all-gather | bytes 491520 | tf_op jit(solution)/shard_map/all_gather | solution.py:186
  128.4 9.2 %all_gather.15 = bf16[8,128,384]{2,1,0:T(8,128)(2,1)S(1)} all-gather(bf16[4,128,384]{2,1,0:T(8,128)(2,1)S(1)} %bitcast.31), channel_id=1, replica_groups=mesh['zq'=4,'zp'=2,'x'=4,'core'=2,'y'=8] {'zp'}, dimensions={0}, use_global_device_ids=true | all-gather | bytes 1179648 | tf_op jit(solution)/shard_map/all_gather | solution.py:187
  137.7 1.9 collective-permute-start.10
  139.6 4.6 %collective-permute-start.11 = (bf16[3,128,384]{2,1,0:T(8,128)(2,1)S(1)}, bf16[3,128,384]{2,1,0:T(8,128)(2,1)S(1)}, u32[]{:S(2)}, u32[]{:S(2)}) collective-permute-start(bf16[3,128,384]{2,1,0:T(8,128)(2,1)S(1)} %slice.19.refs_1_), channel_id=1, source_target_pairs={{0,48},{16,0},{32,16},{48,32},{1,49},{17,1},{33,17},{49,33},{2,50}... | collective-permute-start | bytes 884744 | tf_op jit(solution)/shard_map/ppermute | solution.py:195
  144.2 1.9 collective-permute-start.13
  146.1 4.1 %collective-permute-done.10.refs_2_ = bf16[5,128,384]{2,1,0:T(8,128)(2,1)S(1)} collective-permute-done((bf16[5,128,384]{2,1,0:T(8,128)(2,1)S(1)}, bf16[5,128,384]{2,1,0:T(8,128)(2,1)S(1)}, u32[]{:S(2)}, u32[]{:S(2)}) %collective-permute-start.10) | collective-permute-done | bytes 491552 | tf_op jit(solution)/shard_map/ppermute | solution.py:194
  152.1 1.9 collective-permute-start.12
  154.1 4.6 %collective-permute-start.15 = (bf16[3,128,384]{2,1,0:T(8,128)(2,1)S(1)}, bf16[3,128,384]{2,1,0:T(8,128)(2,1)S(1)}, u32[]{:S(2)}, u32[]{:S(2)}) collective-permute-start(bf16[3,128,384]{2,1,0:T(8,128)(2,1)S(1)} %collective-permute-done.11.refs_3_), channel_id=1, source_target_pairs={{0,48},{16,0},{32,16},{48,32},{1,49},{17,1},{33,17},{49,33},{2,50}... | collective-permute-start | bytes 884744 | tf_op jit(solution)/shard_map/ppermute | solution.py:199
  158.7 9.6 %collective-permute-done.12.refs_4_ = bf16[3,128,384]{2,1,0:T(8,128)(2,1)S(1)} collective-permute-done((bf16[3,128,384]{2,1,0:T(8,128)(2,1)S(1)}, bf16[3,128,384]{2,1,0:T(8,128)(2,1)S(1)}, u32[]{:S(2)}, u32[]{:S(2)}) %collective-permute-start.12) | collective-permute-done | bytes 294944 | tf_op jit(solution)/shard_map/ppermute | solution.py:196
  168.2 2.8 %copy-done.1 = f32[2,16,128,384]{3,2,1,0:T(8,128)S(1)} copy-done((f32[2,16,128,384]{3,2,1,0:T(8,128)S(1)}, f32[2,16,128,384]{3,2,1,0:T(8,128)}, u32[]{:S(2)}) %copy-start.1) | copy-done | bytes 6291480
  171.0 3.2 %shard_map.70.state = f32[2,8,128,384]{3,2,1,0:T(8,128)S(1)} custom-call(s32[5]{0:T(128)S(1)} %stack.36.where, s32[2,64]{1,0:T(2,128)S(1)} %pad_add_fusion.slots.table, s32[2,64]{1,0:T(2,128)S(1)} %collective-permute-done.received.table, bf16[32,2,128,128]{3,2,1,0:T(8,128)(2,1)S(1)} %bitcast.23, bf16[32,2,128,128]{3,2,1,0:T(8,128)(2,1)} %collective-permute-done.9.other, ...), custom_call_target="tpu_custom_call" | custom-call | flops 603979776 | bytes 4194304 | tf_op jit(solution)/shard_map/pallas_call | solution.py:37
  174.2 2.0 shard_map.71
  176.2 6.9 %collective-permute-start.16 = (bf16[8,128,384]{2,1,0:T(8,128)(2,1)S(1)}, bf16[8,128,384]{2,1,0:T(8,128)(2,1)S(1)}, u32[]{:S(2)}, u32[]{:S(2)}) collective-permute-start(bf16[8,128,384]{2,1,0:T(8,128)(2,1)S(1)} %get-tuple-element.12), channel_id=1, source_target_pairs={{0,8},{8,0},{1,9},{9,1},{2,10},{10,2},{3,11},{11,3},{4,12},{12,4},... | collective-permute-start | bytes 2359304 | tf_op jit(solution)/shard_map/ppermute | solution.py:210
  185.2 26.0 %all_to_all.10.parts = bf16[8,128,384]{2,1,0:T(8,128)(2,1)S(1)} all-to-all(bf16[8,128,384]{2,1,0:T(8,128)(2,1)S(1)} %shard_map.73), channel_id=1, replica_groups=mesh['zq'=4,'zp'=2,'x'=4,'core'=2,'y'=8] {'y'}, dimensions={0} | all-to-all | bytes 1572864 | tf_op jit(solution)/shard_map/all_to_all | solution.py:218
  (47 shorter events, 13.0 us)
Async XLA Ops:
  0.0 68.8 %copy-start.3 = (bf16[1,64,1,128,128]{4,3,2,1,0:T(8,128)(2,1)S(1)}, bf16[1,64,1,128,128]{4,3,2,1,0:T(8,128)(2,1)}, u32[]{:S(2)}) copy-start(bf16[1,64,1,128,128]{4,3,2,1,0:T(8,128)(2,1)} %param.8) | copy-start | bytes 6291460
  0.0 50.0 %copy-start.9 = (s32[1,64,1]{1,2,0:T(1,128)S(1)}, s32[1,64,1]{1,2,0:T(1,128)}, u32[]{:S(2)}) copy-start(s32[1,64,1]{1,2,0:T(1,128)} %param.9) | copy-start | bytes 772
  0.0 50.0 %copy-start.8 = (s32[1,64,1]{1,2,0:T(1,128)S(1)}, s32[1,64,1]{1,2,0:T(1,128)}, u32[]{:S(2)}) copy-start(s32[1,64,1]{1,2,0:T(1,128)} %param.11) | copy-start | bytes 772
  0.0 68.8 %collective-permute-start.1 = (bf16[32,2,128,128]{3,2,1,0:T(8,128)(2,1)}, bf16[32,2,128,128]{3,2,1,0:T(8,128)(2,1)}, u32[]{:S(2)}, u32[]{:S(2)}) collective-permute-start(bf16[32,2,128,128]{3,2,1,0:T(8,128)(2,1)} %bitcast.25), channel_id=1, source_target_pairs={{0,8},{8,0},{1,9},{9,1},{2,10},{10,2},{3,11},{11,3},{4,12},{12,4},... | collective-permute-start | bytes 6291464 | tf_op jit(solution)/shard_map/ppermute | solution.py:210
  34.7 13.3 %collective-permute-start.2 = (bf16[5,128,384]{2,1,0:T(8,128)(2,1)S(1)}, bf16[5,128,384]{2,1,0:T(8,128)(2,1)}, u32[]{:S(2)}, u32[]{:S(2)}) collective-permute-start(bf16[5,128,384]{2,1,0:T(8,128)(2,1)S(1)} %slice.16.refs_0_), channel_id=1, source_target_pairs={{0,16},{16,32},{32,48},{48,0},{1,17},{17,33},{33,49},{49,1},{2,18}... | collective-permute-start | bytes 1474568 | tf_op jit(solution)/shard_map/ppermute | solution.py:194
  37.9 21.7 %collective-permute-start.3 = (bf16[3,128,384]{2,1,0:T(8,128)(2,1)S(1)}, bf16[3,128,384]{2,1,0:T(8,128)(2,1)}, u32[]{:S(2)}, u32[]{:S(2)}) collective-permute-start(bf16[3,128,384]{2,1,0:T(8,128)(2,1)S(1)} %slice.17.refs_1_), channel_id=1, source_target_pairs={{0,48},{16,0},{32,16},{48,32},{1,49},{17,1},{33,17},{49,33},{2,50}... | collective-permute-start | bytes 884744 | tf_op jit(solution)/shard_map/ppermute | solution.py:195
  41.3 27.5 %collective-permute-start.5 = (bf16[5,128,384]{2,1,0:T(8,128)(2,1)S(1)}, bf16[5,128,384]{2,1,0:T(8,128)(2,1)}, u32[]{:S(2)}, u32[]{:S(2)}) collective-permute-start(bf16[5,128,384]{2,1,0:T(8,128)(2,1)S(1)} %slice.16.refs_0_), channel_id=1, source_target_pairs={{0,48},{16,0},{32,16},{48,32},{1,49},{17,1},{33,17},{49,33},{2,50}... | collective-permute-start | bytes 1474568 | tf_op jit(solution)/shard_map/ppermute | solution.py:197
  48.1 24.4 %collective-permute-start.6 = (bf16[5,128,384]{2,1,0:T(8,128)(2,1)}, bf16[5,128,384]{2,1,0:T(8,128)(2,1)S(1)}, u32[]{:S(2)}, u32[]{:S(2)}) collective-permute-start(bf16[5,128,384]{2,1,0:T(8,128)(2,1)} %collective-permute-done.2.refs_2_), channel_id=1, source_target_pairs={{0,16},{16,32},{32,48},{48,0},{1,17},{17,33},{33,49},{49,1},{2,18}... | collective-permute-start | bytes 1474568 | tf_op jit(solution)/shard_map/ppermute | solution.py:198
  50.0 6.5 %collective-permute-start = (s32[2,64]{1,0:T(2,128)S(1)}, s32[2,64]{1,0:T(2,128)S(1)}, u32[]{:S(2)}, u32[]{:S(2)}) collective-permute-start(s32[2,64]{1,0:T(2,128)S(1)} %pad_add_fusion.slots.table), channel_id=1, source_target_pairs={{0,8},{8,0},{1,9},{9,1},{2,10},{10,2},{3,11},{11,3},{4,12},{12,4},... | collective-permute-start | bytes 1544 | tf_op jit(solution)/shard_map/ppermute | solution.py:210
  56.5 12.2 %collective-permute-start.4 = (bf16[3,128,384]{2,1,0:T(8,128)(2,1)S(1)}, bf16[3,128,384]{2,1,0:T(8,128)(2,1)}, u32[]{:S(2)}, u32[]{:S(2)}) collective-permute-start(bf16[3,128,384]{2,1,0:T(8,128)(2,1)S(1)} %slice.17.refs_1_), channel_id=1, source_target_pairs={{0,16},{16,32},{32,48},{48,0},{1,17},{17,33},{33,49},{49,1},{2,18}... | collective-permute-start | bytes 884744 | tf_op jit(solution)/shard_map/ppermute | solution.py:196
  59.6 12.8 %collective-permute-start.7 = (bf16[3,128,384]{2,1,0:T(8,128)(2,1)}, bf16[3,128,384]{2,1,0:T(8,128)(2,1)}, u32[]{:S(2)}, u32[]{:S(2)}) collective-permute-start(bf16[3,128,384]{2,1,0:T(8,128)(2,1)} %collective-permute-done.3.refs_3_), channel_id=1, source_target_pairs={{0,48},{16,0},{32,16},{48,32},{1,49},{17,1},{33,17},{49,33},{2,50}... | collective-permute-start | bytes 884744 | tf_op jit(solution)/shard_map/ppermute | solution.py:199
  74.5 6.5 %collective-permute-start.8 = (bf16[8,128,384]{2,1,0:T(8,128)(2,1)S(1)}, bf16[8,128,384]{2,1,0:T(8,128)(2,1)S(1)}, u32[]{:S(2)}, u32[]{:S(2)}) collective-permute-start(bf16[8,128,384]{2,1,0:T(8,128)(2,1)S(1)} %get-tuple-element.10), channel_id=1, source_target_pairs={{0,8},{8,0},{1,9},{9,1},{2,10},{10,2},{3,11},{11,3},{4,12},{12,4},... | collective-permute-start | bytes 2359304 | tf_op jit(solution)/shard_map/ppermute | solution.py:210
  81.0 10.7 %copy-start.2 = (bf16[1,64,1,128,128]{4,3,2,1,0:T(8,128)(2,1)S(1)}, bf16[1,64,1,128,128]{4,3,2,1,0:T(8,128)(2,1)}, u32[]{:S(2)}) copy-start(bf16[1,64,1,128,128]{4,3,2,1,0:T(8,128)(2,1)} %param.10) | copy-start | bytes 6291460
  81.0 34.3 %copy-start.5 = (bf16[3,1,128,384]{3,2,1,0:T(8,128)(2,1)S(1)}, bf16[3,1,128,384]{3,2,1,0:T(8,128)(2,1)}, u32[]{:S(2)}) copy-start(bf16[3,1,128,384]{3,2,1,0:T(8,128)(2,1)} %right.5) | copy-start | bytes 884740
  81.1 34.3 %copy-start.6 = (bf16[3,1,128,128]{3,2,1,0:T(8,128)(2,1)S(1)}, bf16[3,1,128,128]{3,2,1,0:T(8,128)(2,1)}, u32[]{:S(2)}) copy-start(bf16[3,1,128,128]{3,2,1,0:T(8,128)(2,1)} %inverse.5) | copy-start | bytes 294916
  81.3 2.7 %copy-start = (f32[2,16,128,384]{3,2,1,0:T(8,128)}, f32[2,16,128,384]{3,2,1,0:T(8,128)S(1)}, u32[]{:S(2)}) copy-start(f32[2,16,128,384]{3,2,1,0:T(8,128)S(1)} %shard_map.67.state.later) | copy-start | bytes 18874372
  84.0 1.0 copy-start.4
  84.9 30.4 %all-to-all-start = ((bf16[8,128,384]{2,1,0:T(8,128)(2,1)}), bf16[8,128,384]{2,1,0:T(8,128)(2,1)S(1)}, u32[]{:S(2)}, u32[]{:S(2)}) async-start(bf16[8,128,384]{2,1,0:T(8,128)(2,1)} %copy-done.4), calls=%async_computation | async-start | bytes 1572864 | tf_op jit(solution)/shard_map/all_to_all | solution.py:218
  91.8 66.9 %collective-permute-start.9 = (bf16[32,2,128,128]{3,2,1,0:T(8,128)(2,1)S(1)}, bf16[32,2,128,128]{3,2,1,0:T(8,128)(2,1)}, u32[]{:S(2)}, u32[]{:S(2)}) collective-permute-start(bf16[32,2,128,128]{3,2,1,0:T(8,128)(2,1)S(1)} %bitcast.22), channel_id=1, source_target_pairs={{0,8},{8,0},{1,9},{9,1},{2,10},{10,2},{3,11},{11,3},{4,12},{12,4},... | collective-permute-start | bytes 6291464 | tf_op jit(solution)/shard_map/ppermute | solution.py:210
  137.7 12.6 %collective-permute-start.10 = (bf16[5,128,384]{2,1,0:T(8,128)(2,1)S(1)}, bf16[5,128,384]{2,1,0:T(8,128)(2,1)S(1)}, u32[]{:S(2)}, u32[]{:S(2)}) collective-permute-start(bf16[5,128,384]{2,1,0:T(8,128)(2,1)S(1)} %slice.18.refs_0_), channel_id=1, source_target_pairs={{0,16},{16,32},{32,48},{48,0},{1,17},{17,33},{33,49},{49,1},{2,18}... | collective-permute-start | bytes 1474568 | tf_op jit(solution)/shard_map/ppermute | solution.py:194
  139.6 14.4 %collective-permute-start.11 = (bf16[3,128,384]{2,1,0:T(8,128)(2,1)S(1)}, bf16[3,128,384]{2,1,0:T(8,128)(2,1)S(1)}, u32[]{:S(2)}, u32[]{:S(2)}) collective-permute-start(bf16[3,128,384]{2,1,0:T(8,128)(2,1)S(1)} %slice.19.refs_1_), channel_id=1, source_target_pairs={{0,48},{16,0},{32,16},{48,32},{1,49},{17,1},{33,17},{49,33},{2,50}... | collective-permute-start | bytes 884744 | tf_op jit(solution)/shard_map/ppermute | solution.py:195
  144.2 24.0 %collective-permute-start.13 = (bf16[5,128,384]{2,1,0:T(8,128)(2,1)S(1)}, bf16[5,128,384]{2,1,0:T(8,128)(2,1)S(1)}, u32[]{:S(2)}, u32[]{:S(2)}) collective-permute-start(bf16[5,128,384]{2,1,0:T(8,128)(2,1)S(1)} %slice.18.refs_0_), channel_id=1, source_target_pairs={{0,48},{16,0},{32,16},{48,32},{1,49},{17,1},{33,17},{49,33},{2,50}... | collective-permute-start | bytes 1474568 | tf_op jit(solution)/shard_map/ppermute | solution.py:197
  150.2 24.0 %collective-permute-start.14 = (bf16[5,128,384]{2,1,0:T(8,128)(2,1)S(1)}, bf16[5,128,384]{2,1,0:T(8,128)(2,1)S(1)}, u32[]{:S(2)}, u32[]{:S(2)}) collective-permute-start(bf16[5,128,384]{2,1,0:T(8,128)(2,1)S(1)} %collective-permute-done.10.refs_2_), channel_id=1, source_target_pairs={{0,16},{16,32},{32,48},{48,0},{1,17},{17,33},{33,49},{49,1},{2,18}... | collective-permute-start | bytes 1474568 | tf_op jit(solution)/shard_map/ppermute | solution.py:198
  152.1 16.1 %collective-permute-start.12 = (bf16[3,128,384]{2,1,0:T(8,128)(2,1)S(1)}, bf16[3,128,384]{2,1,0:T(8,128)(2,1)S(1)}, u32[]{:S(2)}, u32[]{:S(2)}) collective-permute-start(bf16[3,128,384]{2,1,0:T(8,128)(2,1)S(1)} %slice.19.refs_1_), channel_id=1, source_target_pairs={{0,16},{16,32},{32,48},{48,0},{1,17},{17,33},{33,49},{49,1},{2,18}... | collective-permute-start | bytes 884744 | tf_op jit(solution)/shard_map/ppermute | solution.py:196
  154.1 20.1 %collective-permute-start.15 = (bf16[3,128,384]{2,1,0:T(8,128)(2,1)S(1)}, bf16[3,128,384]{2,1,0:T(8,128)(2,1)S(1)}, u32[]{:S(2)}, u32[]{:S(2)}) collective-permute-start(bf16[3,128,384]{2,1,0:T(8,128)(2,1)S(1)} %collective-permute-done.11.refs_3_), channel_id=1, source_target_pairs={{0,48},{16,0},{32,16},{48,32},{1,49},{17,1},{33,17},{49,33},{2,50}... | collective-permute-start | bytes 884744 | tf_op jit(solution)/shard_map/ppermute | solution.py:199
  168.2 2.8 %copy-start.1 = (f32[2,16,128,384]{3,2,1,0:T(8,128)S(1)}, f32[2,16,128,384]{3,2,1,0:T(8,128)}, u32[]{:S(2)}) copy-start(f32[2,16,128,384]{3,2,1,0:T(8,128)} %copy-done) | copy-start | bytes 18874372
  176.2 8.8 %collective-permute-start.16 = (bf16[8,128,384]{2,1,0:T(8,128)(2,1)S(1)}, bf16[8,128,384]{2,1,0:T(8,128)(2,1)S(1)}, u32[]{:S(2)}, u32[]{:S(2)}) collective-permute-start(bf16[8,128,384]{2,1,0:T(8,128)(2,1)S(1)} %get-tuple-element.12), channel_id=1, source_target_pairs={{0,8},{8,0},{1,9},{9,1},{2,10},{10,2},{3,11},{11,3},{4,12},{12,4},... | collective-permute-start | bytes 2359304 | tf_op jit(solution)/shard_map/ppermute | solution.py:210
  184.6 26.8 %copy-start.7 = (bf16[128,384]{1,0:T(8,128)(2,1)S(1)}, bf16[128,384]{1,0:T(8,128)(2,1)}, u32[]{:S(2)}) copy-start(bf16[128,384]{1,0:T(8,128)(2,1)} %shard_map.64) | copy-start | bytes 294916
